TPU v7x, 512 devices: a whole 4x8x8 slice. The times are simulated.
512 devices in a mesh: blk: 8 (over z), grid: 64 (over y, x, core).
Axes of the slice: x: 4, y: 8, z: 8, core: 2. Of those that a mesh axis runs over, the one named last changes fastest.
Arguments:
- centers: bfloat16 [65536, 512], P(('blk', 'grid')), as said below
- weights: float32 [65536, 1000], P(('blk', 'grid')), may hold values from -4 to 4
- batch_index: int32 [512], replicated, may hold values from 0 to 65535, as said below
- labels: int32 [512], replicated, may hold values from 0 to 999
- sub_index: int32 [4096], P(('blk', 'grid')), may hold values from 0 to 127
- eigvecs: bfloat16 [4096, 160], P(('blk', 'grid')), may hold values from -0.09375 to 0.09375
- scales: float32 [160], replicated, may hold values from 1 to 16
Outputs:
- predictions: bfloat16 [512, 1000], replicated
- center_grad: bfloat16 [65536, 1000], P(('blk', 'grid'))
- sub_increment: float32 [4096, 1000], P(('blk', 'grid'))
Inputs may be any that keep to these rules, and one draw needn't show every extreme that they name: Each device's block of 128 centers is named by exactly 512 / 512 entries of batch_index. sub_index: entry i names center (i // 8) * 128 + sub_index[i]. centers: row scales of order one.
All inputs are finite; a program needn't handle non-finite values.
Results may differ from a plain program's by a relative error of at most 0.0011.
The roundings to bfloat16 on the way count: a program that leaves them out, or rounds other values in their place, can miss the bound.
Values may be sent and summed in bfloat16 or wider, within the bound.
No kernel may reach another device: no remote copies, remote signals or barrier semaphores. Data moves between devices by JAX's collectives and lax.ppermute only.
A program may use at most 64 MiB of HBM per device.

v0:
```python
import jax
import jax.numpy as jnp
from jax import lax
from jax.sharding import Mesh
from jax.sharding import PartitionSpec as P

BLK_GRID = ("blk", "grid_0", "grid_1", "grid_2")


SOFTEN = 1.0
SPREAD = 4.0


def copy_for_each(array, axis):
    devices = lax.axis_size(axis)
    return lax.all_to_all(
        jnp.broadcast_to(array[None], (devices, *array.shape)), axis, 0, 0, tiled=True
    )


def joined_along(pieces, dim):
    shape = list(pieces.shape[1:])
    shape[dim] *= pieces.shape[0]
    return jnp.moveaxis(pieces, 0, dim).reshape(shape)


def gathered_by_axis(array, axes, dim):
    far, near = axes
    pieces = copy_for_each(copy_for_each(array, far), near)
    return joined_along(pieces.swapaxes(0, 1).reshape(-1, *array.shape), dim)


def split_up(array, dim, devices):
    before, after = (array.shape[:dim], array.shape[dim + 1 :])
    return jnp.moveaxis(array.reshape(*before, devices, -1, *after), dim, 0)


def sum_at_owner(array, axis, dim):
    pieces = split_up(array, dim, lax.axis_size(axis))
    arrived = lax.all_to_all(pieces, axis, split_axis=0, concat_axis=0, tiled=True)
    return arrived.sum(axis=0)


def summed_rows(array, axes, dim):
    far, near = axes
    pieces = split_up(array, dim, lax.axis_size(far))
    nearer = sum_at_owner(pieces, near, dim + 1)
    arrived = lax.all_to_all(nearer, far, split_axis=0, concat_axis=0, tiled=True)
    return arrived.sum(axis=0)


def padded_to(lines, devices):
    spare = -lines.shape[0] % devices
    if not spare:
        return lines
    return jnp.concatenate([lines, jnp.zeros((spare, *lines.shape[1:]), lines.dtype)])


def nested_sum(array, axes):
    lines = array.reshape(-1, array.shape[-1])
    own = summed_rows(padded_to(lines, lax.axis_size(axes[0]) * lax.axis_size(axes[1])), axes, 0)
    whole = gathered_by_axis(own, axes, 0)
    return whole[: len(lines)].reshape(array.shape)


def side_by_side(arrays, axis, dim, along):
    ends, at = ([], 0)
    for a in arrays[:-1]:
        at += a.shape[along]
        ends.append(at)
    both = jnp.concatenate(arrays, axis=along)
    return tuple(jnp.split(lax.all_gather(both, axis, axis=dim, tiled=True), ends, axis=along))


def kernel(left, right):
    left_sq = jnp.sum(jnp.square(left.astype(jnp.float32)), axis=1)
    right_sq = jnp.sum(jnp.square(right.astype(jnp.float32)), axis=1)
    cross = lax.dot_general(
        left, right, (((1,), (1,)), ((), ())), preferred_element_type=jnp.float32
    )
    dist = jnp.sqrt(jnp.maximum(left_sq[:, None] + right_sq[None, :] - 2.0 * cross, 0.0) + SOFTEN)
    return jnp.exp(-dist / SPREAD)


def one_hot(label_rows, classes):
    return (label_rows[:, None] == jnp.arange(classes, dtype=jnp.int32)[None, :]).astype(
        jnp.float32
    )


def local(centers, weights, batch_index, labels, sub_index, eigvecs, scales):
    groups = lax.axis_size(BLK_GRID)
    myself = lax.axis_index(BLK_GRID)
    held = centers.shape[0]
    classes = weights.shape[1]
    batch_rows = batch_index.shape[0]
    owner = batch_index // held
    within = batch_index % held
    share = batch_rows // groups
    order = jnp.argsort((owner != myself).astype(jnp.int32), stable=True)[:share]
    mine = jnp.take(centers, jnp.take(within, order), axis=0)
    gathered = gathered_by_axis(mine, (("blk", "grid_0"), ("grid_1", "grid_2")), 0)
    positions = jnp.arange(batch_rows, dtype=jnp.int32)
    earlier = jnp.sum(
        ((owner[None, :] == owner[:, None]) & (positions[None, :] < positions[:, None])).astype(
            jnp.int32
        ),
        axis=1,
    )
    batch = jnp.take(gathered, owner * share + earlier, axis=0)
    kbz = kernel(batch, centers).astype(jnp.bfloat16)
    partial_out = jnp.dot(kbz, weights.astype(jnp.bfloat16), preferred_element_type=jnp.float32)
    total = nested_sum(partial_out, (("blk", "grid_0"), ("grid_1", "grid_2")))
    predictions = total.astype(jnp.bfloat16)
    resid = (total - one_hot(labels, classes)).astype(jnp.bfloat16)
    subset_here = jnp.take(centers, sub_index, axis=0)
    sub_rows, vec_rows = side_by_side((subset_here, eigvecs), BLK_GRID, 0, 1)
    kzs = kernel(centers, sub_rows).astype(jnp.bfloat16)
    ksb_piece = kernel(sub_rows, batch).astype(jnp.bfloat16)
    kze_next = jnp.dot(kzs, vec_rows, preferred_element_type=jnp.float32)
    proj_next = lax.dot_general(
        vec_rows, ksb_piece, (((0,), (0,)), ((), ())), preferred_element_type=jnp.float32
    )
    coeff = jnp.dot(proj_next, resid.astype(jnp.float32), precision=lax.Precision.HIGHEST)
    scaled = scales[:, None] * coeff
    sub_increment = jnp.dot(eigvecs.astype(jnp.float32), scaled, precision=lax.Precision.HIGHEST)
    correction = jnp.dot(kze_next, scaled, precision=lax.Precision.HIGHEST)
    first = lax.dot_general(
        kbz, resid, (((0,), (0,)), ((), ())), preferred_element_type=jnp.float32
    )
    center_grad = (first - correction).astype(jnp.bfloat16)
    return (predictions, center_grad, sub_increment)


def solution(mesh):
    finer = Mesh(
        mesh.devices.reshape(mesh.shape["blk"], 8, 4, 2), ("blk", "grid_0", "grid_1", "grid_2")
    )
    return jax.shard_map(
        local,
        mesh=finer,
        in_specs=(
            P(BLK_GRID, None),
            P(BLK_GRID, None),
            P(),
            P(),
            P(BLK_GRID),
            P(BLK_GRID, None),
            P(),
        ),
        out_specs=(P(), P(BLK_GRID, None), P(BLK_GRID, None)),
        check_vma=False,
    )
```

profile of v0, /device:TPU:1, one launch (start us, length us, event | category | flops | bytes accessed | tf_op | source)
XLA Modules:
  0.0 206.3 jit_solution(2454548041779533252)
XLA Ops:
  7.2 0.7 compare_and_fusion
  7.9 0.7 compare_select_fusion.1
  8.6 1.5 gather_fusion.1
  10.2 1.3 pad_maximum_fusion
  11.5 0.7 compare_convert_fusion
  12.2 3.8 %sort.17 = (s32[512]{0:T(512)}, s32[512]{0:T(512)S(1)}) sort(s32[512]{0:T(512)S(1)} %get-tuple-element.41, s32[512]{0:T(512)S(1)} %iota.15), dimensions={0}, to_apply=%region_1.2 | sort | flops 4608 | bytes 8192 | tf_op jit(solution)/shard_map/jit(argsort)/sort | solution.py:100
  15.9 0.5 slice.3
  18.4 0.7 add_select_fusion
  19.1 0.6 dynamic-slice.5
  20.3 0.7 fusion.37
  21.1 0.5 broadcast.111
  21.7 1.0 reduce.4
  22.7 28.0 %all_to_all.30 = bf16[64,2,256]{2,1,0:T(2,128)(2,1)S(1)} all-to-all(bf16[64,2,256]{2,1,0:T(2,128)(2,1)S(1)} %reshape.126), channel_id=1, replica_groups=mesh['blk'=8,'grid_0'=8,'grid_1'=4,'grid_2'=2] {'blk','grid_0'}, dimensions={0} | all-to-all | bytes 131072 | tf_op jit(solution)/shard_map/all_to_all | solution.py:16
  50.8 0.8 broadcast_in_dim.88
  51.6 6.5 %all-to-all-start.1 = ((bf16[8,64,1,512]{3,1,2,0:T(8,128)(2,1)}), bf16[8,64,1,512]{3,1,2,0:T(8,128)(2,1)S(1)}, u32[]{:S(2)}, u32[]{:S(2)}) async-start(bf16[8,64,1,512]{3,1,2,0:T(8,128)(2,1)} %broadcast_in_dim.88), calls=%async_computation.1 | async-start | bytes 1048576 | tf_op jit(solution)/shard_map/all_to_all | solution.py:16
  58.5 9.0 %all-to-all-done.1 = bf16[8,64,1,512]{3,1,2,0:T(8,128)(2,1)S(1)} async-done(((bf16[8,64,1,512]{3,1,2,0:T(8,128)(2,1)}), bf16[8,64,1,512]{3,1,2,0:T(8,128)(2,1)S(1)}, u32[]{:S(2)}, u32[]{:S(2)}) %all-to-all-start.1) | async-done | bytes 524320 | tf_op jit(solution)/shard_map/all_to_all | solution.py:16
  67.7 2.0 gather_fusion
  70.4 0.5 copy-done.2
  71.4 1.2 copy.24
  72.6 29.9 %all_to_all.31 = f32[8,64,1,1000]{3,1,2,0:T(8,128)S(1)} all-to-all(f32[8,64,1,1000]{3,1,2,0:T(8,128)S(1)} %copy.24), channel_id=1, replica_groups=mesh['blk'=8,'grid_0'=8,'grid_1'=4,'grid_2'=2] {'grid_1','grid_2'}, dimensions={0} | all-to-all | bytes 4096000 | tf_op jit(solution)/shard_map/all_to_all | solution.py:40
  102.9 18.8 %all_to_all.32 = f32[64,1,1000]{2,1,0:T(1,128)S(1)} all-to-all(f32[64,1,1000]{2,1,0:T(1,128)S(1)} %reduce_sum.72), channel_id=1, replica_groups=mesh['blk'=8,'grid_0'=8,'grid_1'=4,'grid_2'=2] {'blk','grid_0'}, dimensions={0} | all-to-all | bytes 512000 | tf_op jit(solution)/shard_map/all_to_all | solution.py:48
  122.0 17.6 %all_to_all.33 = f32[64,1,1000]{2,1,0:T(1,128)S(1)} all-to-all(f32[64,1,1000]{2,1,0:T(1,128)S(1)} %broadcast_in_dim.91), channel_id=1, replica_groups=mesh['blk'=8,'grid_0'=8,'grid_1'=4,'grid_2'=2] {'blk','grid_0'}, dimensions={0} | all-to-all | bytes 512000 | tf_op jit(solution)/shard_map/all_to_all | solution.py:16
  139.9 32.8 %all_to_all.34 = f32[8,64,1,1000]{3,1,2,0:T(8,128)S(1)} all-to-all(f32[8,64,1,1000]{3,1,2,0:T(8,128)S(1)} %broadcast_in_dim.93), channel_id=1, replica_groups=mesh['blk'=8,'grid_0'=8,'grid_1'=4,'grid_2'=2] {'grid_1','grid_2'}, dimensions={0} | all-to-all | bytes 4096000 | tf_op jit(solution)/shard_map/all_to_all | solution.py:16
  172.7 1.1 copy.37
  173.9 1.3 copy.26
  175.2 3.1 %multiply_reduce_fusion = f32[4096]{0:T(1024)S(1)} fusion(bf16[4096,672]{1,0:T(8,128)(2,1)} %all-gather.2.cloned.1.call-done), kind=kLoop, calls=%fused_computation.3 | loop fusion | flops 6287360 | bytes 4210688 | tf_op jit(solution)/shard_map/reduce_sum | solution.py:77
  178.3 9.2 %fusion.12 = f32[160,512]{1,0:T(8,128)S(1)} fusion(bf16[4096,672]{1,0:T(8,128)(2,1)} %all-gather.2.cloned.1.call-done, f32[512]{0:T(512)S(1)} %multiply_reduce_fusion.1, f32[4096]{0:T(1024)S(1)} %multiply_reduce_fusion, bf16[512,512]{1,0:T(8,128)(2,1)S(1)} %copy-done.1, pred[512]{0:T(512)(128)(4,1)S(1)} %get-tuple-element.39), kind=kOutput, calls=%fused_computation.20 | convolution fusion | flops 2835611648 | bytes 6375936 | tf_op jit(solution)/shard_map/dot_general | solution.py:121
  187.6 1.9 convolution_multiply_fusion.1
  189.5 0.9 convolution_bitcast_fusion.1
  190.4 5.0 %fusion.14 = f32[128,160]{0,1:T(8,128)S(1)} fusion(bf16[4096,672]{1,0:T(8,128)(2,1)} %all-gather.2.cloned.1.call-done, bf16[128,512]{1,0:T(8,128)(2,1)S(1)} %copy-done.3, f32[4096]{0:T(1024)S(1)} %multiply_reduce_fusion, f32[128]{0:T(128)S(1)} %multiply_reduce_fusion.2), kind=kOutput, calls=%fused_computation.22 | convolution fusion | flops 708837376 | bytes 5734912 | tf_op jit(solution)/shard_map/dot_general | solution.py:120
  195.4 1.8 fusion.49
  197.2 2.2 %fusion.20 = bf16[128,1000]{0,1:T(8,128)(2,1)} fusion(f32[128,1000]{0,1:T(8,128)S(1)} %fusion.49, bf16[512,128]{1,0:T(8,128)(2,1)S(1)} %fusion.28, f32[64,8,1,1000]{3,0,2,1:T(8,128)S(1)} %bitcast.60, s32[512]{0:T(512)S(1)} %copy-done.5), kind=kOutput, calls=%fused_computation.27 | convolution fusion | flops 133376000 | bytes 2949120 | tf_op jit(solution)/shard_map/dot_general | solution.py:128
  (37 shorter events, 3.1 us)
Async XLA Ops:
  7.2 51.2 %copy-start.3 = (bf16[128,512]{1,0:T(8,128)(2,1)S(1)}, bf16[128,512]{1,0:T(8,128)(2,1)}, u32[]{:S(2)}) copy-start(bf16[128,512]{1,0:T(8,128)(2,1)} %param.7) | copy-start | bytes 393220
  7.2 168.0 %all-gather.2.cloned.1.call-start = ((), (), s32[]{:S(2)}) async-start(), calls=%async_computation.6 | async-start | bytes 6303744 | tf_op jit(solution)/shard_map/all_gather | solution.py:72
  51.6 15.8 %all-to-all-start.1 = ((bf16[8,64,1,512]{3,1,2,0:T(8,128)(2,1)}), bf16[8,64,1,512]{3,1,2,0:T(8,128)(2,1)S(1)}, u32[]{:S(2)}, u32[]{:S(2)}) async-start(bf16[8,64,1,512]{3,1,2,0:T(8,128)(2,1)} %broadcast_in_dim.88), calls=%async_computation.1 | async-start | bytes 1048576 | tf_op jit(solution)/shard_map/all_to_all | solution.py:16
  69.7 1.7 copy-start
  69.7 1.2 copy-start.2
  175.2 3.2 %copy-start.1 = (bf16[512,512]{1,0:T(8,128)(2,1)S(1)}, bf16[512,512]{1,0:T(8,128)(2,1)}, u32[]{:S(2)}) copy-start(bf16[512,512]{1,0:T(8,128)(2,1)} %copy-done) | copy-start | bytes 1572868
  178.3 9.3 %copy-start.5 = (s32[512]{0:T(512)S(1)}, s32[512]{0:T(512)}, u32[]{:S(2)}) copy-start(s32[512]{0:T(512)} %param.10) | copy-start | bytes 6148
  178.3 9.3 %copy-start.6 = (f32[160]{0:T(256)S(1)}, f32[160]{0:T(256)}, u32[]{:S(2)}) copy-start(f32[160]{0:T(256)} %param.13) | copy-start | bytes 1924
  187.6 1.9 copy-start.4
Sparse Core Ops, SparseCore 0:
  12.7 133.9 all-gather.1
where the time goes:
time: 207 us; the launch traced here: 206 us
  blocking collectives  127 us (61%)
  matrix products  21.8 us (11%)
  between operations  16.9 us (8%)
  other arithmetic  13.8 us (7%)
  local copies, waits for them, and re-layouts  11.2 us (5%)
  waiting for transfers between devices  8.97 us (4%)
  starting transfers between devices  6.49 us (3%)
    all_to_all x3, blocking collectives, copy_for_each(): lax.all_to_all(jnp.broadcast_to(array[None], (devices, *array.shape)), ax...  78.4 us
    all_to_all x1, blocking collectives, sum_at_owner(): lax.all_to_all(pieces, axis, split_axis=0, concat_axis=0, tiled=True)  29.9 us
    all_to_all x1, blocking collectives, summed_rows(): lax.all_to_all(nearer, far, split_axis=0, concat_axis=0, tiled=True)  18.8 us
    dot_general x1, matrix products, local(): lax.dot_general(vec_rows, ksb_piece, (((0,), (0,)), ((), ())), preferred_...  9.23 us
    all_to_all x1, waiting for transfers between devices, copy_for_each(): lax.all_to_all(jnp.broadcast_to(array[None], (devices, *array.shape)), ax...  8.95 us
    all_to_all x1, starting transfers between devices, copy_for_each(): lax.all_to_all(jnp.broadcast_to(array[None], (devices, *array.shape)), ax...  6.46 us
    dot_general x1, matrix products, local(): kze_next = jnp.dot(kzs, vec_rows, preferred_element_type=jnp.float32)  4.96 us
  transfers between devices with their start and end apart: 2, of which 1 were waited for; matrix products, arithmetic and copies ran while one was open for 9% of the time, Pallas kernels for 0%

commit v1 on v0

v1 whole, which is shorter than its diff:
```python
import jax
import jax.numpy as jnp
from jax import lax
from jax.sharding import Mesh
from jax.sharding import PartitionSpec as P

Z, Y, X, CORE = "blk", "grid_0", "grid_1", "grid_2"
ALL = (Z, Y, X, CORE)
PLANE = (Z, Y)

SOFTEN = 1.0
SPREAD = 4.0
LARGEST = 3.0e38
TILE = 128


def up_to(size, step):
    return -(-size // step) * step


def exchange(pieces, axis):
    return lax.all_to_all(pieces, axis, 0, 0, tiled=True)


def to_each(array, axis):
    return jnp.broadcast_to(array[None], (lax.axis_size(axis), *array.shape))


def from_other_core(array):
    return lax.ppermute(array, CORE, [(0, 1), (1, 0)])


def squares(rows):
    return jnp.sum(jnp.square(rows.astype(jnp.float32)), axis=1)


def kernel(left, right):
    cross = lax.dot_general(
        left, right, (((1,), (1,)), ((), ())), preferred_element_type=jnp.float32
    )
    apart = squares(left)[:, None] + squares(right)[None, :] - 2.0 * cross
    soft = jnp.minimum(jnp.maximum(apart, 0.0) + SOFTEN, LARGEST)
    return jnp.exp(soft * lax.rsqrt(soft) * (-1.0 / SPREAD)).astype(jnp.bfloat16)


def rounded(array):
    return lax.reduce_precision(array, exponent_bits=8, mantissa_bits=7)


def parts_of(array, count):
    parts = []
    for _ in range(count):
        part = rounded(array)
        parts.append(part.astype(jnp.bfloat16))
        array = array - part
    return parts


def dot(left, right, contract=((1,), (0,))):
    return lax.dot_general(left, right, (contract, ((), ())), preferred_element_type=jnp.float32)


def with_columns(array, columns):
    return jnp.pad(array, [(0, 0)] * (array.ndim - 1) + [(0, columns - array.shape[-1])])


def local(centers, weights, batch_index, labels, sub_index, eigvecs, scales):
    nx, nplane = lax.axis_size(X), lax.axis_size(PLANE)
    held, depth = centers.shape
    classes = weights.shape[1]
    points, rank = eigvecs.shape
    me = lax.axis_index(ALL)
    my_x = lax.axis_index(X)
    my_core = lax.axis_index(CORE)
    block = up_to(-(-classes // nx), TILE)
    ranks = rank // nx
    wide = up_to(block + 2 * ranks + 1, TILE)
    lines = depth // 32

    owner = batch_index // held
    within = batch_index % held
    row = jnp.sum(jnp.where(owner == me, within, 0))
    mine = lax.dynamic_slice(centers, (row, 0), (1, depth))
    picks = sub_index[:, None] == jnp.arange(held, dtype=jnp.int32)[None, :]
    picks = picks.astype(jnp.bfloat16)
    subset = dot(picks, centers).astype(jnp.bfloat16)
    spread_vecs = dot(picks, eigvecs, ((0,), (0,)))

    def by_x(array):
        return jnp.moveaxis(array.reshape(array.shape[0], nx, -1), 1, 0)

    high, low = parts_of(spread_vecs, 2)
    wts = by_x(with_columns(weights.astype(jnp.bfloat16), nx * block))
    room = wide - block - 2 * ranks - 32
    side = jnp.pad(mine.reshape(lines, 32), ((0, held - lines), (room, 0)))
    own_columns = jnp.concatenate([wts, by_x(high), by_x(low), to_each(side, X)], axis=2)
    along_x = exchange(jnp.concatenate([to_each(centers, X), own_columns], axis=2), X)
    opposite = from_other_core(along_x)

    near_rows = along_x[:, :lines, depth + wide - 32 :].reshape(nx, depth)
    half = depth * nx // points
    near_rows = jnp.concatenate(jnp.split(near_rows, points // nx, axis=1), axis=0)
    vec_at = depth + half
    packed = jnp.concatenate([subset, near_rows, eigvecs], axis=1)
    in_plane = exchange(to_each(packed, PLANE), PLANE)
    batch = in_plane[:, :, depth:vec_at].reshape(nplane, points // nx, nx, half)
    batch = jnp.concatenate([batch[:, i] for i in range(points // nx)], axis=2)
    batch = batch.reshape(nplane * nx, depth)
    sub_rows = in_plane[:, :, :depth].reshape(nplane * points, depth)
    vec_rows = in_plane[:, :, vec_at:].reshape(nplane * points, rank)

    here = along_x[:, :, :depth].reshape(nx * held, depth)
    there = opposite[:, :, :depth].reshape(nx * held, depth)
    sums = dot(kernel(batch, here), along_x[:, :, depth:].reshape(nx * held, wide))
    sums = sums + dot(kernel(batch, there), opposite[:, :, depth:].reshape(nx * held, wide))
    arrived = exchange(sums.reshape(nplane, nx, wide), PLANE)

    other_batch = from_other_core(batch)
    kze = dot(kernel(here, sub_rows), vec_rows)
    kze = kze + from_other_core(dot(kernel(there, sub_rows), vec_rows))
    kbz = kernel(centers, batch)
    other_kbz = kernel(centers, other_batch)

    total = jnp.sum(arrived, axis=0)
    first_row = (lax.axis_index(PLANE) * nx + jnp.arange(nx, dtype=jnp.int32)) * 2 + my_core
    row_labels = jnp.sum(jnp.where(owner[None, :] == first_row[:, None], labels[None, :], 0), axis=1)
    mark = row_labels[:, None] == my_x * block + jnp.arange(block, dtype=jnp.int32)[None, :]
    at_label = jnp.sum(jnp.where(mark, total[:, :block] - 1.0, 0.0), axis=1, keepdims=True)
    proj = total[:, block : block + ranks] + total[:, block + ranks : block + 2 * ranks]
    proj_high, proj_low = parts_of(proj, 2)
    ready = jnp.concatenate(
        [total[:, :block].astype(jnp.bfloat16), proj_high, proj_low, at_label.astype(jnp.bfloat16)],
        axis=1,
    )
    rows = exchange(to_each(with_columns(ready, wide), PLANE), PLANE).reshape(-1, wide)

    kze_parts = with_columns(jnp.concatenate(parts_of(kze, 2), axis=1), wide)
    last = jnp.concatenate([to_each(rows, X), kze_parts.reshape(nx, held, wide)], axis=1)
    last = exchange(last, X)
    own_half = last[:, : nplane * nx]
    other_half = from_other_core(own_half)
    kze_sum = jnp.sum(last[:, nplane * nx :].astype(jnp.float32), axis=0)
    kze_sum = kze_sum[:, :rank] + kze_sum[:, rank : 2 * rank]
    left = jnp.concatenate([kze_sum, -eigvecs.astype(jnp.float32)], axis=0) * scales[None, :]

    numbers = jnp.arange(nplane * nx, dtype=jnp.int32)
    gradient, predictions = 0.0, 0.0
    for half_rows, core, near in ((own_half, my_core, kbz), (other_half, 1 - my_core, other_kbz)):
        devices = numbers * 2 + core
        chosen = owner[:, None] == devices[None, :]
        label = jnp.sum(jnp.where(chosen, labels[:, None], 0), axis=0)
        pred = jnp.concatenate([half_rows[i, :, :block] for i in range(nx)], axis=1)[:, :classes]
        predictions = predictions + dot(chosen.astype(jnp.bfloat16), pred)
        at = half_rows[:, :, block + 2 * ranks]
        column = jnp.arange(classes, dtype=jnp.int32)[None, :]
        mark = label[:, None] == column
        value = jnp.sum(
            jnp.where((label // block)[None, :] == jnp.arange(nx)[:, None], at.astype(jnp.float32), 0.0),
            axis=0,
        )
        resid = jnp.where(mark, value[:, None].astype(jnp.bfloat16), pred)
        proj = half_rows[:, :, block : block + ranks].astype(jnp.float32)
        proj = proj + half_rows[:, :, block + ranks : block + 2 * ranks].astype(jnp.float32)
        proj = jnp.moveaxis(proj, 0, 1).reshape(nplane * nx, rank)
        back = lax.dot_general(
            left, proj, (((1,), (1,)), ((), ())), precision=lax.Precision.HIGHEST
        )
        near = jnp.pad(near.astype(jnp.float32), ((0, points), (0, 0)))
        pieces = parts_of(near - back, 3)
        gradient = gradient + sum(dot(piece, resid) for piece in pieces)
    center_grad = gradient[:held].astype(jnp.bfloat16)
    return (predictions.astype(jnp.bfloat16), center_grad, gradient[held:])


def solution(mesh):
    finer = Mesh(mesh.devices.reshape(mesh.shape["blk"], 8, 4, 2), ALL)
    return jax.shard_map(
        local,
        mesh=finer,
        in_specs=(
            P(ALL, None),
            P(ALL, None),
            P(),
            P(),
            P(ALL),
            P(ALL, None),
            P(),
        ),
        out_specs=(P(), P(ALL, None), P(ALL, None)),
        check_vma=False,
    )
```

time: 207 us -> 154 us (0.74)
  blocking collectives: 127 us -> 0 us
  starting transfers between devices: 6.49 us -> 65.6 us
  waiting for transfers between devices: 8.97 us -> 48.4 us
  between operations: 16.9 us -> 3.17 us
  matrix products: 21.8 us -> 16 us
  other arithmetic: 13.8 us -> 8.68 us
    all_to_all x5 -> x0, blocking collectives: 127 us -> none  [the longest x3 78.4 us: copy_for_each(): lax.all_to_all(jnp.broadcast_to(array[None], (devices, *array.shape)), ax...]
    all_to_all x1 -> x5, waiting for transfers between devices: 8.95 us -> 47.6 us  [exchange(): return lax.all_to_all(pieces, axis, 0, 0, tiled=True)]
    all_to_all x1 -> x5, starting transfers between devices: 6.46 us -> 43.9 us  [exchange(): return lax.all_to_all(pieces, axis, 0, 0, tiled=True)]
    ppermute x0 -> x4, starting transfers between devices: none -> 21.7 us  [from_other_core(): return lax.ppermute(array, CORE, [(0, 1), (1, 0)])]
    dot_general x7 -> x16, matrix products: 21.4 us -> 14.9 us  [the longest x14 13.4 us: dot(): lax.dot_general(left, right, (contract, ((), ())), preferred_element_type...]
    gather x3 -> x0, local copies, waits for them, and re-layouts: 4.05 us -> none  [the longest x1 1.97 us: local(): batch = jnp.take(gathered, owner * share + earlier, axis=0)]
    sort x1 -> x0, other arithmetic: 3.77 us -> none  [local(): jnp.argsort((owner != myself).astype(jnp.int32), stable=True)[:share]]
    slice x1 -> x11, local copies, waits for them, and re-layouts: 0.51 us -> 2.59 us  [the longest x1 0.92 us: local(): there = opposite[:, :, :depth].reshape(nx * held, depth)]
  transfers between devices with their start and end apart: 2 -> 9, of which waited for: 1 -> 6; matrix products, arithmetic and copies ran while one was open for 9% -> 9% of each run, Pallas kernels for 0% -> 0%
where the time goes in v1:
time: 154 us
  starting transfers between devices  65.6 us (43%)
  waiting for transfers between devices  48.4 us (31%)
  matrix products  16 us (10%)
  local copies, waits for them, and re-layouts  11.7 us (8%)
  other arithmetic  8.68 us (6%)
  between operations  3.17 us (2%)
    all_to_all x5, waiting for transfers between devices, exchange(): return lax.all_to_all(pieces, axis, 0, 0, tiled=True)  47.6 us
    all_to_all x5, starting transfers between devices, exchange(): return lax.all_to_all(pieces, axis, 0, 0, tiled=True)  43.9 us
    ppermute x4, starting transfers between devices, from_other_core(): return lax.ppermute(array, CORE, [(0, 1), (1, 0)])  21.7 us
    dot_general x14, matrix products, dot(): lax.dot_general(left, right, (contract, ((), ())), preferred_element_type...  13.4 us
  transfers between devices with their start and end apart: 9, of which 6 were waited for; matrix products, arithmetic and copies ran while one was open for 9% of the time, Pallas kernels for 0%

profile of v1, /device:TPU:1, one launch (start us, length us, event | category | flops | bytes accessed | tf_op | source)
XLA Modules:
  0.0 153.5 jit_solution(3545265726352122585)
XLA Ops:
  0.6 1.3 fusion.120
  4.7 1.0 fusion.102
  6.0 1.1 convert_element_type.171
  7.4 1.1 concatenate.35
  8.5 5.0 %all-to-all-start = ((bf16[4,128,896]{2,1,0:T(8,128)(2,1)}), bf16[4,128,896]{2,1,0:T(8,128)(2,1)S(1)}, u32[]{:S(2)}, u32[]{:S(2)}) async-start(bf16[4,128,896]{2,1,0:T(8,128)(2,1)} %concatenate.35), calls=%async_computation | async-start | bytes 1835008 | tf_op jit(solution)/shard_map/all_to_all | solution.py:22
  13.7 8.9 %all-to-all-done = bf16[4,128,896]{2,1,0:T(8,128)(2,1)S(1)} async-done(((bf16[4,128,896]{2,1,0:T(8,128)(2,1)}), bf16[4,128,896]{2,1,0:T(8,128)(2,1)S(1)}, u32[]{:S(2)}, u32[]{:S(2)}) %all-to-all-start) | async-done | bytes 917536 | tf_op jit(solution)/shard_map/all_to_all | solution.py:22
  22.7 1.1 broadcast_in_dim.56
  23.8 20.2 %all-to-all-start.1 = ((bf16[64,8,928]{2,1,0:T(8,128)(2,1)}), bf16[64,8,928]{2,1,0:T(8,128)(2,1)S(1)}, u32[]{:S(2)}, u32[]{:S(2)}) async-start(bf16[64,8,928]{2,1,0:T(8,128)(2,1)} %broadcast_in_dim.56), calls=%async_computation.1 | async-start | bytes 2097152 | tf_op jit(solution)/shard_map/all_to_all | solution.py:22
  44.1 4.0 %collective-permute-start = (bf16[4,128,896]{2,1,0:T(8,128)(2,1)S(1)}, bf16[4,128,896]{2,1,0:T(8,128)(2,1)S(1)}, u32[]{:S(2)}, u32[]{:S(2)}) collective-permute-start(bf16[4,128,896]{2,1,0:T(8,128)(2,1)S(1)} %all-to-all-done), channel_id=1, source_target_pairs={{0,1},{1,0},{2,3},{3,2},{4,5},{5,4},{6,7},{7,6},{8,9},{9,8},{10,11... | collective-permute-start | bytes 2752520 | tf_op jit(solution)/shard_map/ppermute | solution.py:30
  51.7 0.9 slice.155
  52.8 17.2 %all-to-all-done.1 = bf16[64,8,928]{2,1,0:T(8,128)(2,1)S(1)} async-done(((bf16[64,8,928]{2,1,0:T(8,128)(2,1)}), bf16[64,8,928]{2,1,0:T(8,128)(2,1)S(1)}, u32[]{:S(2)}, u32[]{:S(2)}) %all-to-all-start.1) | async-done | bytes 950304 | tf_op jit(solution)/shard_map/all_to_all | solution.py:22
  70.7 2.5 %fusion.41 = f32[256,384]{1,0:T(8,128)} fusion(bf16[512,384]{1,0:T(8,128)(2,1)} %bitcast.107, bf16[256,512]{1,0:T(8,128)(2,1)S(1)} %constant_dynamic-update-slice_fusion, bf16[512,512]{1,0:T(8,128)(2,1)S(1)} %bitcast.103, f32[512]{0:T(512)S(1)} %bitcast.110, f32[256]{0:T(256)S(1)} %multiply_reduce_fusion.4), kind=kOutput, calls=%fused_computation.67 | convolution fusion | flops 236060672 | bytes 1575936 | tf_op jit(solution)/shard_map/dot_general | solution.py:60
  73.3 1.7 %convolution_add_fusion.4 = f32[256,384]{1,0:T(8,128)S(1)} fusion(f32[256,384]{1,0:T(8,128)} %fusion.41, bf16[512,384]{1,0:T(8,128)(2,1)S(1)} %bitcast.95, bf16[256,512]{1,0:T(8,128)(2,1)S(1)} %constant_dynamic-update-slice_fusion, bf16[512,512]{1,0:T(8,128)(2,1)S(1)} %bitcast.105, f32[512]{0:T(512)S(1)} %bitcast.112, f32[256]{0:T(256)S(1)} %multiply_reduce_fusion.4), kind=kOutput, calls=%fused_computation.36 | convolution fusion | flops 236158976 | bytes 1969152 | tf_op jit(solution)/shard_map/dot_general | solution.py:60
  75.0 0.9 reshape.174
  75.8 8.6 %all-to-all-start.2 = ((f32[64,4,384]{2,1,0:T(4,128)}), f32[64,4,384]{2,1,0:T(4,128)S(1)}, u32[]{:S(2)}, u32[]{:S(2)}) async-start(f32[64,4,384]{2,1,0:T(4,128)} %reshape.174), calls=%async_computation.2 | async-start | bytes 786432 | tf_op jit(solution)/shard_map/all_to_all | solution.py:22
  84.9 1.7 %fusion.15 = f32[512,160]{0,1:T(8,128)} fusion(bf16[512,512]{1,0:T(8,128)(2,1)S(1)} %bitcast.106, f32[512]{0:T(512)S(1)} %bitcast.113, f32[512]{0:T(512)S(1)} %add.254, bf16[64,8,928]{2,1,0:T(8,128)(2,1)S(1)} %all-to-all-done.1), kind=kOutput, calls=%fused_computation.24 | convolution fusion | flops 354680832 | bytes 1642496 | tf_op jit(solution)/shard_map/dot_general | solution.py:60
  86.7 4.4 %collective-permute-start.1 = (f32[512,160]{0,1:T(8,128)}, f32[512,160]{0,1:T(8,128)S(1)}, u32[]{:S(2)}, u32[]{:S(2)}) collective-permute-start(f32[512,160]{0,1:T(8,128)} %fusion.15), channel_id=1, source_target_pairs={{0,1},{1,0},{2,3},{3,2},{4,5},{5,4},{6,7},{7,6},{8,9},{9,8},{10,11... | collective-permute-start | bytes 983048 | tf_op jit(solution)/shard_map/ppermute | solution.py:30
  91.1 7.0 %all-to-all-done.2 = f32[64,4,384]{2,1,0:T(4,128)S(1)} async-done(((f32[64,4,384]{2,1,0:T(4,128)}), f32[64,4,384]{2,1,0:T(4,128)S(1)}, u32[]{:S(2)}, u32[]{:S(2)}) %all-to-all-start.2) | async-done | bytes 393248 | tf_op jit(solution)/shard_map/all_to_all | solution.py:22
  99.3 6.4 %all-to-all-start.3 = ((bf16[64,4,384]{2,1,0:T(4,128)(2,1)}), bf16[64,4,384]{2,1,0:T(4,128)(2,1)S(1)}, u32[]{:S(2)}, u32[]{:S(2)}) async-start(bf16[64,4,384]{2,1,0:T(4,128)(2,1)} %broadcast_in_dim.64), calls=%async_computation.3 | async-start | bytes 393216 | tf_op jit(solution)/shard_map/all_to_all | solution.py:22
  105.7 1.0 fusion.16
  107.2 10.6 %all-to-all-done.3 = bf16[64,4,384]{2,1,0:T(4,128)(2,1)S(1)} async-done(((bf16[64,4,384]{2,1,0:T(4,128)(2,1)}), bf16[64,4,384]{2,1,0:T(4,128)(2,1)S(1)}, u32[]{:S(2)}, u32[]{:S(2)}) %all-to-all-start.3) | async-done | bytes 196640 | tf_op jit(solution)/shard_map/all_to_all | solution.py:22
  117.9 1.1 pad_maximum_fusion
  119.0 3.7 %all-to-all-start.4 = ((bf16[4,384,384]{2,1,0:T(8,128)(2,1)}), bf16[4,384,384]{2,1,0:T(8,128)(2,1)S(1)}, u32[]{:S(2)}, u32[]{:S(2)}) async-start(bf16[4,384,384]{2,1,0:T(8,128)(2,1)} %pad_maximum_fusion), calls=%async_computation.4 | async-start | bytes 2359296 | tf_op jit(solution)/shard_map/all_to_all | solution.py:22
  122.7 6.0 %collective-permute-start.3 = (bf16[256,512]{1,0:T(8,128)(2,1)S(1)}, bf16[256,512]{1,0:T(8,128)(2,1)S(1)}, u32[]{:S(2)}, u32[]{:S(2)}) collective-permute-start(bf16[256,512]{1,0:T(8,128)(2,1)S(1)} %constant_dynamic-update-slice_fusion), channel_id=1, source_target_pairs={{0,1},{1,0},{2,3},{3,2},{4,5},{5,4},{6,7},{7,6},{8,9},{9,8},{10,11... | collective-permute-start | bytes 786440 | tf_op jit(solution)/shard_map/ppermute | solution.py:30
  130.0 0.9 fusion.100
  130.9 4.0 %all-to-all-done.4 = bf16[4,384,384]{2,1,0:T(8,128)(2,1)S(1)} async-done(((bf16[4,384,384]{2,1,0:T(8,128)(2,1)}), bf16[4,384,384]{2,1,0:T(8,128)(2,1)S(1)}, u32[]{:S(2)}, u32[]{:S(2)}) %all-to-all-start.4) | async-done | bytes 1179680 | tf_op jit(solution)/shard_map/all_to_all | solution.py:22
  135.4 7.3 %collective-permute-start.2 = (bf16[4,256,384]{2,1,0:T(8,128)(2,1)S(1)}, bf16[4,256,384]{2,1,0:T(8,128)(2,1)S(1)}, u32[]{:S(2)}, u32[]{:S(2)}) collective-permute-start(bf16[4,256,384]{2,1,0:T(8,128)(2,1)S(1)} %slice.166), channel_id=1, source_target_pairs={{0,1},{1,0},{2,3},{3,2},{4,5},{5,4},{6,7},{7,6},{8,9},{9,8},{10,11... | collective-permute-start | bytes 2359304 | tf_op jit(solution)/shard_map/ppermute | solution.py:30
  144.2 1.2 convolution_add_fusion.2
  146.2 0.8 copy.59
  147.3 1.2 convolution_subtract_fusion
  151.1 0.9 copy.60
  152.0 1.5 %add_convert_fusion = bf16[512,1000]{0,1:T(8,128)(2,1)} fusion(f32[512,1000]{0,1:T(8,128)S(1)} %fusion.43, s32[256]{0:T(256)S(1)} %copy-done.13, s32[512]{0:T(512)S(1)} %get-tuple-element.21, bf16[256,256]{1,0:T(8,128)(2,1)S(1)} %get-tuple-element.27, bf16[256,256]{1,0:T(8,128)(2,1)S(1)} %get-tuple-element.28, bf16[256,256]{1,0:T(8,128)(2,1)S(1)} %get-tuple-element.29, ...), kind=kOutput, calls=%fused_computation | convolution fusion | flops 265347072 | bytes 3599360 | tf_op jit(solution)/shard_map/dot_general | solution.py:60
  (120 shorter events, 15.1 us)
Async XLA Ops:
  5.7 1.6 %copy-start.1 = (bf16[128,512]{1,0:T(8,128)(2,1)S(1)}, bf16[128,512]{1,0:T(8,128)(2,1)}, u32[]{:S(2)}) copy-start(bf16[128,512]{1,0:T(8,128)(2,1)} %param.7) | copy-start | bytes 393220
  8.5 5.0 %copy-start.18 = (s32[8]{0:T(128)S(1)}, s32[8]{0:T(128)}, u32[]{:S(2)}) copy-start(s32[8]{0:T(128)} %param.11) | copy-start | bytes 100
  8.5 14.2 %copy-start.3 = (bf16[8,160]{1,0:T(8,128)(2,1)S(1)}, bf16[8,160]{1,0:T(8,128)(2,1)}, u32[]{:S(2)}) copy-start(bf16[8,160]{1,0:T(8,128)(2,1)} %param.12) | copy-start | bytes 7684
  8.5 14.0 %all-to-all-start = ((bf16[4,128,896]{2,1,0:T(8,128)(2,1)}), bf16[4,128,896]{2,1,0:T(8,128)(2,1)S(1)}, u32[]{:S(2)}, u32[]{:S(2)}) async-start(bf16[4,128,896]{2,1,0:T(8,128)(2,1)} %concatenate.35), calls=%async_computation | async-start | bytes 1835008 | tf_op jit(solution)/shard_map/all_to_all | solution.py:22
  23.8 24.9 %copy-start.4 = (s32[512]{0:T(512)S(1)}, s32[512]{0:T(512)}, u32[]{:S(2)}) copy-start(s32[512]{0:T(512)} %param.10) | copy-start | bytes 6148
  23.8 46.2 %all-to-all-start.1 = ((bf16[64,8,928]{2,1,0:T(8,128)(2,1)}), bf16[64,8,928]{2,1,0:T(8,128)(2,1)S(1)}, u32[]{:S(2)}, u32[]{:S(2)}) async-start(bf16[64,8,928]{2,1,0:T(8,128)(2,1)} %broadcast_in_dim.56), calls=%async_computation.1 | async-start | bytes 2097152 | tf_op jit(solution)/shard_map/all_to_all | solution.py:22
  44.1 7.6 %collective-permute-start = (bf16[4,128,896]{2,1,0:T(8,128)(2,1)S(1)}, bf16[4,128,896]{2,1,0:T(8,128)(2,1)S(1)}, u32[]{:S(2)}, u32[]{:S(2)}) collective-permute-start(bf16[4,128,896]{2,1,0:T(8,128)(2,1)S(1)} %all-to-all-done), channel_id=1, source_target_pairs={{0,1},{1,0},{2,3},{3,2},{4,5},{5,4},{6,7},{7,6},{8,9},{9,8},{10,11... | collective-permute-start | bytes 2752520 | tf_op jit(solution)/shard_map/ppermute | solution.py:30
  48.1 3.6 %copy-start.6 = (s32[256]{0:T(256)}, s32[256]{0:T(256)S(1)}, u32[]{:S(2)}) copy-start(s32[256]{0:T(256)S(1)} %fusion.125) | copy-start | bytes 3076
  48.1 2.0 %copy-start.12 = (s32[256]{0:T(256)}, s32[256]{0:T(256)S(1)}, u32[]{:S(2)}) copy-start(s32[256]{0:T(256)S(1)} %fusion.124) | copy-start | bytes 3076
  49.5 0.6 copy-start.9
  51.7 1.1 copy-start
  52.8 20.4 %copy-start.15 = (f32[4,128]{1,0:T(4,128)}, f32[4,128]{1,0:T(4,128)S(1)}, u32[]{:S(2)}) copy-start(f32[4,128]{1,0:T(4,128)S(1)} %multiply_reduce_fusion.1) | copy-start | bytes 6148
  70.0 0.7 copy-start.14
  70.7 2.5 %slice-start = ((bf16[4,128,896]{2,1,0:T(8,128)(2,1)}), bf16[4,128,384]{2,1,0:T(8,128)(2,1)S(1)}, s32[]{:S(2)}) async-start(bf16[4,128,896]{2,1,0:T(8,128)(2,1)} %copy-done), calls=%async_computation.5 | async-start | bytes 786432 | tf_op jit(solution)/shard_map/slice | solution.py:115
  70.7 2.5 %copy-start.2 = (bf16[4,128,512]{2,1,0:T(8,128)(2,1)S(1)}, bf16[4,128,512]{2,1,0:T(8,128)(2,1)}, u32[]{:S(2)}) copy-start(bf16[4,128,512]{2,1,0:T(8,128)(2,1)} %slice.155) | copy-start | bytes 1572868
  74.9 10.0 %copy-start.16 = (f32[4,128]{1,0:T(4,128)S(1)}, f32[4,128]{1,0:T(4,128)}, u32[]{:S(2)}) copy-start(f32[4,128]{1,0:T(4,128)} %copy-done.15) | copy-start | bytes 6148
  75.8 22.2 %all-to-all-start.2 = ((f32[64,4,384]{2,1,0:T(4,128)}), f32[64,4,384]{2,1,0:T(4,128)S(1)}, u32[]{:S(2)}, u32[]{:S(2)}) async-start(f32[64,4,384]{2,1,0:T(4,128)} %reshape.174), calls=%async_computation.2 | async-start | bytes 786432 | tf_op jit(solution)/shard_map/all_to_all | solution.py:22
  84.9 13.3 %copy-start.17 = (s32[256]{0:T(256)S(1)}, s32[256]{0:T(256)}, u32[]{:S(2)}) copy-start(s32[256]{0:T(256)} %iota_add_fusion) | copy-start | bytes 3076
  86.7 20.1 %collective-permute-start.1 = (f32[512,160]{0,1:T(8,128)}, f32[512,160]{0,1:T(8,128)S(1)}, u32[]{:S(2)}, u32[]{:S(2)}) collective-permute-start(f32[512,160]{0,1:T(8,128)} %fusion.15), channel_id=1, source_target_pairs={{0,1},{1,0},{2,3},{3,2},{4,5},{5,4},{6,7},{7,6},{8,9},{9,8},{10,11... | collective-permute-start | bytes 983048 | tf_op jit(solution)/shard_map/ppermute | solution.py:30
  99.3 18.4 %all-to-all-start.3 = ((bf16[64,4,384]{2,1,0:T(4,128)(2,1)}), bf16[64,4,384]{2,1,0:T(4,128)(2,1)S(1)}, u32[]{:S(2)}, u32[]{:S(2)}) async-start(bf16[64,4,384]{2,1,0:T(4,128)(2,1)} %broadcast_in_dim.64), calls=%async_computation.3 | async-start | bytes 393216 | tf_op jit(solution)/shard_map/all_to_all | solution.py:22
  119.0 3.7 %copy-start.11 = (s32[256]{0:T(256)S(1)}, s32[256]{0:T(256)}, u32[]{:S(2)}) copy-start(s32[256]{0:T(256)} %get-tuple-element.19) | copy-start | bytes 3076
  119.0 15.8 %all-to-all-start.4 = ((bf16[4,384,384]{2,1,0:T(8,128)(2,1)}), bf16[4,384,384]{2,1,0:T(8,128)(2,1)S(1)}, u32[]{:S(2)}, u32[]{:S(2)}) async-start(bf16[4,384,384]{2,1,0:T(8,128)(2,1)} %pad_maximum_fusion), calls=%async_computation.4 | async-start | bytes 2359296 | tf_op jit(solution)/shard_map/all_to_all | solution.py:22
  122.7 7.2 %collective-permute-start.3 = (bf16[256,512]{1,0:T(8,128)(2,1)S(1)}, bf16[256,512]{1,0:T(8,128)(2,1)S(1)}, u32[]{:S(2)}, u32[]{:S(2)}) collective-permute-start(bf16[256,512]{1,0:T(8,128)(2,1)S(1)} %constant_dynamic-update-slice_fusion), channel_id=1, source_target_pairs={{0,1},{1,0},{2,3},{3,2},{4,5},{5,4},{6,7},{7,6},{8,9},{9,8},{10,11... | collective-permute-start | bytes 786440 | tf_op jit(solution)/shard_map/ppermute | solution.py:30
  135.2 7.9 %copy-start.5 = (f32[160]{0:T(256)S(1)}, f32[160]{0:T(256)}, u32[]{:S(2)}) copy-start(f32[160]{0:T(256)} %param.13) | copy-start | bytes 1924
  135.4 10.6 %collective-permute-start.2 = (bf16[4,256,384]{2,1,0:T(8,128)(2,1)S(1)}, bf16[4,256,384]{2,1,0:T(8,128)(2,1)S(1)}, u32[]{:S(2)}, u32[]{:S(2)}) collective-permute-start(bf16[4,256,384]{2,1,0:T(8,128)(2,1)S(1)} %slice.166), channel_id=1, source_target_pairs={{0,1},{1,0},{2,3},{3,2},{4,5},{5,4},{6,7},{7,6},{8,9},{9,8},{10,11... | collective-permute-start | bytes 2359304 | tf_op jit(solution)/shard_map/ppermute | solution.py:30
  144.2 1.2 copy-start.7
  146.0 1.3 copy-start.8
  146.2 2.4 %copy-start.10 = (s32[256]{0:T(256)S(1)}, s32[256]{0:T(256)}, u32[]{:S(2)}) copy-start(s32[256]{0:T(256)} %copy-done.9) | copy-start | bytes 3076
  149.0 1.1 copy-start.19
  150.0 1.9 %copy-start.13 = (s32[256]{0:T(256)S(1)}, s32[256]{0:T(256)}, u32[]{:S(2)}) copy-start(s32[256]{0:T(256)} %copy-done.12) | copy-start | bytes 3076

commit v2 on v1

v2 whole, which is shorter than its diff:
```python
import jax
import jax.numpy as jnp
from jax import lax
from jax.sharding import Mesh
from jax.sharding import PartitionSpec as P

Z, Y, X, CORE = "blk", "grid_0", "grid_1", "grid_2"
ALL = (Z, Y, X, CORE)
PLANE = (Z, Y)

SOFTEN = 1.0
SPREAD = 4.0
LARGEST = 3.0e38
TILE = 128


def up_to(size, step):
    return -(-size // step) * step


def exchange(pieces, axis):
    return lax.all_to_all(pieces, axis, 0, 0, tiled=True)


def to_each(array, axis):
    return jnp.broadcast_to(array[None], (lax.axis_size(axis), *array.shape))


def from_other_core(array):
    return lax.ppermute(array, CORE, [(0, 1), (1, 0)])


def to_next(array, axis, step):
    count = lax.axis_size(axis)
    return lax.ppermute(array, axis, [(i, (i + step) % count) for i in range(count)])


def squares(rows):
    return jnp.sum(jnp.square(rows.astype(jnp.float32)), axis=1)


def kernel(left, right):
    cross = lax.dot_general(
        left, right, (((1,), (1,)), ((), ())), preferred_element_type=jnp.float32
    )
    apart = squares(left)[:, None] + squares(right)[None, :] - 2.0 * cross
    soft = jnp.minimum(jnp.maximum(apart, 0.0) + SOFTEN, LARGEST)
    return jnp.exp(soft * lax.rsqrt(soft) * (-1.0 / SPREAD)).astype(jnp.bfloat16)


def rounded(array):
    return lax.reduce_precision(array, exponent_bits=8, mantissa_bits=7)


def parts_of(array, count):
    parts = []
    for _ in range(count):
        part = rounded(array)
        parts.append(part.astype(jnp.bfloat16))
        array = array - part
    return parts


def dot(left, right, contract=((1,), (0,))):
    return lax.dot_general(left, right, (contract, ((), ())), preferred_element_type=jnp.float32)


def with_columns(array, columns):
    return jnp.pad(array, [(0, 0)] * (array.ndim - 1) + [(0, columns - array.shape[-1])])


def step(centers, weights, batch_index, labels, sub_index, eigvecs, scales):
    nx, nplane = lax.axis_size(X), lax.axis_size(PLANE)
    held, depth = centers.shape
    classes = weights.shape[1]
    points, rank = eigvecs.shape
    me = lax.axis_index(ALL)
    my_x = lax.axis_index(X)
    my_core = lax.axis_index(CORE)
    block = up_to(-(-classes // nx), TILE)
    ranks = rank // nx
    wide = up_to(block + 2 * ranks + 1, TILE)
    half = nplane * nx
    label_at = 2 * ranks

    owner = batch_index // held
    within = batch_index % held
    row = jnp.sum(jnp.where(owner == me, within, 0))
    mine = lax.dynamic_slice(centers, (row, 0), (1, depth))
    picks = sub_index[:, None] == jnp.arange(held, dtype=jnp.int32)[None, :]
    picks = picks.astype(jnp.bfloat16)
    subset = dot(picks, centers).astype(jnp.bfloat16)
    packed = jnp.concatenate([subset, eigvecs, mine.reshape(points, -1)], axis=1)
    in_plane = exchange(to_each(packed, PLANE), PLANE)
    sub_rows = in_plane[:, :, :depth].reshape(nplane * points, depth)
    vec_rows = in_plane[:, :, depth : depth + rank].reshape(nplane * points, rank)
    column = in_plane[:, :, depth + rank :].reshape(nplane, depth)
    batch = exchange(to_each(column, X), X).reshape(half, depth)

    def by_x(array):
        return jnp.moveaxis(array.reshape(array.shape[0], nx, -1), 1, 0)

    high, low = parts_of(dot(picks, eigvecs, ((0,), (0,))), 2)
    wts = by_x(with_columns(weights.astype(jnp.bfloat16), nx * block))
    shares = with_columns(jnp.concatenate([wts, by_x(high), by_x(low)], axis=2), wide)

    def share_for(x):
        share = lax.dynamic_index_in_dim(shares, x % nx, 0, keepdims=False)
        return jnp.concatenate([centers, share], axis=1)

    around = [share_for(my_x)] + [to_next(share_for(my_x + k), X, k) for k in range(1, nx)]
    around = jnp.concatenate(around, axis=0)
    opposite = from_other_core(around)
    here, there = around[:, :depth], opposite[:, :depth]

    sums = dot(kernel(batch, here), around[:, depth:])
    sums = sums + dot(kernel(batch, there), opposite[:, depth:])
    arrived = exchange(sums.reshape(nplane, nx, wide), PLANE)

    other_batch = from_other_core(batch)
    kze = dot(kernel(here, sub_rows), vec_rows)
    kze = kze + from_other_core(dot(kernel(there, sub_rows), vec_rows))
    kze_sum = kze[:held]
    for k in range(1, nx):
        kze_sum = kze_sum + to_next(kze[k * held : (k + 1) * held], X, -k)
    kbz = kernel(centers, batch)
    other_kbz = kernel(centers, other_batch)

    def device_of(number, core):
        return (number % nplane * nx + number // nplane) * 2 + core

    total = jnp.sum(arrived, axis=0)
    numbers = lax.axis_index(PLANE) * nx + jnp.arange(nx, dtype=jnp.int32)
    found = owner[None, :] == device_of(numbers, my_core)[:, None]
    row_labels = jnp.sum(jnp.where(found, labels[None, :], 0), axis=1)
    mark = row_labels[:, None] == my_x * block + jnp.arange(block, dtype=jnp.int32)[None, :]
    at_label = jnp.sum(jnp.where(mark, total[:, :block] - 1.0, 0.0), axis=1, keepdims=True)
    proj = total[:, block : block + ranks] + total[:, block + ranks : block + 2 * ranks]
    ready = [total[:, :block].astype(jnp.bfloat16), *parts_of(proj, 2), at_label.astype(jnp.bfloat16)]
    ready = with_columns(jnp.concatenate(ready, axis=1), wide)
    rows = exchange(to_each(ready, PLANE), PLANE).reshape(half, wide)
    own_half = exchange(to_each(rows, X), X)
    other_half = from_other_core(own_half)

    left = jnp.concatenate([kze_sum, -eigvecs.astype(jnp.float32)], axis=0) * scales[None, :]
    left = left.reshape(held + points, nx, ranks)
    left = with_columns(jnp.concatenate([left, left], axis=2), wide - block)
    left = parts_of(left.reshape(held + points, nx * (wide - block)), 2)

    numbers = jnp.arange(half, dtype=jnp.int32)
    gradient, predictions = 0.0, 0.0
    for half_rows, core, near in ((own_half, my_core, kbz), (other_half, 1 - my_core, other_kbz)):
        chosen = owner[:, None] == device_of(numbers, core)[None, :]
        label = jnp.sum(jnp.where(chosen, labels[:, None], 0), axis=0)
        pred = jnp.concatenate([half_rows[i, :, :block] for i in range(nx)], axis=1)[:, :classes]
        predictions = predictions + dot(chosen.astype(jnp.bfloat16), pred)
        value = half_rows[:, :, block + label_at].astype(jnp.float32).sum(axis=0)
        mark = label[:, None] == jnp.arange(classes, dtype=jnp.int32)[None, :]
        resid = jnp.where(mark, value[:, None].astype(jnp.bfloat16), pred)
        proj = jnp.concatenate([half_rows[i, :, block:] for i in range(nx)], axis=1)
        back = sum(dot(piece, proj, ((1,), (1,))) for piece in left)
        near = jnp.pad(near.astype(jnp.float32), ((0, points), (0, 0)))
        gradient = gradient + sum(dot(piece, resid) for piece in parts_of(near - back, 2))
    center_grad = gradient[:held].astype(jnp.bfloat16)
    return (predictions.astype(jnp.bfloat16), center_grad, gradient[held:])


def solution(mesh):
    finer = Mesh(mesh.devices.reshape(mesh.shape["blk"], 8, 4, 2), ALL)
    return jax.shard_map(
        step,
        mesh=finer,
        in_specs=(
            P(ALL, None),
            P(ALL, None),
            P(),
            P(),
            P(ALL),
            P(ALL, None),
            P(),
        ),
        out_specs=(P(), P(ALL, None), P(ALL, None)),
        check_vma=False,
    )
```

time: 154 us -> 149 us (0.968)
  starting transfers between devices: 65.6 us -> 82.1 us
  waiting for transfers between devices: 48.4 us -> 36.8 us
  other arithmetic: 8.68 us -> 4.43 us
  local copies, waits for them, and re-layouts: 11.7 us -> 7.64 us
  matrix products: 16 us -> 13.9 us
    ppermute x0 -> x6, starting transfers between devices: none -> 19.2 us  [to_next(): lax.ppermute(array, axis, [(i, (i + step) % count) for i in range(count)])]
    all_to_all x5, waiting for transfers between devices: 47.6 us -> 35.4 us  [exchange(): return lax.all_to_all(pieces, axis, 0, 0, tiled=True)]
    all_to_all x5, starting transfers between devices: 43.9 us -> 41.5 us  [exchange(): return lax.all_to_all(pieces, axis, 0, 0, tiled=True)]
    slice x11 -> x5, local copies, waits for them, and re-layouts: 2.59 us -> 0.77 us  [the longest x1 0.62 us: step(): return (predictions.astype(jnp.bfloat16), center_grad, gradient[held:])]
    dot_general x14 -> x16, matrix products: 13.4 us -> 12.7 us  [dot(): lax.dot_general(left, right, (contract, ((), ())), preferred_element_type...]
  transfers between devices with their start and end apart: 9 -> 15, of which waited for: 6 -> 4; matrix products, arithmetic and copies ran while one was open for 9% -> 11% of each run, Pallas kernels for 0% -> 0%
where the time goes in v2:
time: 149 us; the launch traced here: 148 us
  starting transfers between devices  82.1 us (55%)
  waiting for transfers between devices  36.8 us (25%)
  matrix products  13.9 us (9%)
  local copies, waits for them, and re-layouts  7.64 us (5%)
  other arithmetic  4.43 us (3%)
  between operations  3.26 us (2%)
    all_to_all x5, starting transfers between devices, exchange(): return lax.all_to_all(pieces, axis, 0, 0, tiled=True)  41.5 us
    all_to_all x5, waiting for transfers between devices, exchange(): return lax.all_to_all(pieces, axis, 0, 0, tiled=True)  35.4 us
    ppermute x4, starting transfers between devices, from_other_core(): return lax.ppermute(array, CORE, [(0, 1), (1, 0)])  21.4 us
    ppermute x6, starting transfers between devices, to_next(): lax.ppermute(array, axis, [(i, (i + step) % count) for i in range(count)])  19.2 us
    dot_general x16, matrix products, dot(): lax.dot_general(left, right, (contract, ((), ())), preferred_element_type...  12.7 us
    broadcast_in_dim x6, local copies, waits for them, and re-layouts, to_each(): return jnp.broadcast_to(array[None], (lax.axis_size(axis), *array.shape))  3.53 us
  transfers between devices with their start and end apart: 15, of which 4 were waited for; matrix products, arithmetic and copies ran while one was open for 11% of the time, Pallas kernels for 0%

profile of v2, /device:TPU:1, one launch (start us, length us, event | category | flops | bytes accessed | tf_op | source)
XLA Modules:
  0.0 148.0 jit_solution(973202572181816738)
XLA Ops:
  0.7 1.1 convert_element_type.136
  1.8 1.0 reduce-precision_convert_fusion.3
  3.4 3.9 %collective-permute-start = (bf16[128,896]{1,0:T(8,128)(2,1)S(1)}, bf16[128,896]{1,0:T(8,128)(2,1)S(1)}, u32[]{:S(2)}, u32[]{:S(2)}) collective-permute-start(bf16[128,896]{1,0:T(8,128)(2,1)S(1)} %get-tuple-element.44), channel_id=1, source_target_pairs={{0,2},{2,4},{4,6},{6,0},{1,3},{3,5},{5,7},{7,1},{8,10},{10,12},{12... | collective-permute-start | bytes 688136 | tf_op jit(solution)/shard_map/ppermute | solution.py:35
  7.3 4.4 %collective-permute-start.1 = (bf16[128,896]{1,0:T(8,128)(2,1)S(1)}, bf16[128,896]{1,0:T(8,128)(2,1)S(1)}, u32[]{:S(2)}, u32[]{:S(2)}) collective-permute-start(bf16[128,896]{1,0:T(8,128)(2,1)S(1)} %get-tuple-element.45), channel_id=1, source_target_pairs={{0,4},{2,6},{4,0},{6,2},{1,5},{3,7},{5,1},{7,3},{8,12},{10,14},{12... | collective-permute-start | bytes 688136 | tf_op jit(solution)/shard_map/ppermute | solution.py:35
  11.7 3.1 %collective-permute-start.2 = (bf16[128,896]{1,0:T(8,128)(2,1)S(1)}, bf16[128,896]{1,0:T(8,128)(2,1)S(1)}, u32[]{:S(2)}, u32[]{:S(2)}) collective-permute-start(bf16[128,896]{1,0:T(8,128)(2,1)S(1)} %get-tuple-element.46), channel_id=1, source_target_pairs={{0,6},{2,0},{4,2},{6,4},{1,7},{3,1},{5,3},{7,5},{8,14},{10,8},{12,... | collective-permute-start | bytes 688136 | tf_op jit(solution)/shard_map/ppermute | solution.py:35
  17.8 0.9 broadcast_in_dim.52
  18.7 16.4 %all-to-all-start = ((bf16[64,8,736]{2,1,0:T(8,128)(2,1)}), bf16[64,8,736]{2,1,0:T(8,128)(2,1)S(1)}, u32[]{:S(2)}, u32[]{:S(2)}) async-start(bf16[64,8,736]{2,1,0:T(8,128)(2,1)} %broadcast_in_dim.52), calls=%async_computation | async-start | bytes 1572864 | tf_op jit(solution)/shard_map/all_to_all | solution.py:22
  35.4 3.7 %collective-permute-start.3 = (bf16[512,896]{1,0:T(8,128)(2,1)S(1)}, bf16[512,896]{1,0:T(8,128)(2,1)S(1)}, u32[]{:S(2)}, u32[]{:S(2)}) collective-permute-start(bf16[512,896]{1,0:T(8,128)(2,1)S(1)} %pad_maximum_fusion), channel_id=1, source_target_pairs={{0,1},{1,0},{2,3},{3,2},{4,5},{5,4},{6,7},{7,6},{8,9},{9,8},{10,11... | collective-permute-start | bytes 2752520 | tf_op jit(solution)/shard_map/ppermute | solution.py:30
  39.9 1.3 collective-permute-done.3
  41.4 14.9 %all-to-all-done = bf16[64,8,736]{2,1,0:T(8,128)(2,1)S(1)} async-done(((bf16[64,8,736]{2,1,0:T(8,128)(2,1)}), bf16[64,8,736]{2,1,0:T(8,128)(2,1)S(1)}, u32[]{:S(2)}, u32[]{:S(2)}) %all-to-all-start) | async-done | bytes 753696 | tf_op jit(solution)/shard_map/all_to_all | solution.py:22
  57.5 3.4 %all-to-all-start.1 = ((bf16[4,64,512]{2,1,0:T(8,128)(2,1)}), bf16[4,64,512]{2,1,0:T(8,128)(2,1)S(1)}, u32[]{:S(2)}, u32[]{:S(2)}) async-start(bf16[4,64,512]{2,1,0:T(8,128)(2,1)} %broadcast_in_dim.58), calls=%async_computation.1 | async-start | bytes 524288 | tf_op jit(solution)/shard_map/all_to_all | solution.py:22
  60.9 1.7 %fusion.15 = f32[512,160]{0,1:T(8,128)} fusion(f32[512]{0:T(512)S(1)} %multiply_reduce_fusion.1, f32[512]{0:T(512)S(1)} %add.358, bf16[64,8,736]{2,1,0:T(8,128)(2,1)S(1)} %all-to-all-done, bf16[512,896]{1,0:T(8,128)(2,1)S(1)} %collective-permute-done.3), kind=kOutput, calls=%fused_computation.22 | convolution fusion | flops 354680832 | bytes 1642496 | tf_op jit(solution)/shard_map/dot_general | solution.py:65
  62.6 6.3 %collective-permute-start.5 = (f32[512,160]{0,1:T(8,128)}, f32[512,160]{0,1:T(8,128)}, u32[]{:S(2)}, u32[]{:S(2)}) collective-permute-start(f32[512,160]{0,1:T(8,128)} %fusion.15), channel_id=1, source_target_pairs={{0,1},{1,0},{2,3},{3,2},{4,5},{5,4},{6,7},{7,6},{8,9},{9,8},{10,11... | collective-permute-start | bytes 983048 | tf_op jit(solution)/shard_map/ppermute | solution.py:30
  69.2 1.4 fusion.44
  70.6 1.7 %convolution_add_fusion.2 = f32[256,384]{1,0:T(8,128)S(1)} fusion(f32[256,384]{1,0:T(8,128)} %fusion.44, bf16[256,512]{1,0:T(8,128)(2,1)S(1)} %bitcast.101, bf16[512,896]{1,0:T(8,128)(2,1)S(1)} %pad_maximum_fusion, f32[512]{0:T(512)S(1)} %multiply_reduce_fusion.2, f32[256]{0:T(256)S(1)} %add.320), kind=kOutput, calls=%fused_computation.34 | convolution fusion | flops 236158976 | bytes 1969152 | tf_op jit(solution)/shard_map/dot_general | solution.py:65
  72.3 0.9 reshape.156
  73.2 5.6 %all-to-all-start.2 = ((f32[64,4,384]{2,1,0:T(4,128)}), f32[64,4,384]{2,1,0:T(4,128)S(1)}, u32[]{:S(2)}, u32[]{:S(2)}) async-start(f32[64,4,384]{2,1,0:T(4,128)} %reshape.156), calls=%async_computation.2 | async-start | bytes 786432 | tf_op jit(solution)/shard_map/all_to_all | solution.py:22
  79.1 5.2 %collective-permute-start.9 = (bf16[256,512]{1,0:T(8,128)(2,1)S(1)}, bf16[256,512]{1,0:T(8,128)(2,1)S(1)}, u32[]{:S(2)}, u32[]{:S(2)}) collective-permute-start(bf16[256,512]{1,0:T(8,128)(2,1)S(1)} %bitcast.102), channel_id=1, source_target_pairs={{0,1},{1,0},{2,3},{3,2},{4,5},{5,4},{6,7},{7,6},{8,9},{9,8},{10,11... | collective-permute-start | bytes 786440 | tf_op jit(solution)/shard_map/ppermute | solution.py:30
  84.2 0.9 fusion.111
  85.1 2.0 %fusion.25 = f32[512,160]{0,1:T(8,128)S(1)} fusion(f32[512,160]{0,1:T(8,128)} %collective-permute-done.5, f32[512]{0:T(512)S(1)} %add.358, f32[512]{0:T(512)S(1)} %multiply_reduce_fusion.2, bf16[64,8,736]{2,1,0:T(8,128)(2,1)S(1)} %all-to-all-done, bf16[512,896]{1,0:T(8,128)(2,1)S(1)} %pad_maximum_fusion), kind=kOutput, calls=%fused_computation.35 | convolution fusion | flops 354762752 | bytes 1970176 | tf_op jit(solution)/shard_map/dot_general | solution.py:65
  87.2 2.8 %collective-permute-start.6 = (f32[128,160]{0,1:T(8,128)S(1)}, f32[128,160]{0,1:T(8,128)S(1)}, u32[]{:S(2)}, u32[]{:S(2)}) collective-permute-start(f32[128,160]{0,1:T(8,128)S(1)} %get-tuple-element.41), channel_id=1, source_target_pairs={{0,6},{2,0},{4,2},{6,4},{1,7},{3,1},{5,3},{7,5},{8,14},{10,8},{12,... | collective-permute-start | bytes 245768 | tf_op jit(solution)/shard_map/ppermute | solution.py:35
  90.0 2.5 %collective-permute-start.8 = (f32[128,160]{0,1:T(8,128)S(1)}, f32[128,160]{0,1:T(8,128)S(1)}, u32[]{:S(2)}, u32[]{:S(2)}) collective-permute-start(f32[128,160]{0,1:T(8,128)S(1)} %get-tuple-element.42), channel_id=1, source_target_pairs={{0,2},{2,4},{4,6},{6,0},{1,3},{3,5},{5,7},{7,1},{8,10},{10,12},{12... | collective-permute-start | bytes 245768 | tf_op jit(solution)/shard_map/ppermute | solution.py:35
  92.5 2.5 %collective-permute-start.7 = (f32[128,160]{0,1:T(8,128)S(1)}, f32[128,160]{0,1:T(8,128)S(1)}, u32[]{:S(2)}, u32[]{:S(2)}) collective-permute-start(f32[128,160]{0,1:T(8,128)S(1)} %get-tuple-element.43), channel_id=1, source_target_pairs={{0,4},{2,6},{4,0},{6,2},{1,5},{3,7},{5,1},{7,3},{8,12},{10,14},{12... | collective-permute-start | bytes 245768 | tf_op jit(solution)/shard_map/ppermute | solution.py:35
  95.6 0.7 broadcast_in_dim.62
  96.3 12.4 %all-to-all-start.3 = ((bf16[64,4,384]{2,1,0:T(4,128)(2,1)}), bf16[64,4,384]{2,1,0:T(4,128)(2,1)S(1)}, u32[]{:S(2)}, u32[]{:S(2)}) async-start(bf16[64,4,384]{2,1,0:T(4,128)(2,1)} %broadcast_in_dim.62), calls=%async_computation.3 | async-start | bytes 393216 | tf_op jit(solution)/shard_map/all_to_all | solution.py:22
  108.9 11.9 %all-to-all-done.3 = bf16[64,4,384]{2,1,0:T(4,128)(2,1)S(1)} async-done(((bf16[64,4,384]{2,1,0:T(4,128)(2,1)}), bf16[64,4,384]{2,1,0:T(4,128)(2,1)S(1)}, u32[]{:S(2)}, u32[]{:S(2)}) %all-to-all-start.3) | async-done | bytes 196640 | tf_op jit(solution)/shard_map/all_to_all | solution.py:22
  120.9 0.9 broadcast_in_dim.67
  121.8 3.6 %all-to-all-start.4 = ((bf16[4,256,384]{2,1,0:T(8,128)(2,1)}), bf16[4,256,384]{2,1,0:T(8,128)(2,1)S(1)}, u32[]{:S(2)}, u32[]{:S(2)}) async-start(bf16[4,256,384]{2,1,0:T(8,128)(2,1)} %broadcast_in_dim.67), calls=%async_computation.4 | async-start | bytes 1572864 | tf_op jit(solution)/shard_map/all_to_all | solution.py:22
  125.9 8.6 %all-to-all-done.4 = bf16[4,256,384]{2,1,0:T(8,128)(2,1)S(1)} async-done(((bf16[4,256,384]{2,1,0:T(8,128)(2,1)}), bf16[4,256,384]{2,1,0:T(8,128)(2,1)S(1)}, u32[]{:S(2)}, u32[]{:S(2)}) %all-to-all-start.4) | async-done | bytes 786464 | tf_op jit(solution)/shard_map/all_to_all | solution.py:22
  135.2 6.2 %collective-permute-start.4 = (bf16[4,256,384]{2,1,0:T(8,128)(2,1)S(1)}, bf16[4,256,384]{2,1,0:T(8,128)(2,1)S(1)}, u32[]{:S(2)}, u32[]{:S(2)}) collective-permute-start(bf16[4,256,384]{2,1,0:T(8,128)(2,1)S(1)} %all-to-all-done.4), channel_id=1, source_target_pairs={{0,1},{1,0},{2,3},{3,2},{4,5},{5,4},{6,7},{7,6},{8,9},{9,8},{10,11... | collective-permute-start | bytes 2359304 | tf_op jit(solution)/shard_map/ppermute | solution.py:30
  145.6 0.9 copy.52
  146.5 1.5 %add_convert_fusion = bf16[512,1000]{0,1:T(8,128)(2,1)} fusion(f32[512,1000]{0,1:T(8,128)S(1)} %fusion.49, s32[256]{0:T(256)S(1)} %broadcast_add_fusion, s32[512]{0:T(512)S(1)} %get-tuple-element.18, bf16[256,256]{1,0:T(8,128)(2,1)S(1)} %get-tuple-element.28, bf16[256,256]{1,0:T(8,128)(2,1)S(1)} %get-tuple-element.29, ...), kind=kOutput, calls=%fused_computation | convolution fusion | flops 265347072 | bytes 3599360 | tf_op jit(solution)/shard_map/dot_general | solution.py:65
  (97 shorter events, 10.3 us)
Async XLA Ops:
  0.6 2.7 %copy-start = (bf16[128,512]{1,0:T(8,128)(2,1)S(1)}, bf16[128,512]{1,0:T(8,128)(2,1)}, u32[]{:S(2)}) copy-start(bf16[128,512]{1,0:T(8,128)(2,1)} %param.7) | copy-start | bytes 393220
  2.8 12.0 %copy-start.9 = (s32[8]{0:T(128)S(1)}, s32[8]{0:T(128)}, u32[]{:S(2)}) copy-start(s32[8]{0:T(128)} %param.11) | copy-start | bytes 100
  2.8 12.2 %copy-start.7 = (s32[512]{0:T(512)S(1)}, s32[512]{0:T(512)}, u32[]{:S(2)}) copy-start(s32[512]{0:T(512)} %param.9) | copy-start | bytes 6148
  2.8 14.9 %copy-start.5 = (bf16[8,160]{1,0:T(8,128)(2,1)S(1)}, bf16[8,160]{1,0:T(8,128)(2,1)}, u32[]{:S(2)}) copy-start(bf16[8,160]{1,0:T(8,128)(2,1)} %param.12) | copy-start | bytes 7684
  3.4 31.9 %collective-permute-start = (bf16[128,896]{1,0:T(8,128)(2,1)S(1)}, bf16[128,896]{1,0:T(8,128)(2,1)S(1)}, u32[]{:S(2)}, u32[]{:S(2)}) collective-permute-start(bf16[128,896]{1,0:T(8,128)(2,1)S(1)} %get-tuple-element.44), channel_id=1, source_target_pairs={{0,2},{2,4},{4,6},{6,0},{1,3},{3,5},{5,7},{7,1},{8,10},{10,12},{12... | collective-permute-start | bytes 688136 | tf_op jit(solution)/shard_map/ppermute | solution.py:35
  7.3 28.0 %collective-permute-start.1 = (bf16[128,896]{1,0:T(8,128)(2,1)S(1)}, bf16[128,896]{1,0:T(8,128)(2,1)S(1)}, u32[]{:S(2)}, u32[]{:S(2)}) collective-permute-start(bf16[128,896]{1,0:T(8,128)(2,1)S(1)} %get-tuple-element.45), channel_id=1, source_target_pairs={{0,4},{2,6},{4,0},{6,2},{1,5},{3,7},{5,1},{7,3},{8,12},{10,14},{12... | collective-permute-start | bytes 688136 | tf_op jit(solution)/shard_map/ppermute | solution.py:35
  11.7 23.6 %collective-permute-start.2 = (bf16[128,896]{1,0:T(8,128)(2,1)S(1)}, bf16[128,896]{1,0:T(8,128)(2,1)S(1)}, u32[]{:S(2)}, u32[]{:S(2)}) collective-permute-start(bf16[128,896]{1,0:T(8,128)(2,1)S(1)} %get-tuple-element.46), channel_id=1, source_target_pairs={{0,6},{2,0},{4,2},{6,4},{1,7},{3,1},{5,3},{7,5},{8,14},{10,8},{12,... | collective-permute-start | bytes 688136 | tf_op jit(solution)/shard_map/ppermute | solution.py:35
  18.7 20.5 %copy-start.6 = (s32[512]{0:T(512)S(1)}, s32[512]{0:T(512)}, u32[]{:S(2)}) copy-start(s32[512]{0:T(512)} %param.10) | copy-start | bytes 6148
  18.7 37.6 %all-to-all-start = ((bf16[64,8,736]{2,1,0:T(8,128)(2,1)}), bf16[64,8,736]{2,1,0:T(8,128)(2,1)S(1)}, u32[]{:S(2)}, u32[]{:S(2)}) async-start(bf16[64,8,736]{2,1,0:T(8,128)(2,1)} %broadcast_in_dim.52), calls=%async_computation | async-start | bytes 1572864 | tf_op jit(solution)/shard_map/all_to_all | solution.py:22
  35.4 5.8 %collective-permute-start.3 = (bf16[512,896]{1,0:T(8,128)(2,1)S(1)}, bf16[512,896]{1,0:T(8,128)(2,1)S(1)}, u32[]{:S(2)}, u32[]{:S(2)}) collective-permute-start(bf16[512,896]{1,0:T(8,128)(2,1)S(1)} %pad_maximum_fusion), channel_id=1, source_target_pairs={{0,1},{1,0},{2,3},{3,2},{4,5},{5,4},{6,7},{7,6},{8,9},{9,8},{10,11... | collective-permute-start | bytes 2752520 | tf_op jit(solution)/shard_map/ppermute | solution.py:30
  57.5 11.5 %all-to-all-start.1 = ((bf16[4,64,512]{2,1,0:T(8,128)(2,1)}), bf16[4,64,512]{2,1,0:T(8,128)(2,1)S(1)}, u32[]{:S(2)}, u32[]{:S(2)}) async-start(bf16[4,64,512]{2,1,0:T(8,128)(2,1)} %broadcast_in_dim.58), calls=%async_computation.1 | async-start | bytes 524288 | tf_op jit(solution)/shard_map/all_to_all | solution.py:22
  62.6 22.5 %collective-permute-start.5 = (f32[512,160]{0,1:T(8,128)}, f32[512,160]{0,1:T(8,128)}, u32[]{:S(2)}, u32[]{:S(2)}) collective-permute-start(f32[512,160]{0,1:T(8,128)} %fusion.15), channel_id=1, source_target_pairs={{0,1},{1,0},{2,3},{3,2},{4,5},{5,4},{6,7},{7,6},{8,9},{9,8},{10,11... | collective-permute-start | bytes 983048 | tf_op jit(solution)/shard_map/ppermute | solution.py:30
  70.6 8.2 %copy-start.8 = (f32[160]{0:T(256)S(1)}, f32[160]{0:T(256)}, u32[]{:S(2)}) copy-start(f32[160]{0:T(256)} %param.13) | copy-start | bytes 1924
  73.2 21.8 %all-to-all-start.2 = ((f32[64,4,384]{2,1,0:T(4,128)}), f32[64,4,384]{2,1,0:T(4,128)S(1)}, u32[]{:S(2)}, u32[]{:S(2)}) async-start(f32[64,4,384]{2,1,0:T(4,128)} %reshape.156), calls=%async_computation.2 | async-start | bytes 786432 | tf_op jit(solution)/shard_map/all_to_all | solution.py:22
  79.1 46.4 %collective-permute-start.9 = (bf16[256,512]{1,0:T(8,128)(2,1)S(1)}, bf16[256,512]{1,0:T(8,128)(2,1)S(1)}, u32[]{:S(2)}, u32[]{:S(2)}) collective-permute-start(bf16[256,512]{1,0:T(8,128)(2,1)S(1)} %bitcast.102), channel_id=1, source_target_pairs={{0,1},{1,0},{2,3},{3,2},{4,5},{5,4},{6,7},{7,6},{8,9},{9,8},{10,11... | collective-permute-start | bytes 786440 | tf_op jit(solution)/shard_map/ppermute | solution.py:30
  87.2 21.6 %collective-permute-start.6 = (f32[128,160]{0,1:T(8,128)S(1)}, f32[128,160]{0,1:T(8,128)S(1)}, u32[]{:S(2)}, u32[]{:S(2)}) collective-permute-start(f32[128,160]{0,1:T(8,128)S(1)} %get-tuple-element.41), channel_id=1, source_target_pairs={{0,6},{2,0},{4,2},{6,4},{1,7},{3,1},{5,3},{7,5},{8,14},{10,8},{12,... | collective-permute-start | bytes 245768 | tf_op jit(solution)/shard_map/ppermute | solution.py:35
  90.0 18.8 %collective-permute-start.8 = (f32[128,160]{0,1:T(8,128)S(1)}, f32[128,160]{0,1:T(8,128)S(1)}, u32[]{:S(2)}, u32[]{:S(2)}) collective-permute-start(f32[128,160]{0,1:T(8,128)S(1)} %get-tuple-element.42), channel_id=1, source_target_pairs={{0,2},{2,4},{4,6},{6,0},{1,3},{3,5},{5,7},{7,1},{8,10},{10,12},{12... | collective-permute-start | bytes 245768 | tf_op jit(solution)/shard_map/ppermute | solution.py:35
  92.5 16.3 %collective-permute-start.7 = (f32[128,160]{0,1:T(8,128)S(1)}, f32[128,160]{0,1:T(8,128)S(1)}, u32[]{:S(2)}, u32[]{:S(2)}) collective-permute-start(f32[128,160]{0,1:T(8,128)S(1)} %get-tuple-element.43), channel_id=1, source_target_pairs={{0,4},{2,6},{4,0},{6,2},{1,5},{3,7},{5,1},{7,3},{8,12},{10,14},{12... | collective-permute-start | bytes 245768 | tf_op jit(solution)/shard_map/ppermute | solution.py:35
  96.3 24.5 %all-to-all-start.3 = ((bf16[64,4,384]{2,1,0:T(4,128)(2,1)}), bf16[64,4,384]{2,1,0:T(4,128)(2,1)S(1)}, u32[]{:S(2)}, u32[]{:S(2)}) async-start(bf16[64,4,384]{2,1,0:T(4,128)(2,1)} %broadcast_in_dim.62), calls=%async_computation.3 | async-start | bytes 393216 | tf_op jit(solution)/shard_map/all_to_all | solution.py:22
  121.8 12.7 %all-to-all-start.4 = ((bf16[4,256,384]{2,1,0:T(8,128)(2,1)}), bf16[4,256,384]{2,1,0:T(8,128)(2,1)S(1)}, u32[]{:S(2)}, u32[]{:S(2)}) async-start(bf16[4,256,384]{2,1,0:T(8,128)(2,1)} %broadcast_in_dim.67), calls=%async_computation.4 | async-start | bytes 1572864 | tf_op jit(solution)/shard_map/all_to_all | solution.py:22
  125.4 9.4 %copy-start.10 = (bf16[128,256]{1,0:T(8,128)(2,1)S(1)}, bf16[128,256]{1,0:T(8,128)(2,1)}, u32[]{:S(2)}) copy-start(bf16[128,256]{1,0:T(8,128)(2,1)} %fusion.111) | copy-start | bytes 196612
  125.5 9.6 %copy-start.1 = (bf16[136,512]{0,1:T(8,128)(2,1)}, bf16[136,512]{0,1:T(8,128)(2,1)S(1)}, u32[]{:S(2)}) copy-start(bf16[136,512]{0,1:T(8,128)(2,1)S(1)} %get-tuple-element.36) | copy-start | bytes 417796
  125.5 9.6 %copy-start.3 = (bf16[136,512]{0,1:T(8,128)(2,1)}, bf16[136,512]{0,1:T(8,128)(2,1)S(1)}, u32[]{:S(2)}) copy-start(bf16[136,512]{0,1:T(8,128)(2,1)S(1)} %get-tuple-element.35) | copy-start | bytes 417796
  135.2 7.9 %collective-permute-start.4 = (bf16[4,256,384]{2,1,0:T(8,128)(2,1)S(1)}, bf16[4,256,384]{2,1,0:T(8,128)(2,1)S(1)}, u32[]{:S(2)}, u32[]{:S(2)}) collective-permute-start(bf16[4,256,384]{2,1,0:T(8,128)(2,1)S(1)} %all-to-all-done.4), channel_id=1, source_target_pairs={{0,1},{1,0},{2,3},{3,2},{4,5},{5,4},{6,7},{7,6},{8,9},{9,8},{10,11... | collective-permute-start | bytes 2359304 | tf_op jit(solution)/shard_map/ppermute | solution.py:30
  142.4 1.0 copy-start.4
  142.4 1.2 copy-start.2

commit v3 on v2

--- a/solution.py
+++ b/solution.py
@@ -84,12 +84,13 @@
     label_at = 2 * ranks
 
     owner = batch_index // held
-    within = batch_index % held
-    row = jnp.sum(jnp.where(owner == me, within, 0))
-    mine = lax.dynamic_slice(centers, (row, 0), (1, depth))
-    picks = sub_index[:, None] == jnp.arange(held, dtype=jnp.int32)[None, :]
+    places = jnp.arange(held, dtype=jnp.int32)
+    taken = jnp.any(batch_index[None, :] == (me * held + places)[:, None], axis=1)
+    picks = sub_index[:, None] == places[None, :]
+    chosen = jnp.concatenate([picks, taken[None, :]], axis=0).astype(jnp.bfloat16)
     picks = picks.astype(jnp.bfloat16)
-    subset = dot(picks, centers).astype(jnp.bfloat16)
+    rows = dot(chosen, centers).astype(jnp.bfloat16)
+    subset, mine = rows[:points], rows[points:]
     packed = jnp.concatenate([subset, eigvecs, mine.reshape(points, -1)], axis=1)
     in_plane = exchange(to_each(packed, PLANE), PLANE)
     sub_rows = in_plane[:, :, :depth].reshape(nplane * points, depth)
@@ -160,9 +161,11 @@
         proj = jnp.concatenate([half_rows[i, :, block:] for i in range(nx)], axis=1)
         back = sum(dot(piece, proj, ((1,), (1,))) for piece in left)
         near = jnp.pad(near.astype(jnp.float32), ((0, points), (0, 0)))
-        gradient = gradient + sum(dot(piece, resid) for piece in parts_of(near - back, 2))
-    center_grad = gradient[:held].astype(jnp.bfloat16)
-    return (predictions.astype(jnp.bfloat16), center_grad, gradient[held:])
+        gradient = gradient + sum(
+            dot(resid, piece, ((0,), (1,))) for piece in parts_of(near - back, 2)
+        )
+    center_grad = gradient[:, :held].astype(jnp.bfloat16).T
+    return (predictions.astype(jnp.bfloat16), center_grad, gradient[:, held:].T)
 
 
 def solution(mesh):

time: 149 us -> 146 us (0.980)
  between operations: 3.26 us -> 1.32 us
  transfers between devices with their start and end apart: 15 -> 15, of which waited for: 4 -> 5; matrix products, arithmetic and copies ran while one was open for 11% -> 11% of each run, Pallas kernels for 0% -> 0%
where the time goes in v3:
time: 146 us
  starting transfers between devices  82.1 us (56%)
  waiting for transfers between devices  36.8 us (25%)
  matrix products  13.7 us (9%)
  local copies, waits for them, and re-layouts  7.57 us (5%)
  other arithmetic  4.03 us (3%)
    all_to_all x5, starting transfers between devices, exchange(): return lax.all_to_all(pieces, axis, 0, 0, tiled=True)  41.5 us
    all_to_all x5, waiting for transfers between devices, exchange(): return lax.all_to_all(pieces, axis, 0, 0, tiled=True)  35.4 us
    ppermute x4, starting transfers between devices, from_other_core(): return lax.ppermute(array, CORE, [(0, 1), (1, 0)])  21.4 us
    ppermute x6, starting transfers between devices, to_next(): lax.ppermute(array, axis, [(i, (i + step) % count) for i in range(count)])  19.2 us
    dot_general x16, matrix products, dot(): lax.dot_general(left, right, (contract, ((), ())), preferred_element_type...  12.5 us
    broadcast_in_dim x6, local copies, waits for them, and re-layouts, to_each(): return jnp.broadcast_to(array[None], (lax.axis_size(axis), *array.shape))  3.54 us
  transfers between devices with their start and end apart: 15, of which 5 were waited for; matrix products, arithmetic and copies ran while one was open for 11% of the time, Pallas kernels for 0%

profile of v3, /device:TPU:1, one launch (start us, length us, event | category | flops | bytes accessed | tf_op | source)
XLA Modules:
  0.0 145.5 jit_solution(9313419237565844106)
XLA Ops:
  0.7 1.1 convert_element_type.137
  1.8 1.0 reduce-precision_convert_fusion.3
  3.4 3.9 %collective-permute-start = (bf16[128,896]{1,0:T(8,128)(2,1)S(1)}, bf16[128,896]{1,0:T(8,128)(2,1)S(1)}, u32[]{:S(2)}, u32[]{:S(2)}) collective-permute-start(bf16[128,896]{1,0:T(8,128)(2,1)S(1)} %get-tuple-element.42), channel_id=1, source_target_pairs={{0,2},{2,4},{4,6},{6,0},{1,3},{3,5},{5,7},{7,1},{8,10},{10,12},{12... | collective-permute-start | bytes 688136 | tf_op jit(solution)/shard_map/ppermute | solution.py:35
  7.3 4.4 %collective-permute-start.1 = (bf16[128,896]{1,0:T(8,128)(2,1)S(1)}, bf16[128,896]{1,0:T(8,128)(2,1)S(1)}, u32[]{:S(2)}, u32[]{:S(2)}) collective-permute-start(bf16[128,896]{1,0:T(8,128)(2,1)S(1)} %get-tuple-element.43), channel_id=1, source_target_pairs={{0,4},{2,6},{4,0},{6,2},{1,5},{3,7},{5,1},{7,3},{8,12},{10,14},{12... | collective-permute-start | bytes 688136 | tf_op jit(solution)/shard_map/ppermute | solution.py:35
  11.7 3.1 %collective-permute-start.2 = (bf16[128,896]{1,0:T(8,128)(2,1)S(1)}, bf16[128,896]{1,0:T(8,128)(2,1)S(1)}, u32[]{:S(2)}, u32[]{:S(2)}) collective-permute-start(bf16[128,896]{1,0:T(8,128)(2,1)S(1)} %get-tuple-element.44), channel_id=1, source_target_pairs={{0,6},{2,0},{4,2},{6,4},{1,7},{3,1},{5,3},{7,5},{8,14},{10,8},{12,... | collective-permute-start | bytes 688136 | tf_op jit(solution)/shard_map/ppermute | solution.py:35
  15.4 0.9 broadcast_in_dim.53
  16.3 16.4 %all-to-all-start = ((bf16[64,8,736]{2,1,0:T(8,128)(2,1)}), bf16[64,8,736]{2,1,0:T(8,128)(2,1)S(1)}, u32[]{:S(2)}, u32[]{:S(2)}) async-start(bf16[64,8,736]{2,1,0:T(8,128)(2,1)} %broadcast_in_dim.53), calls=%async_computation | async-start | bytes 1572864 | tf_op jit(solution)/shard_map/all_to_all | solution.py:22
  33.1 3.7 %collective-permute-start.3 = (bf16[512,896]{1,0:T(8,128)(2,1)S(1)}, bf16[512,896]{1,0:T(8,128)(2,1)S(1)}, u32[]{:S(2)}, u32[]{:S(2)}) collective-permute-start(bf16[512,896]{1,0:T(8,128)(2,1)S(1)} %pad_maximum_fusion), channel_id=1, source_target_pairs={{0,1},{1,0},{2,3},{3,2},{4,5},{5,4},{6,7},{7,6},{8,9},{9,8},{10,11... | collective-permute-start | bytes 2752520 | tf_op jit(solution)/shard_map/ppermute | solution.py:30
  37.5 1.3 collective-permute-done.3
  39.0 14.8 %all-to-all-done = bf16[64,8,736]{2,1,0:T(8,128)(2,1)S(1)} async-done(((bf16[64,8,736]{2,1,0:T(8,128)(2,1)}), bf16[64,8,736]{2,1,0:T(8,128)(2,1)S(1)}, u32[]{:S(2)}, u32[]{:S(2)}) %all-to-all-start) | async-done | bytes 753696 | tf_op jit(solution)/shard_map/all_to_all | solution.py:22
  55.1 3.4 %all-to-all-start.1 = ((bf16[4,64,512]{2,1,0:T(8,128)(2,1)}), bf16[4,64,512]{2,1,0:T(8,128)(2,1)S(1)}, u32[]{:S(2)}, u32[]{:S(2)}) async-start(bf16[4,64,512]{2,1,0:T(8,128)(2,1)} %broadcast_in_dim.59), calls=%async_computation.1 | async-start | bytes 524288 | tf_op jit(solution)/shard_map/all_to_all | solution.py:22
  58.5 1.7 %fusion.15 = f32[512,160]{0,1:T(8,128)} fusion(f32[512]{0:T(512)S(1)} %multiply_reduce_fusion.1, f32[512]{0:T(512)S(1)} %add.359, bf16[64,8,736]{2,1,0:T(8,128)(2,1)S(1)} %all-to-all-done, bf16[512,896]{1,0:T(8,128)(2,1)S(1)} %collective-permute-done.3), kind=kOutput, calls=%fused_computation.22 | convolution fusion | flops 354680832 | bytes 1642496 | tf_op jit(solution)/shard_map/dot_general | solution.py:65
  60.3 6.3 %collective-permute-start.5 = (f32[512,160]{0,1:T(8,128)}, f32[512,160]{0,1:T(8,128)}, u32[]{:S(2)}, u32[]{:S(2)}) collective-permute-start(f32[512,160]{0,1:T(8,128)} %fusion.15), channel_id=1, source_target_pairs={{0,1},{1,0},{2,3},{3,2},{4,5},{5,4},{6,7},{7,6},{8,9},{9,8},{10,11... | collective-permute-start | bytes 983048 | tf_op jit(solution)/shard_map/ppermute | solution.py:30
  66.8 1.4 fusion.44
  68.2 1.7 %convolution_add_fusion.2 = f32[256,384]{1,0:T(8,128)S(1)} fusion(f32[256,384]{1,0:T(8,128)} %fusion.44, bf16[256,512]{1,0:T(8,128)(2,1)S(1)} %bitcast.106, bf16[512,896]{1,0:T(8,128)(2,1)S(1)} %pad_maximum_fusion, f32[512]{0:T(512)S(1)} %multiply_reduce_fusion.2, f32[256]{0:T(256)S(1)} %add.321), kind=kOutput, calls=%fused_computation.34 | convolution fusion | flops 236158976 | bytes 1969152 | tf_op jit(solution)/shard_map/dot_general | solution.py:65
  69.9 0.9 reshape.161
  70.8 5.6 %all-to-all-start.2 = ((f32[64,4,384]{2,1,0:T(4,128)}), f32[64,4,384]{2,1,0:T(4,128)S(1)}, u32[]{:S(2)}, u32[]{:S(2)}) async-start(f32[64,4,384]{2,1,0:T(4,128)} %reshape.161), calls=%async_computation.2 | async-start | bytes 786432 | tf_op jit(solution)/shard_map/all_to_all | solution.py:22
  76.7 5.2 %collective-permute-start.9 = (bf16[256,512]{1,0:T(8,128)(2,1)S(1)}, bf16[256,512]{1,0:T(8,128)(2,1)S(1)}, u32[]{:S(2)}, u32[]{:S(2)}) collective-permute-start(bf16[256,512]{1,0:T(8,128)(2,1)S(1)} %bitcast.107), channel_id=1, source_target_pairs={{0,1},{1,0},{2,3},{3,2},{4,5},{5,4},{6,7},{7,6},{8,9},{9,8},{10,11... | collective-permute-start | bytes 786440 | tf_op jit(solution)/shard_map/ppermute | solution.py:30
  81.9 0.9 fusion.112
  82.7 2.0 %fusion.25 = f32[512,160]{0,1:T(8,128)S(1)} fusion(f32[512,160]{0,1:T(8,128)} %collective-permute-done.5, f32[512]{0:T(512)S(1)} %add.359, f32[512]{0:T(512)S(1)} %multiply_reduce_fusion.2, bf16[64,8,736]{2,1,0:T(8,128)(2,1)S(1)} %all-to-all-done, bf16[512,896]{1,0:T(8,128)(2,1)S(1)} %pad_maximum_fusion), kind=kOutput, calls=%fused_computation.35 | convolution fusion | flops 354762752 | bytes 1970176 | tf_op jit(solution)/shard_map/dot_general | solution.py:65
  84.8 2.8 %collective-permute-start.6 = (f32[128,160]{0,1:T(8,128)S(1)}, f32[128,160]{0,1:T(8,128)S(1)}, u32[]{:S(2)}, u32[]{:S(2)}) collective-permute-start(f32[128,160]{0,1:T(8,128)S(1)} %get-tuple-element.39), channel_id=1, source_target_pairs={{0,6},{2,0},{4,2},{6,4},{1,7},{3,1},{5,3},{7,5},{8,14},{10,8},{12,... | collective-permute-start | bytes 245768 | tf_op jit(solution)/shard_map/ppermute | solution.py:35
  87.6 2.5 %collective-permute-start.8 = (f32[128,160]{0,1:T(8,128)S(1)}, f32[128,160]{0,1:T(8,128)S(1)}, u32[]{:S(2)}, u32[]{:S(2)}) collective-permute-start(f32[128,160]{0,1:T(8,128)S(1)} %get-tuple-element.40), channel_id=1, source_target_pairs={{0,2},{2,4},{4,6},{6,0},{1,3},{3,5},{5,7},{7,1},{8,10},{10,12},{12... | collective-permute-start | bytes 245768 | tf_op jit(solution)/shard_map/ppermute | solution.py:35
  90.1 2.5 %collective-permute-start.7 = (f32[128,160]{0,1:T(8,128)S(1)}, f32[128,160]{0,1:T(8,128)S(1)}, u32[]{:S(2)}, u32[]{:S(2)}) collective-permute-start(f32[128,160]{0,1:T(8,128)S(1)} %get-tuple-element.41), channel_id=1, source_target_pairs={{0,4},{2,6},{4,0},{6,2},{1,5},{3,7},{5,1},{7,3},{8,12},{10,14},{12... | collective-permute-start | bytes 245768 | tf_op jit(solution)/shard_map/ppermute | solution.py:35
  93.2 0.7 broadcast_in_dim.63
  93.9 12.4 %all-to-all-start.3 = ((bf16[64,4,384]{2,1,0:T(4,128)(2,1)}), bf16[64,4,384]{2,1,0:T(4,128)(2,1)S(1)}, u32[]{:S(2)}, u32[]{:S(2)}) async-start(bf16[64,4,384]{2,1,0:T(4,128)(2,1)} %broadcast_in_dim.63), calls=%async_computation.3 | async-start | bytes 393216 | tf_op jit(solution)/shard_map/all_to_all | solution.py:22
  106.5 11.9 %all-to-all-done.3 = bf16[64,4,384]{2,1,0:T(4,128)(2,1)S(1)} async-done(((bf16[64,4,384]{2,1,0:T(4,128)(2,1)}), bf16[64,4,384]{2,1,0:T(4,128)(2,1)S(1)}, u32[]{:S(2)}, u32[]{:S(2)}) %all-to-all-start.3) | async-done | bytes 196640 | tf_op jit(solution)/shard_map/all_to_all | solution.py:22
  118.5 0.9 broadcast_in_dim.68
  119.4 3.6 %all-to-all-start.4 = ((bf16[4,256,384]{2,1,0:T(8,128)(2,1)}), bf16[4,256,384]{2,1,0:T(8,128)(2,1)S(1)}, u32[]{:S(2)}, u32[]{:S(2)}) async-start(bf16[4,256,384]{2,1,0:T(8,128)(2,1)} %broadcast_in_dim.68), calls=%async_computation.4 | async-start | bytes 1572864 | tf_op jit(solution)/shard_map/all_to_all | solution.py:22
  123.5 8.6 %all-to-all-done.4 = bf16[4,256,384]{2,1,0:T(8,128)(2,1)S(1)} async-done(((bf16[4,256,384]{2,1,0:T(8,128)(2,1)}), bf16[4,256,384]{2,1,0:T(8,128)(2,1)S(1)}, u32[]{:S(2)}, u32[]{:S(2)}) %all-to-all-start.4) | async-done | bytes 786464 | tf_op jit(solution)/shard_map/all_to_all | solution.py:22
  132.7 6.2 %collective-permute-start.4 = (bf16[4,256,384]{2,1,0:T(8,128)(2,1)S(1)}, bf16[4,256,384]{2,1,0:T(8,128)(2,1)S(1)}, u32[]{:S(2)}, u32[]{:S(2)}) collective-permute-start(bf16[4,256,384]{2,1,0:T(8,128)(2,1)S(1)} %all-to-all-done.4), channel_id=1, source_target_pairs={{0,1},{1,0},{2,3},{3,2},{4,5},{5,4},{6,7},{7,6},{8,9},{9,8},{10,11... | collective-permute-start | bytes 2359304 | tf_op jit(solution)/shard_map/ppermute | solution.py:30
  143.1 0.9 copy.52
  144.0 1.5 %add_convert_fusion = bf16[512,1000]{0,1:T(8,128)(2,1)} fusion(f32[512,1000]{0,1:T(8,128)S(1)} %fusion.49, s32[256]{0:T(256)S(1)} %broadcast_add_fusion, s32[512]{0:T(512)S(1)} %add_select_fusion, bf16[256,256]{1,0:T(8,128)(2,1)S(1)} %get-tuple-element.26, bf16[256,256]{1,0:T(8,128)(2,1)S(1)} %get-tuple-element.27, ...), kind=kOutput, calls=%fused_computation | convolution fusion | flops 265347072 | bytes 3599360 | tf_op jit(solution)/shard_map/dot_general | solution.py:65
  (97 shorter events, 9.7 us)
Async XLA Ops:
  0.6 2.7 %copy-start = (bf16[128,512]{1,0:T(8,128)(2,1)S(1)}, bf16[128,512]{1,0:T(8,128)(2,1)}, u32[]{:S(2)}) copy-start(bf16[128,512]{1,0:T(8,128)(2,1)} %param.7) | copy-start | bytes 393220
  2.8 12.0 %copy-start.7 = (s32[8]{0:T(128)S(1)}, s32[8]{0:T(128)}, u32[]{:S(2)}) copy-start(s32[8]{0:T(128)} %param.11) | copy-start | bytes 100
  2.8 12.1 %copy-start.4 = (s32[512]{0:T(512)S(1)}, s32[512]{0:T(512)}, u32[]{:S(2)}) copy-start(s32[512]{0:T(512)} %param.9) | copy-start | bytes 6148
  2.8 12.5 %copy-start.3 = (bf16[8,160]{1,0:T(8,128)(2,1)S(1)}, bf16[8,160]{1,0:T(8,128)(2,1)}, u32[]{:S(2)}) copy-start(bf16[8,160]{1,0:T(8,128)(2,1)} %param.12) | copy-start | bytes 7684
  3.4 29.6 %collective-permute-start = (bf16[128,896]{1,0:T(8,128)(2,1)S(1)}, bf16[128,896]{1,0:T(8,128)(2,1)S(1)}, u32[]{:S(2)}, u32[]{:S(2)}) collective-permute-start(bf16[128,896]{1,0:T(8,128)(2,1)S(1)} %get-tuple-element.42), channel_id=1, source_target_pairs={{0,2},{2,4},{4,6},{6,0},{1,3},{3,5},{5,7},{7,1},{8,10},{10,12},{12... | collective-permute-start | bytes 688136 | tf_op jit(solution)/shard_map/ppermute | solution.py:35
  7.3 25.6 %collective-permute-start.1 = (bf16[128,896]{1,0:T(8,128)(2,1)S(1)}, bf16[128,896]{1,0:T(8,128)(2,1)S(1)}, u32[]{:S(2)}, u32[]{:S(2)}) collective-permute-start(bf16[128,896]{1,0:T(8,128)(2,1)S(1)} %get-tuple-element.43), channel_id=1, source_target_pairs={{0,4},{2,6},{4,0},{6,2},{1,5},{3,7},{5,1},{7,3},{8,12},{10,14},{12... | collective-permute-start | bytes 688136 | tf_op jit(solution)/shard_map/ppermute | solution.py:35
  11.7 21.3 %collective-permute-start.2 = (bf16[128,896]{1,0:T(8,128)(2,1)S(1)}, bf16[128,896]{1,0:T(8,128)(2,1)S(1)}, u32[]{:S(2)}, u32[]{:S(2)}) collective-permute-start(bf16[128,896]{1,0:T(8,128)(2,1)S(1)} %get-tuple-element.44), channel_id=1, source_target_pairs={{0,6},{2,0},{4,2},{6,4},{1,7},{3,1},{5,3},{7,5},{8,14},{10,8},{12,... | collective-permute-start | bytes 688136 | tf_op jit(solution)/shard_map/ppermute | solution.py:35
  16.3 20.5 %copy-start.5 = (s32[512]{0:T(512)S(1)}, s32[512]{0:T(512)}, u32[]{:S(2)}) copy-start(s32[512]{0:T(512)} %param.10) | copy-start | bytes 6148
  16.3 37.6 %all-to-all-start = ((bf16[64,8,736]{2,1,0:T(8,128)(2,1)}), bf16[64,8,736]{2,1,0:T(8,128)(2,1)S(1)}, u32[]{:S(2)}, u32[]{:S(2)}) async-start(bf16[64,8,736]{2,1,0:T(8,128)(2,1)} %broadcast_in_dim.53), calls=%async_computation | async-start | bytes 1572864 | tf_op jit(solution)/shard_map/all_to_all | solution.py:22
  33.1 5.8 %collective-permute-start.3 = (bf16[512,896]{1,0:T(8,128)(2,1)S(1)}, bf16[512,896]{1,0:T(8,128)(2,1)S(1)}, u32[]{:S(2)}, u32[]{:S(2)}) collective-permute-start(bf16[512,896]{1,0:T(8,128)(2,1)S(1)} %pad_maximum_fusion), channel_id=1, source_target_pairs={{0,1},{1,0},{2,3},{3,2},{4,5},{5,4},{6,7},{7,6},{8,9},{9,8},{10,11... | collective-permute-start | bytes 2752520 | tf_op jit(solution)/shard_map/ppermute | solution.py:30
  55.1 11.5 %all-to-all-start.1 = ((bf16[4,64,512]{2,1,0:T(8,128)(2,1)}), bf16[4,64,512]{2,1,0:T(8,128)(2,1)S(1)}, u32[]{:S(2)}, u32[]{:S(2)}) async-start(bf16[4,64,512]{2,1,0:T(8,128)(2,1)} %broadcast_in_dim.59), calls=%async_computation.1 | async-start | bytes 524288 | tf_op jit(solution)/shard_map/all_to_all | solution.py:22
  60.3 22.5 %collective-permute-start.5 = (f32[512,160]{0,1:T(8,128)}, f32[512,160]{0,1:T(8,128)}, u32[]{:S(2)}, u32[]{:S(2)}) collective-permute-start(f32[512,160]{0,1:T(8,128)} %fusion.15), channel_id=1, source_target_pairs={{0,1},{1,0},{2,3},{3,2},{4,5},{5,4},{6,7},{7,6},{8,9},{9,8},{10,11... | collective-permute-start | bytes 983048 | tf_op jit(solution)/shard_map/ppermute | solution.py:30
  68.2 8.2 %copy-start.6 = (f32[160]{0:T(256)S(1)}, f32[160]{0:T(256)}, u32[]{:S(2)}) copy-start(f32[160]{0:T(256)} %param.13) | copy-start | bytes 1924
  70.8 21.8 %all-to-all-start.2 = ((f32[64,4,384]{2,1,0:T(4,128)}), f32[64,4,384]{2,1,0:T(4,128)S(1)}, u32[]{:S(2)}, u32[]{:S(2)}) async-start(f32[64,4,384]{2,1,0:T(4,128)} %reshape.161), calls=%async_computation.2 | async-start | bytes 786432 | tf_op jit(solution)/shard_map/all_to_all | solution.py:22
  76.7 46.4 %collective-permute-start.9 = (bf16[256,512]{1,0:T(8,128)(2,1)S(1)}, bf16[256,512]{1,0:T(8,128)(2,1)S(1)}, u32[]{:S(2)}, u32[]{:S(2)}) collective-permute-start(bf16[256,512]{1,0:T(8,128)(2,1)S(1)} %bitcast.107), channel_id=1, source_target_pairs={{0,1},{1,0},{2,3},{3,2},{4,5},{5,4},{6,7},{7,6},{8,9},{9,8},{10,11... | collective-permute-start | bytes 786440 | tf_op jit(solution)/shard_map/ppermute | solution.py:30
  84.8 21.6 %collective-permute-start.6 = (f32[128,160]{0,1:T(8,128)S(1)}, f32[128,160]{0,1:T(8,128)S(1)}, u32[]{:S(2)}, u32[]{:S(2)}) collective-permute-start(f32[128,160]{0,1:T(8,128)S(1)} %get-tuple-element.39), channel_id=1, source_target_pairs={{0,6},{2,0},{4,2},{6,4},{1,7},{3,1},{5,3},{7,5},{8,14},{10,8},{12,... | collective-permute-start | bytes 245768 | tf_op jit(solution)/shard_map/ppermute | solution.py:35
  87.6 18.8 %collective-permute-start.8 = (f32[128,160]{0,1:T(8,128)S(1)}, f32[128,160]{0,1:T(8,128)S(1)}, u32[]{:S(2)}, u32[]{:S(2)}) collective-permute-start(f32[128,160]{0,1:T(8,128)S(1)} %get-tuple-element.40), channel_id=1, source_target_pairs={{0,2},{2,4},{4,6},{6,0},{1,3},{3,5},{5,7},{7,1},{8,10},{10,12},{12... | collective-permute-start | bytes 245768 | tf_op jit(solution)/shard_map/ppermute | solution.py:35
  90.1 16.3 %collective-permute-start.7 = (f32[128,160]{0,1:T(8,128)S(1)}, f32[128,160]{0,1:T(8,128)S(1)}, u32[]{:S(2)}, u32[]{:S(2)}) collective-permute-start(f32[128,160]{0,1:T(8,128)S(1)} %get-tuple-element.41), channel_id=1, source_target_pairs={{0,4},{2,6},{4,0},{6,2},{1,5},{3,7},{5,1},{7,3},{8,12},{10,14},{12... | collective-permute-start | bytes 245768 | tf_op jit(solution)/shard_map/ppermute | solution.py:35
  93.9 24.5 %all-to-all-start.3 = ((bf16[64,4,384]{2,1,0:T(4,128)(2,1)}), bf16[64,4,384]{2,1,0:T(4,128)(2,1)S(1)}, u32[]{:S(2)}, u32[]{:S(2)}) async-start(bf16[64,4,384]{2,1,0:T(4,128)(2,1)} %broadcast_in_dim.63), calls=%async_computation.3 | async-start | bytes 393216 | tf_op jit(solution)/shard_map/all_to_all | solution.py:22
  119.4 12.7 %all-to-all-start.4 = ((bf16[4,256,384]{2,1,0:T(8,128)(2,1)}), bf16[4,256,384]{2,1,0:T(8,128)(2,1)S(1)}, u32[]{:S(2)}, u32[]{:S(2)}) async-start(bf16[4,256,384]{2,1,0:T(8,128)(2,1)} %broadcast_in_dim.68), calls=%async_computation.4 | async-start | bytes 1572864 | tf_op jit(solution)/shard_map/all_to_all | solution.py:22
  123.0 9.4 %copy-start.8 = (bf16[128,256]{1,0:T(8,128)(2,1)S(1)}, bf16[128,256]{1,0:T(8,128)(2,1)}, u32[]{:S(2)}) copy-start(bf16[128,256]{1,0:T(8,128)(2,1)} %fusion.112) | copy-start | bytes 196612
  123.1 9.6 %copy-start.1 = (bf16[136,512]{0,1:T(8,128)(2,1)}, bf16[136,512]{0,1:T(8,128)(2,1)S(1)}, u32[]{:S(2)}) copy-start(bf16[136,512]{0,1:T(8,128)(2,1)S(1)} %get-tuple-element.33) | copy-start | bytes 417796
  132.7 7.9 %collective-permute-start.4 = (bf16[4,256,384]{2,1,0:T(8,128)(2,1)S(1)}, bf16[4,256,384]{2,1,0:T(8,128)(2,1)S(1)}, u32[]{:S(2)}, u32[]{:S(2)}) collective-permute-start(bf16[4,256,384]{2,1,0:T(8,128)(2,1)S(1)} %all-to-all-done.4), channel_id=1, source_target_pairs={{0,1},{1,0},{2,3},{3,2},{4,5},{5,4},{6,7},{7,6},{8,9},{9,8},{10,11... | collective-permute-start | bytes 2359304 | tf_op jit(solution)/shard_map/ppermute | solution.py:30
  140.0 1.0 copy-start.2

commit v4 on v3

--- a/solution.py
+++ b/solution.py
@@ -1,6 +1,7 @@
 import jax
 import jax.numpy as jnp
 from jax import lax
+from jax.experimental.layout import Layout, with_layout_constraint
 from jax.sharding import Mesh
 from jax.sharding import PartitionSpec as P
 
@@ -91,12 +92,19 @@
     picks = picks.astype(jnp.bfloat16)
     rows = dot(chosen, centers).astype(jnp.bfloat16)
     subset, mine = rows[:points], rows[points:]
-    packed = jnp.concatenate([subset, eigvecs, mine.reshape(points, -1)], axis=1)
+    near_rows = exchange(to_each(mine.reshape(nx, -1), X), X).reshape(nx, depth)
+
+    def side_by_side(array):
+        return jnp.concatenate(jnp.split(array, points // nx, axis=0), axis=1)
+
+    def stacked(array):
+        pieces = jnp.split(array, points // nx, axis=2)
+        return jnp.concatenate([piece.reshape(half, -1) for piece in pieces], axis=0)
+
+    deep = depth * points // nx
+    packed = jnp.concatenate([side_by_side(subset), near_rows, side_by_side(eigvecs)], axis=1)
     in_plane = exchange(to_each(packed, PLANE), PLANE)
-    sub_rows = in_plane[:, :, :depth].reshape(nplane * points, depth)
-    vec_rows = in_plane[:, :, depth : depth + rank].reshape(nplane * points, rank)
-    column = in_plane[:, :, depth + rank :].reshape(nplane, depth)
-    batch = exchange(to_each(column, X), X).reshape(half, depth)
+    batch = in_plane[:, :, deep : deep + depth].reshape(half, depth)
 
     def by_x(array):
         return jnp.moveaxis(array.reshape(array.shape[0], nx, -1), 1, 0)
@@ -116,6 +124,9 @@
 
     sums = dot(kernel(batch, here), around[:, depth:])
     sums = sums + dot(kernel(batch, there), opposite[:, depth:])
+    later, sums = lax.optimization_barrier((in_plane, sums))
+    sub_rows = stacked(later[:, :, :deep])
+    vec_rows = stacked(later[:, :, deep + depth :])
     arrived = exchange(sums.reshape(nplane, nx, wide), PLANE)
 
     other_batch = from_other_core(batch)
@@ -128,7 +139,7 @@
     other_kbz = kernel(centers, other_batch)
 
     def device_of(number, core):
-        return (number % nplane * nx + number // nplane) * 2 + core
+        return number * 2 + core
 
     total = jnp.sum(arrived, axis=0)
     numbers = lax.axis_index(PLANE) * nx + jnp.arange(nx, dtype=jnp.int32)
@@ -164,6 +175,7 @@
         gradient = gradient + sum(
             dot(resid, piece, ((0,), (1,))) for piece in parts_of(near - back, 2)
         )
+    gradient = with_layout_constraint(gradient, Layout((0, 1)))
     center_grad = gradient[:, :held].astype(jnp.bfloat16).T
     return (predictions.astype(jnp.bfloat16), center_grad, gradient[:, held:].T)
 

time: 146 us -> 148 us (1.014)
  waiting for transfers between devices: 36.8 us -> 26.7 us
  other arithmetic: 4.03 us -> 8.56 us
  local copies, waits for them, and re-layouts: 7.57 us -> 10.3 us
  matrix products: 13.7 us -> 15.6 us
  starting transfers between devices: 82.1 us -> 83.8 us
    all_to_all x5, waiting for transfers between devices: 35.4 us -> 21.3 us  [exchange(): return lax.all_to_all(pieces, axis, 0, 0, tiled=True)]
    ppermute x6, waiting for transfers between devices: 0.02 us -> 5.28 us  [to_next(): lax.ppermute(array, axis, [(i, (i + step) % count) for i in range(count)])]
    all_to_all x5, starting transfers between devices: 41.5 us -> 45.5 us  [exchange(): return lax.all_to_all(pieces, axis, 0, 0, tiled=True)]
    ppermute x4, starting transfers between devices: 21.4 us -> 19.5 us  [from_other_core(): return lax.ppermute(array, CORE, [(0, 1), (1, 0)])]
    reduce_sum x6, other arithmetic: 0.9 us -> 2.57 us  [squares(): return jnp.sum(jnp.square(rows.astype(jnp.float32)), axis=1)]
    broadcast_in_dim x6 -> x5, local copies, waits for them, and re-layouts: 3.54 us -> 3.54 us  [to_each(): return jnp.broadcast_to(array[None], (lax.axis_size(axis), *array.shape))]
  transfers between devices with their start and end apart: 15 -> 15, of which waited for: 5 -> 6; matrix products, arithmetic and copies ran while one was open for 11% -> 15% of each run, Pallas kernels for 0% -> 0%
where the time goes in v4:
time: 148 us; the launch traced here: 147 us
  starting transfers between devices  83.8 us (57%)
  waiting for transfers between devices  26.7 us (18%)
  matrix products  15.6 us (11%)
  local copies, waits for them, and re-layouts  10.3 us (7%)
  other arithmetic  8.56 us (6%)
  between operations  1.54 us (1%)
    all_to_all x5, starting transfers between devices, exchange(): return lax.all_to_all(pieces, axis, 0, 0, tiled=True)  45.5 us
    all_to_all x5, waiting for transfers between devices, exchange(): return lax.all_to_all(pieces, axis, 0, 0, tiled=True)  21.3 us
    ppermute x4, starting transfers between devices, from_other_core(): return lax.ppermute(array, CORE, [(0, 1), (1, 0)])  19.5 us
    ppermute x6, starting transfers between devices, to_next(): lax.ppermute(array, axis, [(i, (i + step) % count) for i in range(count)])  18.9 us
    dot_general x16, matrix products, dot(): lax.dot_general(left, right, (contract, ((), ())), preferred_element_type...  13.6 us
    ppermute x6, waiting for transfers between devices, to_next(): lax.ppermute(array, axis, [(i, (i + step) % count) for i in range(count)])  5.28 us
    broadcast_in_dim x5, local copies, waits for them, and re-layouts, to_each(): return jnp.broadcast_to(array[None], (lax.axis_size(axis), *array.shape))  3.54 us
  transfers between devices with their start and end apart: 15, of which 6 were waited for; matrix products, arithmetic and copies ran while one was open for 15% of the time, Pallas kernels for 0%

profile of v4, /device:TPU:1, one launch (start us, length us, event | category | flops | bytes accessed | tf_op | source)
XLA Modules:
  0.0 146.6 jit_solution(15636564459510670608)
XLA Ops:
  2.2 1.0 convolution_convert_fusion
  3.9 4.8 %all-to-all-start = ((bf16[4,4,128]{2,1,0:T(4,128)(2,1)}), bf16[4,4,128]{2,1,0:T(4,128)(2,1)S(1)}, u32[]{:S(2)}, u32[]{:S(2)}) async-start(bf16[4,4,128]{2,1,0:T(4,128)(2,1)} %broadcast_in_dim.54), calls=%async_computation | async-start | bytes 8192 | tf_op jit(solution)/shard_map/all_to_all | solution.py:23
  9.5 1.0 reduce-precision_convert_fusion.3
  10.5 1.1 convert_element_type.136
  11.7 1.2 all-to-all-done
  13.0 1.2 broadcast_in_dim.59
  14.2 16.4 %all-to-all-start.1 = ((bf16[64,4,1856]{2,1,0:T(4,128)(2,1)}), bf16[64,4,1856]{2,1,0:T(4,128)(2,1)S(1)}, u32[]{:S(2)}, u32[]{:S(2)}) async-start(bf16[64,4,1856]{2,1,0:T(4,128)(2,1)} %broadcast_in_dim.59), calls=%async_computation.1 | async-start | bytes 1966080 | tf_op jit(solution)/shard_map/all_to_all | solution.py:23
  31.2 2.2 %collective-permute-start = (bf16[128,896]{1,0:T(8,128)(2,1)S(1)}, bf16[128,896]{1,0:T(8,128)(2,1)S(1)}, u32[]{:S(2)}, u32[]{:S(2)}) collective-permute-start(bf16[128,896]{1,0:T(8,128)(2,1)S(1)} %get-tuple-element.50), channel_id=1, source_target_pairs={{0,2},{2,4},{4,6},{6,0},{1,3},{3,5},{5,7},{7,1},{8,10},{10,12},{12... | collective-permute-start | bytes 688136 | tf_op jit(solution)/shard_map/ppermute | solution.py:36
  33.4 4.3 %collective-permute-start.1 = (bf16[128,896]{1,0:T(8,128)(2,1)S(1)}, bf16[128,896]{1,0:T(8,128)(2,1)S(1)}, u32[]{:S(2)}, u32[]{:S(2)}) collective-permute-start(bf16[128,896]{1,0:T(8,128)(2,1)S(1)} %get-tuple-element.51), channel_id=1, source_target_pairs={{0,4},{2,6},{4,0},{6,2},{1,5},{3,7},{5,1},{7,3},{8,12},{10,14},{12... | collective-permute-start | bytes 688136 | tf_op jit(solution)/shard_map/ppermute | solution.py:36
  37.7 3.1 %collective-permute-start.2 = (bf16[128,896]{1,0:T(8,128)(2,1)S(1)}, bf16[128,896]{1,0:T(8,128)(2,1)S(1)}, u32[]{:S(2)}, u32[]{:S(2)}) collective-permute-start(bf16[128,896]{1,0:T(8,128)(2,1)S(1)} %get-tuple-element.52), channel_id=1, source_target_pairs={{0,6},{2,0},{4,2},{6,4},{1,7},{3,1},{5,3},{7,5},{8,14},{10,8},{12,... | collective-permute-start | bytes 688136 | tf_op jit(solution)/shard_map/ppermute | solution.py:36
  41.8 2.8 %collective-permute-done.1 = bf16[128,896]{1,0:T(8,128)(2,1)S(1)} collective-permute-done((bf16[128,896]{1,0:T(8,128)(2,1)S(1)}, bf16[128,896]{1,0:T(8,128)(2,1)S(1)}, u32[]{:S(2)}, u32[]{:S(2)}) %collective-permute-start.1) | collective-permute-done | bytes 229408 | tf_op jit(solution)/shard_map/ppermute | solution.py:36
  44.5 2.5 %collective-permute-done.2 = bf16[128,896]{1,0:T(8,128)(2,1)S(1)} collective-permute-done((bf16[128,896]{1,0:T(8,128)(2,1)S(1)}, bf16[128,896]{1,0:T(8,128)(2,1)S(1)}, u32[]{:S(2)}, u32[]{:S(2)}) %collective-permute-start.2) | collective-permute-done | bytes 229408 | tf_op jit(solution)/shard_map/ppermute | solution.py:36
  47.1 4.9 %collective-permute-start.3 = (bf16[512,896]{1,0:T(8,128)(2,1)S(1)}, bf16[512,896]{1,0:T(8,128)(2,1)}, u32[]{:S(2)}, u32[]{:S(2)}) collective-permute-start(bf16[512,896]{1,0:T(8,128)(2,1)S(1)} %pad_maximum_fusion), channel_id=1, source_target_pairs={{0,1},{1,0},{2,3},{3,2},{4,5},{5,4},{6,7},{7,6},{8,9},{9,8},{10,11... | collective-permute-start | bytes 2752520 | tf_op jit(solution)/shard_map/ppermute | solution.py:31
  55.0 1.2 multiply_reduce_fusion.1
  57.5 5.8 %collective-permute-start.9 = (bf16[256,512]{1,0:T(8,128)(2,1)}, bf16[256,512]{1,0:T(8,128)(2,1)S(1)}, u32[]{:S(2)}, u32[]{:S(2)}) collective-permute-start(bf16[256,512]{1,0:T(8,128)(2,1)} %reshape.117), channel_id=1, source_target_pairs={{0,1},{1,0},{2,3},{3,2},{4,5},{5,4},{6,7},{7,6},{8,9},{9,8},{10,11... | collective-permute-start | bytes 786440 | tf_op jit(solution)/shard_map/ppermute | solution.py:31
  63.2 1.9 %fusion.44 = f32[256,384]{1,0:T(8,128)S(1)} fusion(bf16[256,512]{1,0:T(8,128)(2,1)} %reshape.117, bf16[512,896]{1,0:T(8,128)(2,1)} %collective-permute-done.3, f32[512]{0:T(512)S(1)} %multiply_reduce_fusion.1, f32[256]{0:T(256)S(1)} %add.257), kind=kOutput, calls=%fused_computation.67 | convolution fusion | flops 236060672 | bytes 1575936 | tf_op jit(solution)/shard_map/dot_general | solution.py:66
  65.2 1.6 %convolution_add_fusion.2 = f32[256,384]{1,0:T(8,128)S(1)} fusion(f32[256,384]{1,0:T(8,128)S(1)} %fusion.44, bf16[256,512]{1,0:T(8,128)(2,1)} %reshape.117, bf16[512,896]{1,0:T(8,128)(2,1)S(1)} %pad_maximum_fusion, f32[512]{0:T(512)S(1)} %multiply_reduce_fusion.2, f32[256]{0:T(256)S(1)} %add.257), kind=kOutput, calls=%fused_computation.34 | convolution fusion | flops 236158976 | bytes 1969152 | tf_op jit(solution)/shard_map/dot_general | solution.py:66
  68.0 8.3 %all-to-all-start.2 = ((f32[64,4,384]{2,1,0:T(4,128)}), f32[64,4,384]{2,1,0:T(4,128)S(1)}, u32[]{:S(2)}, u32[]{:S(2)}) async-start(f32[64,4,384]{2,1,0:T(4,128)} %reshape.118), calls=%async_computation.2 | async-start | bytes 786432 | tf_op jit(solution)/shard_map/all_to_all | solution.py:23
  77.0 2.1 %fusion.15 = f32[512,160]{0,1:T(8,128)S(1)} fusion(bf16[512,160]{1,0:T(8,128)(2,1)S(1)} %constant_dynamic-update-slice_fusion.2, bf16[512,512]{1,0:T(8,128)(2,1)S(1)} %constant_dynamic-update-slice_fusion, f32[512]{0:T(512)S(1)} %copy-done.15, f32[512]{0:T(512)S(1)} %multiply_reduce_fusion, bf16[512,896]{1,0:T(8,128)(2,1)} %collective-permute-done.3), kind=kOutput, calls=%fused_computation.22 | convolution fusion | flops 354680832 | bytes 1544192 | tf_op jit(solution)/shard_map/dot_general | solution.py:66
  79.1 2.7 %collective-permute-start.5 = (f32[512,160]{0,1:T(8,128)S(1)}, f32[512,160]{0,1:T(8,128)S(1)}, u32[]{:S(2)}, u32[]{:S(2)}) collective-permute-start(f32[512,160]{0,1:T(8,128)S(1)} %fusion.15), channel_id=1, source_target_pairs={{0,1},{1,0},{2,3},{3,2},{4,5},{5,4},{6,7},{7,6},{8,9},{9,8},{10,11... | collective-permute-start | bytes 983048 | tf_op jit(solution)/shard_map/ppermute | solution.py:31
  81.8 1.2 fusion.104
  83.2 1.0 fusion.25
  84.2 4.3 %collective-permute-start.6 = (f32[128,160]{0,1:T(8,128)S(1)}, f32[128,160]{0,1:T(8,128)S(1)}, u32[]{:S(2)}, u32[]{:S(2)}) collective-permute-start(f32[128,160]{0,1:T(8,128)S(1)} %get-tuple-element.47), channel_id=1, source_target_pairs={{0,6},{2,0},{4,2},{6,4},{1,7},{3,1},{5,3},{7,5},{8,14},{10,8},{12,... | collective-permute-start | bytes 245768 | tf_op jit(solution)/shard_map/ppermute | solution.py:36
  88.5 1.9 %collective-permute-start.8 = (f32[128,160]{0,1:T(8,128)S(1)}, f32[128,160]{0,1:T(8,128)S(1)}, u32[]{:S(2)}, u32[]{:S(2)}) collective-permute-start(f32[128,160]{0,1:T(8,128)S(1)} %get-tuple-element.48), channel_id=1, source_target_pairs={{0,2},{2,4},{4,6},{6,0},{1,3},{3,5},{5,7},{7,1},{8,10},{10,12},{12... | collective-permute-start | bytes 245768 | tf_op jit(solution)/shard_map/ppermute | solution.py:36
  90.5 3.1 %collective-permute-start.7 = (f32[128,160]{0,1:T(8,128)S(1)}, f32[128,160]{0,1:T(8,128)S(1)}, u32[]{:S(2)}, u32[]{:S(2)}) collective-permute-start(f32[128,160]{0,1:T(8,128)S(1)} %get-tuple-element.49), channel_id=1, source_target_pairs={{0,4},{2,6},{4,0},{6,2},{1,5},{3,7},{5,1},{7,3},{8,12},{10,14},{12... | collective-permute-start | bytes 245768 | tf_op jit(solution)/shard_map/ppermute | solution.py:36
  94.9 12.4 %all-to-all-start.3 = ((bf16[64,4,384]{2,1,0:T(4,128)(2,1)}), bf16[64,4,384]{2,1,0:T(4,128)(2,1)S(1)}, u32[]{:S(2)}, u32[]{:S(2)}) async-start(bf16[64,4,384]{2,1,0:T(4,128)(2,1)} %broadcast_in_dim.63), calls=%async_computation.3 | async-start | bytes 393216 | tf_op jit(solution)/shard_map/all_to_all | solution.py:23
  108.2 11.1 %all-to-all-done.3 = bf16[64,4,384]{2,1,0:T(4,128)(2,1)S(1)} async-done(((bf16[64,4,384]{2,1,0:T(4,128)(2,1)}), bf16[64,4,384]{2,1,0:T(4,128)(2,1)S(1)}, u32[]{:S(2)}, u32[]{:S(2)}) %all-to-all-start.3) | async-done | bytes 196640 | tf_op jit(solution)/shard_map/all_to_all | solution.py:23
  119.4 0.9 broadcast_in_dim.68
  120.4 3.5 %all-to-all-start.4 = ((bf16[4,256,384]{2,1,0:T(8,128)(2,1)}), bf16[4,256,384]{2,1,0:T(8,128)(2,1)S(1)}, u32[]{:S(2)}, u32[]{:S(2)}) async-start(bf16[4,256,384]{2,1,0:T(8,128)(2,1)} %broadcast_in_dim.68), calls=%async_computation.4 | async-start | bytes 1572864 | tf_op jit(solution)/shard_map/all_to_all | solution.py:23
  124.1 8.9 %all-to-all-done.4 = bf16[4,256,384]{2,1,0:T(8,128)(2,1)S(1)} async-done(((bf16[4,256,384]{2,1,0:T(8,128)(2,1)}), bf16[4,256,384]{2,1,0:T(8,128)(2,1)S(1)}, u32[]{:S(2)}, u32[]{:S(2)}) %all-to-all-start.4) | async-done | bytes 786464 | tf_op jit(solution)/shard_map/all_to_all | solution.py:23
  133.8 6.1 %collective-permute-start.4 = (bf16[4,256,384]{2,1,0:T(8,128)(2,1)S(1)}, bf16[4,256,384]{2,1,0:T(8,128)(2,1)S(1)}, u32[]{:S(2)}, u32[]{:S(2)}) collective-permute-start(bf16[4,256,384]{2,1,0:T(8,128)(2,1)S(1)} %all-to-all-done.4), channel_id=1, source_target_pairs={{0,1},{1,0},{2,3},{3,2},{4,5},{5,4},{6,7},{7,6},{8,9},{9,8},{10,11... | collective-permute-start | bytes 2359304 | tf_op jit(solution)/shard_map/ppermute | solution.py:31
  145.0 1.5 %add_convert_fusion = bf16[512,1000]{0,1:T(8,128)(2,1)} fusion(f32[512,1000]{0,1:T(8,128)S(1)} %fusion.49, s32[256]{0:T(256)S(1)} %copy-done.11, s32[512]{0:T(512)S(1)} %copy-done.2, bf16[256,256]{1,0:T(8,128)(2,1)S(1)} %get-tuple-element.34, bf16[256,256]{1,0:T(8,128)(2,1)S(1)} %get-tuple-element.35, bf16[256,256]{1,0:T(8,128)(2,1)S(1)} %get-tuple-element.36, ...), kind=kOutput, calls=%fused_computation | convolution fusion | flops 265347072 | bytes 3599360 | tf_op jit(solution)/shard_map/dot_general | solution.py:66
  (137 shorter events, 18.9 us)
Async XLA Ops:
  3.9 9.0 %all-to-all-start = ((bf16[4,4,128]{2,1,0:T(4,128)(2,1)}), bf16[4,4,128]{2,1,0:T(4,128)(2,1)S(1)}, u32[]{:S(2)}, u32[]{:S(2)}) async-start(bf16[4,4,128]{2,1,0:T(4,128)(2,1)} %broadcast_in_dim.54), calls=%async_computation | async-start | bytes 8192 | tf_op jit(solution)/shard_map/all_to_all | solution.py:23
  14.2 16.9 %copy-start = (bf16[128,512]{1,0:T(8,128)(2,1)S(1)}, bf16[128,512]{1,0:T(8,128)(2,1)}, u32[]{:S(2)}) copy-start(bf16[128,512]{1,0:T(8,128)(2,1)} %param.7) | copy-start | bytes 393220
  14.2 26.6 %copy-start.3 = (bf16[8,160]{1,0:T(8,128)(2,1)S(1)}, bf16[8,160]{1,0:T(8,128)(2,1)}, u32[]{:S(2)}) copy-start(bf16[8,160]{1,0:T(8,128)(2,1)} %param.12) | copy-start | bytes 7684
  14.2 26.6 %copy-start.17 = (f32[160]{0:T(256)S(1)}, f32[160]{0:T(256)}, u32[]{:S(2)}) copy-start(f32[160]{0:T(256)} %param.13) | copy-start | bytes 1924
  14.2 42.0 %all-to-all-start.1 = ((bf16[64,4,1856]{2,1,0:T(4,128)(2,1)}), bf16[64,4,1856]{2,1,0:T(4,128)(2,1)S(1)}, u32[]{:S(2)}, u32[]{:S(2)}) async-start(bf16[64,4,1856]{2,1,0:T(4,128)(2,1)} %broadcast_in_dim.59), calls=%async_computation.1 | async-start | bytes 1966080 | tf_op jit(solution)/shard_map/all_to_all | solution.py:23
  30.8 21.8 %copy-start.5 = (s32[512]{0:T(512)S(1)}, s32[512]{0:T(512)}, u32[]{:S(2)}) copy-start(s32[512]{0:T(512)} %param.9) | copy-start | bytes 6148
  30.8 21.8 %copy-start.6 = (s32[512]{0:T(512)S(1)}, s32[512]{0:T(512)}, u32[]{:S(2)}) copy-start(s32[512]{0:T(512)} %param.10) | copy-start | bytes 6148
  31.2 10.6 %collective-permute-start = (bf16[128,896]{1,0:T(8,128)(2,1)S(1)}, bf16[128,896]{1,0:T(8,128)(2,1)S(1)}, u32[]{:S(2)}, u32[]{:S(2)}) collective-permute-start(bf16[128,896]{1,0:T(8,128)(2,1)S(1)} %get-tuple-element.50), channel_id=1, source_target_pairs={{0,2},{2,4},{4,6},{6,0},{1,3},{3,5},{5,7},{7,1},{8,10},{10,12},{12... | collective-permute-start | bytes 688136 | tf_op jit(solution)/shard_map/ppermute | solution.py:36
  33.4 11.2 %collective-permute-start.1 = (bf16[128,896]{1,0:T(8,128)(2,1)S(1)}, bf16[128,896]{1,0:T(8,128)(2,1)S(1)}, u32[]{:S(2)}, u32[]{:S(2)}) collective-permute-start(bf16[128,896]{1,0:T(8,128)(2,1)S(1)} %get-tuple-element.51), channel_id=1, source_target_pairs={{0,4},{2,6},{4,0},{6,2},{1,5},{3,7},{5,1},{7,3},{8,12},{10,14},{12... | collective-permute-start | bytes 688136 | tf_op jit(solution)/shard_map/ppermute | solution.py:36
  37.7 9.4 %collective-permute-start.2 = (bf16[128,896]{1,0:T(8,128)(2,1)S(1)}, bf16[128,896]{1,0:T(8,128)(2,1)S(1)}, u32[]{:S(2)}, u32[]{:S(2)}) collective-permute-start(bf16[128,896]{1,0:T(8,128)(2,1)S(1)} %get-tuple-element.52), channel_id=1, source_target_pairs={{0,6},{2,0},{4,2},{6,4},{1,7},{3,1},{5,3},{7,5},{8,14},{10,8},{12,... | collective-permute-start | bytes 688136 | tf_op jit(solution)/shard_map/ppermute | solution.py:36
  41.7 14.9 %copy-start.8 = (s32[256]{0:T(256)}, s32[256]{0:T(256)S(1)}, u32[]{:S(2)}) copy-start(s32[256]{0:T(256)S(1)} %fusion.137) | copy-start | bytes 3076
  41.7 14.9 %copy-start.10 = (s32[256]{0:T(256)}, s32[256]{0:T(256)S(1)}, u32[]{:S(2)}) copy-start(s32[256]{0:T(256)S(1)} %fusion.136) | copy-start | bytes 3076
  47.1 7.9 %collective-permute-start.3 = (bf16[512,896]{1,0:T(8,128)(2,1)S(1)}, bf16[512,896]{1,0:T(8,128)(2,1)}, u32[]{:S(2)}, u32[]{:S(2)}) collective-permute-start(bf16[512,896]{1,0:T(8,128)(2,1)S(1)} %pad_maximum_fusion), channel_id=1, source_target_pairs={{0,1},{1,0},{2,3},{3,2},{4,5},{5,4},{6,7},{7,6},{8,9},{9,8},{10,11... | collective-permute-start | bytes 2752520 | tf_op jit(solution)/shard_map/ppermute | solution.py:31
  55.0 10.2 %copy-start.12 = (f32[512]{0:T(512)}, f32[512]{0:T(512)S(1)}, u32[]{:S(2)}) copy-start(f32[512]{0:T(512)S(1)} %multiply_reduce_fusion.2) | copy-start | bytes 6148
  56.2 7.0 %copy-start.14 = (f32[512]{0:T(512)}, f32[512]{0:T(512)S(1)}, u32[]{:S(2)}) copy-start(f32[512]{0:T(512)S(1)} %multiply_reduce_fusion.1) | copy-start | bytes 6148
  56.6 8.6 %copy-start.18 = (f32[256]{0:T(256)}, f32[256]{0:T(256)S(1)}, u32[]{:S(2)}) copy-start(f32[256]{0:T(256)S(1)} %add.257) | copy-start | bytes 3076
  57.5 25.5 %collective-permute-start.9 = (bf16[256,512]{1,0:T(8,128)(2,1)}, bf16[256,512]{1,0:T(8,128)(2,1)S(1)}, u32[]{:S(2)}, u32[]{:S(2)}) collective-permute-start(bf16[256,512]{1,0:T(8,128)(2,1)} %reshape.117), channel_id=1, source_target_pairs={{0,1},{1,0},{2,3},{3,2},{4,5},{5,4},{6,7},{7,6},{8,9},{9,8},{10,11... | collective-permute-start | bytes 786440 | tf_op jit(solution)/shard_map/ppermute | solution.py:31
  68.0 25.5 %all-to-all-start.2 = ((f32[64,4,384]{2,1,0:T(4,128)}), f32[64,4,384]{2,1,0:T(4,128)S(1)}, u32[]{:S(2)}, u32[]{:S(2)}) async-start(f32[64,4,384]{2,1,0:T(4,128)} %reshape.118), calls=%async_computation.2 | async-start | bytes 786432 | tf_op jit(solution)/shard_map/all_to_all | solution.py:23
  77.0 6.2 %copy-start.13 = (f32[512]{0:T(512)S(1)}, f32[512]{0:T(512)}, u32[]{:S(2)}) copy-start(f32[512]{0:T(512)} %copy-done.12) | copy-start | bytes 6148
  79.1 4.1 %collective-permute-start.5 = (f32[512,160]{0,1:T(8,128)S(1)}, f32[512,160]{0,1:T(8,128)S(1)}, u32[]{:S(2)}, u32[]{:S(2)}) collective-permute-start(f32[512,160]{0,1:T(8,128)S(1)} %fusion.15), channel_id=1, source_target_pairs={{0,1},{1,0},{2,3},{3,2},{4,5},{5,4},{6,7},{7,6},{8,9},{9,8},{10,11... | collective-permute-start | bytes 983048 | tf_op jit(solution)/shard_map/ppermute | solution.py:31
  83.1 10.6 %copy-start.16 = (s32[4]{0:T(128)S(1)}, s32[4]{0:T(128)}, u32[]{:S(2)}) copy-start(s32[4]{0:T(128)} %select_reduce_fusion) | copy-start | bytes 52
  83.1 10.6 %copy-start.20 = (s32[256]{0:T(256)S(1)}, s32[256]{0:T(256)}, u32[]{:S(2)}) copy-start(s32[256]{0:T(256)} %iota_add_fusion) | copy-start | bytes 3076
  84.2 24.0 %collective-permute-start.6 = (f32[128,160]{0,1:T(8,128)S(1)}, f32[128,160]{0,1:T(8,128)S(1)}, u32[]{:S(2)}, u32[]{:S(2)}) collective-permute-start(f32[128,160]{0,1:T(8,128)S(1)} %get-tuple-element.47), channel_id=1, source_target_pairs={{0,6},{2,0},{4,2},{6,4},{1,7},{3,1},{5,3},{7,5},{8,14},{10,8},{12,... | collective-permute-start | bytes 245768 | tf_op jit(solution)/shard_map/ppermute | solution.py:36
  88.5 19.6 %collective-permute-start.8 = (f32[128,160]{0,1:T(8,128)S(1)}, f32[128,160]{0,1:T(8,128)S(1)}, u32[]{:S(2)}, u32[]{:S(2)}) collective-permute-start(f32[128,160]{0,1:T(8,128)S(1)} %get-tuple-element.48), channel_id=1, source_target_pairs={{0,2},{2,4},{4,6},{6,0},{1,3},{3,5},{5,7},{7,1},{8,10},{10,12},{12... | collective-permute-start | bytes 245768 | tf_op jit(solution)/shard_map/ppermute | solution.py:36
  90.5 17.7 %collective-permute-start.7 = (f32[128,160]{0,1:T(8,128)S(1)}, f32[128,160]{0,1:T(8,128)S(1)}, u32[]{:S(2)}, u32[]{:S(2)}) collective-permute-start(f32[128,160]{0,1:T(8,128)S(1)} %get-tuple-element.49), channel_id=1, source_target_pairs={{0,4},{2,6},{4,0},{6,2},{1,5},{3,7},{5,1},{7,3},{8,12},{10,14},{12... | collective-permute-start | bytes 245768 | tf_op jit(solution)/shard_map/ppermute | solution.py:36
  94.9 24.5 %all-to-all-start.3 = ((bf16[64,4,384]{2,1,0:T(4,128)(2,1)}), bf16[64,4,384]{2,1,0:T(4,128)(2,1)S(1)}, u32[]{:S(2)}, u32[]{:S(2)}) async-start(bf16[64,4,384]{2,1,0:T(4,128)(2,1)} %broadcast_in_dim.63), calls=%async_computation.3 | async-start | bytes 393216 | tf_op jit(solution)/shard_map/all_to_all | solution.py:23
  108.2 15.7 %copy-start.4 = (f32[4,40]{1,0:T(4,128)S(1)}, f32[4,40]{1,0:T(4,128)}, u32[]{:S(2)}) copy-start(f32[4,40]{1,0:T(4,128)} %mul.137) | copy-start | bytes 1924
  120.4 12.7 %all-to-all-start.4 = ((bf16[4,256,384]{2,1,0:T(8,128)(2,1)}), bf16[4,256,384]{2,1,0:T(8,128)(2,1)S(1)}, u32[]{:S(2)}, u32[]{:S(2)}) async-start(bf16[4,256,384]{2,1,0:T(8,128)(2,1)} %broadcast_in_dim.68), calls=%async_computation.4 | async-start | bytes 1572864 | tf_op jit(solution)/shard_map/all_to_all | solution.py:23
  133.1 6.9 %copy-start.21 = (s32[256]{0:T(256)S(1)}, s32[256]{0:T(256)}, u32[]{:S(2)}) copy-start(s32[256]{0:T(256)} %get-tuple-element.20) | copy-start | bytes 3076
  133.8 6.7 %copy-start.2 = (s32[512]{0:T(512)S(1)}, s32[512]{0:T(512)}, u32[]{:S(2)}) copy-start(s32[512]{0:T(512)} %copy-done.1) | copy-start | bytes 6148
  133.8 6.7 %copy-start.9 = (s32[256]{0:T(256)S(1)}, s32[256]{0:T(256)}, u32[]{:S(2)}) copy-start(s32[256]{0:T(256)} %copy-done.8) | copy-start | bytes 3076
  133.8 7.9 %collective-permute-start.4 = (bf16[4,256,384]{2,1,0:T(8,128)(2,1)S(1)}, bf16[4,256,384]{2,1,0:T(8,128)(2,1)S(1)}, u32[]{:S(2)}, u32[]{:S(2)}) collective-permute-start(bf16[4,256,384]{2,1,0:T(8,128)(2,1)S(1)} %all-to-all-done.4), channel_id=1, source_target_pairs={{0,1},{1,0},{2,3},{3,2},{4,5},{5,4},{6,7},{7,6},{8,9},{9,8},{10,11... | collective-permute-start | bytes 2359304 | tf_op jit(solution)/shard_map/ppermute | solution.py:31
  (7 other events, 17.1 us)

commit v5 on v3

--- a/solution.py
+++ b/solution.py
@@ -1,6 +1,8 @@
 import jax
 import jax.numpy as jnp
 from jax import lax
+from jax.experimental import pallas as pl
+from jax.experimental.pallas import tpu as pltpu
 from jax.sharding import Mesh
 from jax.sharding import PartitionSpec as P
 
@@ -69,12 +71,51 @@
     return jnp.pad(array, [(0, 0)] * (array.ndim - 1) + [(0, columns - array.shape[-1])])
 
 
+def packed_rows(batch_index, sub_index, centers, eigvecs, copies):
+    held, depth = centers.shape
+    points, rank = eigvecs.shape
+    piece = depth // points
+
+    def body(sub_ref, batch_ref, centers_ref, eigvecs_ref, out_ref):
+        start = lax.axis_index(ALL) * held
+        within = batch_ref[...] - start
+        inside = jnp.logical_and(within >= 0, within < held)
+        row = jnp.sum(jnp.where(inside, within, 0).astype(jnp.float32)).astype(jnp.int32)
+        lines = lax.broadcasted_iota(jnp.int32, (2 * points, held), 0)
+        target = jnp.full((2 * points, held), row, jnp.int32)
+        for i in range(points):
+            target = jnp.where(lines == i, sub_ref[i], target)
+        lanes = lax.broadcasted_iota(jnp.int32, (2 * points, held), 1)
+        picks = jnp.where(lanes == target, 1.0, 0.0).astype(jnp.bfloat16)
+        rows = dot(picks, centers_ref[...])
+        mine = rows[points:]
+        line = lax.broadcasted_iota(jnp.int32, (points, piece), 0)
+        block = mine[:, :piece]
+        for i in range(1, points):
+            block = jnp.where(line == i, mine[:, i * piece : (i + 1) * piece], block)
+        vecs = eigvecs_ref[...].astype(jnp.float32)
+        packed = jnp.concatenate([rows[:points], vecs, block], axis=1).astype(jnp.bfloat16)
+        out_ref[...] = jnp.broadcast_to(packed[None], out_ref.shape)
+
+    return pl.pallas_call(
+        body,
+        out_shape=jax.ShapeDtypeStruct((copies, points, depth + rank + piece), jnp.bfloat16),
+        in_specs=[
+            pl.BlockSpec(memory_space=pltpu.SMEM),
+            pl.BlockSpec(memory_space=pltpu.VMEM),
+            pl.BlockSpec(memory_space=pltpu.VMEM),
+            pl.BlockSpec(memory_space=pltpu.VMEM),
+        ],
+        out_specs=pl.BlockSpec(memory_space=pltpu.VMEM),
+        name="packed_rows",
+    )(sub_index, batch_index.reshape(-1, min(TILE, batch_index.shape[0])), centers, eigvecs)
+
+
 def step(centers, weights, batch_index, labels, sub_index, eigvecs, scales):
     nx, nplane = lax.axis_size(X), lax.axis_size(PLANE)
     held, depth = centers.shape
     classes = weights.shape[1]
     points, rank = eigvecs.shape
-    me = lax.axis_index(ALL)
     my_x = lax.axis_index(X)
     my_core = lax.axis_index(CORE)
     block = up_to(-(-classes // nx), TILE)
@@ -84,15 +125,8 @@
     label_at = 2 * ranks
 
     owner = batch_index // held
-    places = jnp.arange(held, dtype=jnp.int32)
-    taken = jnp.any(batch_index[None, :] == (me * held + places)[:, None], axis=1)
-    picks = sub_index[:, None] == places[None, :]
-    chosen = jnp.concatenate([picks, taken[None, :]], axis=0).astype(jnp.bfloat16)
-    picks = picks.astype(jnp.bfloat16)
-    rows = dot(chosen, centers).astype(jnp.bfloat16)
-    subset, mine = rows[:points], rows[points:]
-    packed = jnp.concatenate([subset, eigvecs, mine.reshape(points, -1)], axis=1)
-    in_plane = exchange(to_each(packed, PLANE), PLANE)
+    packed = packed_rows(batch_index, sub_index, centers, eigvecs, nplane)
+    in_plane = exchange(packed, PLANE)
     sub_rows = in_plane[:, :, :depth].reshape(nplane * points, depth)
     vec_rows = in_plane[:, :, depth : depth + rank].reshape(nplane * points, rank)
     column = in_plane[:, :, depth + rank :].reshape(nplane, depth)
@@ -101,6 +135,8 @@
     def by_x(array):
         return jnp.moveaxis(array.reshape(array.shape[0], nx, -1), 1, 0)
 
+    picks = sub_index[:, None] == jnp.arange(held, dtype=jnp.int32)[None, :]
+    picks = picks.astype(jnp.bfloat16)
     high, low = parts_of(dot(picks, eigvecs, ((0,), (0,))), 2)
     wts = by_x(with_columns(weights.astype(jnp.bfloat16), nx * block))
     shares = with_columns(jnp.concatenate([wts, by_x(high), by_x(low)], axis=2), wide)
@@ -154,7 +190,7 @@
         chosen = owner[:, None] == device_of(numbers, core)[None, :]
         label = jnp.sum(jnp.where(chosen, labels[:, None], 0), axis=0)
         pred = jnp.concatenate([half_rows[i, :, :block] for i in range(nx)], axis=1)[:, :classes]
-        predictions = predictions + dot(chosen.astype(jnp.bfloat16), pred)
+        predictions = predictions + dot(pred, chosen.astype(jnp.bfloat16), ((0,), (1,)))
         value = half_rows[:, :, block + label_at].astype(jnp.float32).sum(axis=0)
         mark = label[:, None] == jnp.arange(classes, dtype=jnp.int32)[None, :]
         resid = jnp.where(mark, value[:, None].astype(jnp.bfloat16), pred)
@@ -165,7 +201,7 @@
             dot(resid, piece, ((0,), (1,))) for piece in parts_of(near - back, 2)
         )
     center_grad = gradient[:, :held].astype(jnp.bfloat16).T
-    return (predictions.astype(jnp.bfloat16), center_grad, gradient[:, held:].T)
+    return (predictions.astype(jnp.bfloat16).T, center_grad, gradient[:, held:].T)
 
 
 def solution(mesh):

time: 146 us -> 147 us (level)
  waiting for transfers between devices: 36.8 us -> 33.9 us
  Pallas kernels: 0 us -> 2.61 us
  other arithmetic: 4.03 us -> 5.93 us
    pallas_call x0 -> x1, Pallas kernels: none -> 2.61 us  [packed_rows(): pl.pallas_call(body, out_shape=jax.ShapeDtypeStruct((copies, points, dept...]
    all_to_all x5, waiting for transfers between devices: 35.4 us -> 33.8 us  [exchange(): return lax.all_to_all(pieces, axis, 0, 0, tiled=True)]
    broadcast_in_dim x6 -> x5, local copies, waits for them, and re-layouts: 3.54 us -> 2.6 us  [to_each(): return jnp.broadcast_to(array[None], (lax.axis_size(axis), *array.shape))]
    dot_general x16 -> x15, matrix products: 12.5 us -> 12.4 us  [dot(): lax.dot_general(left, right, (contract, ((), ())), preferred_element_type...]
  transfers between devices with their start and end apart: 15 -> 15, of which waited for: 5 -> 4; matrix products, arithmetic and copies ran while one was open for 11% -> 12% of each run, Pallas kernels for 0% -> 2%
where the time goes in v5:
time: 147 us; the launch traced here: 146 us
  starting transfers between devices  82.1 us (56%)
  waiting for transfers between devices  33.9 us (23%)
  matrix products  13.6 us (9%)
  local copies, waits for them, and re-layouts  6.57 us (4%)
  other arithmetic  5.93 us (4%)
  Pallas kernels  2.61 us (2%)
    all_to_all x5, starting transfers between devices, exchange(): return lax.all_to_all(pieces, axis, 0, 0, tiled=True)  41.6 us
    all_to_all x5, waiting for transfers between devices, exchange(): return lax.all_to_all(pieces, axis, 0, 0, tiled=True)  33.8 us
    ppermute x4, starting transfers between devices, from_other_core(): return lax.ppermute(array, CORE, [(0, 1), (1, 0)])  21.4 us
    ppermute x6, starting transfers between devices, to_next(): lax.ppermute(array, axis, [(i, (i + step) % count) for i in range(count)])  19.2 us
    dot_general x15, matrix products, dot(): lax.dot_general(left, right, (contract, ((), ())), preferred_element_type...  12.4 us
  transfers between devices with their start and end apart: 15, of which 4 were waited for; matrix products, arithmetic and copies ran while one was open for 12% of the time, Pallas kernels for 2%

profile of v5, /device:TPU:1, one launch (start us, length us, event | category | flops | bytes accessed | tf_op | source)
XLA Modules:
  0.0 146.1 jit_solution(15896244662091080459)
XLA Ops:
  0.7 1.1 convert_element_type.133
  1.8 1.0 reduce-precision_convert_fusion.3
  3.4 3.9 %collective-permute-start = (bf16[128,896]{1,0:T(8,128)(2,1)S(1)}, bf16[128,896]{1,0:T(8,128)(2,1)S(1)}, u32[]{:S(2)}, u32[]{:S(2)}) collective-permute-start(bf16[128,896]{1,0:T(8,128)(2,1)S(1)} %get-tuple-element.42), channel_id=1, source_target_pairs={{0,2},{2,4},{4,6},{6,0},{1,3},{3,5},{5,7},{7,1},{8,10},{10,12},{12... | collective-permute-start | bytes 688136 | tf_op jit(solution)/shard_map/ppermute | solution.py:37
  7.3 4.4 %collective-permute-start.1 = (bf16[128,896]{1,0:T(8,128)(2,1)S(1)}, bf16[128,896]{1,0:T(8,128)(2,1)S(1)}, u32[]{:S(2)}, u32[]{:S(2)}) collective-permute-start(bf16[128,896]{1,0:T(8,128)(2,1)S(1)} %get-tuple-element.43), channel_id=1, source_target_pairs={{0,4},{2,6},{4,0},{6,2},{1,5},{3,7},{5,1},{7,3},{8,12},{10,14},{12... | collective-permute-start | bytes 688136 | tf_op jit(solution)/shard_map/ppermute | solution.py:37
  11.7 3.1 %collective-permute-start.2 = (bf16[128,896]{1,0:T(8,128)(2,1)S(1)}, bf16[128,896]{1,0:T(8,128)(2,1)S(1)}, u32[]{:S(2)}, u32[]{:S(2)}) collective-permute-start(bf16[128,896]{1,0:T(8,128)(2,1)S(1)} %get-tuple-element.44), channel_id=1, source_target_pairs={{0,6},{2,0},{4,2},{6,4},{1,7},{3,1},{5,3},{7,5},{8,14},{10,8},{12,... | collective-permute-start | bytes 688136 | tf_op jit(solution)/shard_map/ppermute | solution.py:37
  14.7 2.6 %packed_rows.1 = bf16[64,8,736]{2,1,0:T(8,128)(2,1)} custom-call(s32[8]{0:T(128)} %sub_ref.1, s32[4,128]{1,0:T(4,128)} %bitcast.116, bf16[128,512]{1,0:T(8,128)(2,1)} %centers_ref.1, bf16[8,160]{1,0:T(8,128)(2,1)} %eigvecs_ref.1), custom_call_target="tpu_custom_call" | custom-call | tf_op jit(solution)/shard_map/packed_rows/pallas_call | solution.py:100
  17.4 16.4 %all-to-all-start = ((bf16[64,8,736]{2,1,0:T(8,128)(2,1)}), bf16[64,8,736]{2,1,0:T(8,128)(2,1)S(1)}, u32[]{:S(2)}, u32[]{:S(2)}) async-start(bf16[64,8,736]{2,1,0:T(8,128)(2,1)} %packed_rows.1), calls=%async_computation | async-start | bytes 1572864 | tf_op jit(solution)/shard_map/all_to_all | solution.py:24
  34.1 3.7 %collective-permute-start.3 = (bf16[512,896]{1,0:T(8,128)(2,1)S(1)}, bf16[512,896]{1,0:T(8,128)(2,1)S(1)}, u32[]{:S(2)}, u32[]{:S(2)}) collective-permute-start(bf16[512,896]{1,0:T(8,128)(2,1)S(1)} %pad_maximum_fusion), channel_id=1, source_target_pairs={{0,1},{1,0},{2,3},{3,2},{4,5},{5,4},{6,7},{7,6},{8,9},{9,8},{10,11... | collective-permute-start | bytes 2752520 | tf_op jit(solution)/shard_map/ppermute | solution.py:32
  39.3 0.8 fusion.52
  40.1 0.8 multiply_reduce_fusion.2
  41.0 13.9 %all-to-all-done = bf16[64,8,736]{2,1,0:T(8,128)(2,1)S(1)} async-done(((bf16[64,8,736]{2,1,0:T(8,128)(2,1)}), bf16[64,8,736]{2,1,0:T(8,128)(2,1)S(1)}, u32[]{:S(2)}, u32[]{:S(2)}) %all-to-all-start) | async-done | bytes 753696 | tf_op jit(solution)/shard_map/all_to_all | solution.py:24
  56.2 3.4 %all-to-all-start.1 = ((bf16[4,64,512]{2,1,0:T(8,128)(2,1)}), bf16[4,64,512]{2,1,0:T(8,128)(2,1)S(1)}, u32[]{:S(2)}, u32[]{:S(2)}) async-start(bf16[4,64,512]{2,1,0:T(8,128)(2,1)} %broadcast_in_dim.53), calls=%async_computation.1 | async-start | bytes 524288 | tf_op jit(solution)/shard_map/all_to_all | solution.py:24
  59.6 1.7 %fusion.15 = f32[512,160]{0,1:T(8,128)} fusion(f32[512]{0:T(512)S(1)} %multiply_reduce_fusion.1, f32[512]{0:T(512)S(1)} %add.336, bf16[64,8,736]{2,1,0:T(8,128)(2,1)S(1)} %all-to-all-done, bf16[512,896]{1,0:T(8,128)(2,1)S(1)} %collective-permute-done.3), kind=kOutput, calls=%fused_computation.22 | convolution fusion | flops 354680832 | bytes 1642496 | tf_op jit(solution)/shard_map/dot_general | solution.py:67
  61.3 6.5 %collective-permute-start.5 = (f32[512,160]{0,1:T(8,128)}, f32[512,160]{0,1:T(8,128)}, u32[]{:S(2)}, u32[]{:S(2)}) collective-permute-start(f32[512,160]{0,1:T(8,128)} %fusion.15), channel_id=1, source_target_pairs={{0,1},{1,0},{2,3},{3,2},{4,5},{5,4},{6,7},{7,6},{8,9},{9,8},{10,11... | collective-permute-start | bytes 983048 | tf_op jit(solution)/shard_map/ppermute | solution.py:32
  68.0 1.4 fusion.44
  69.5 1.7 %convolution_add_fusion.2 = f32[256,384]{1,0:T(8,128)S(1)} fusion(f32[256,384]{1,0:T(8,128)} %fusion.44, bf16[256,512]{1,0:T(8,128)(2,1)S(1)} %bitcast.105, bf16[512,896]{1,0:T(8,128)(2,1)S(1)} %pad_maximum_fusion, f32[512]{0:T(512)S(1)} %copy-done.9, f32[256]{0:T(256)S(1)} %add.298), kind=kOutput, calls=%fused_computation.34 | convolution fusion | flops 236158976 | bytes 1969152 | tf_op jit(solution)/shard_map/dot_general | solution.py:67
  71.2 0.9 reshape.155
  72.0 5.6 %all-to-all-start.2 = ((f32[64,4,384]{2,1,0:T(4,128)}), f32[64,4,384]{2,1,0:T(4,128)S(1)}, u32[]{:S(2)}, u32[]{:S(2)}) async-start(f32[64,4,384]{2,1,0:T(4,128)} %reshape.155), calls=%async_computation.2 | async-start | bytes 786432 | tf_op jit(solution)/shard_map/all_to_all | solution.py:24
  77.9 5.0 %collective-permute-start.9 = (bf16[256,512]{1,0:T(8,128)(2,1)S(1)}, bf16[256,512]{1,0:T(8,128)(2,1)S(1)}, u32[]{:S(2)}, u32[]{:S(2)}) collective-permute-start(bf16[256,512]{1,0:T(8,128)(2,1)S(1)} %bitcast.106), channel_id=1, source_target_pairs={{0,1},{1,0},{2,3},{3,2},{4,5},{5,4},{6,7},{7,6},{8,9},{9,8},{10,11... | collective-permute-start | bytes 786440 | tf_op jit(solution)/shard_map/ppermute | solution.py:32
  83.2 2.0 %fusion.25 = f32[512,160]{0,1:T(8,128)S(1)} fusion(f32[512,160]{0,1:T(8,128)} %collective-permute-done.5, f32[512]{0:T(512)S(1)} %copy-done.11, f32[512]{0:T(512)S(1)} %copy-done.9, bf16[64,8,736]{2,1,0:T(8,128)(2,1)S(1)} %all-to-all-done, bf16[512,896]{1,0:T(8,128)(2,1)S(1)} %pad_maximum_fusion), kind=kOutput, calls=%fused_computation.35 | convolution fusion | flops 354762752 | bytes 1970176 | tf_op jit(solution)/shard_map/dot_general | solution.py:67
  85.3 2.8 %collective-permute-start.6 = (f32[128,160]{0,1:T(8,128)S(1)}, f32[128,160]{0,1:T(8,128)S(1)}, u32[]{:S(2)}, u32[]{:S(2)}) collective-permute-start(f32[128,160]{0,1:T(8,128)S(1)} %get-tuple-element.39), channel_id=1, source_target_pairs={{0,6},{2,0},{4,2},{6,4},{1,7},{3,1},{5,3},{7,5},{8,14},{10,8},{12,... | collective-permute-start | bytes 245768 | tf_op jit(solution)/shard_map/ppermute | solution.py:37
  88.1 2.5 %collective-permute-start.8 = (f32[128,160]{0,1:T(8,128)S(1)}, f32[128,160]{0,1:T(8,128)S(1)}, u32[]{:S(2)}, u32[]{:S(2)}) collective-permute-start(f32[128,160]{0,1:T(8,128)S(1)} %get-tuple-element.40), channel_id=1, source_target_pairs={{0,2},{2,4},{4,6},{6,0},{1,3},{3,5},{5,7},{7,1},{8,10},{10,12},{12... | collective-permute-start | bytes 245768 | tf_op jit(solution)/shard_map/ppermute | solution.py:37
  90.6 2.5 %collective-permute-start.7 = (f32[128,160]{0,1:T(8,128)S(1)}, f32[128,160]{0,1:T(8,128)S(1)}, u32[]{:S(2)}, u32[]{:S(2)}) collective-permute-start(f32[128,160]{0,1:T(8,128)S(1)} %get-tuple-element.41), channel_id=1, source_target_pairs={{0,4},{2,6},{4,0},{6,2},{1,5},{3,7},{5,1},{7,3},{8,12},{10,14},{12... | collective-permute-start | bytes 245768 | tf_op jit(solution)/shard_map/ppermute | solution.py:37
  94.4 12.4 %all-to-all-start.3 = ((bf16[64,4,384]{2,1,0:T(4,128)(2,1)}), bf16[64,4,384]{2,1,0:T(4,128)(2,1)S(1)}, u32[]{:S(2)}, u32[]{:S(2)}) async-start(bf16[64,4,384]{2,1,0:T(4,128)(2,1)} %broadcast_in_dim.57), calls=%async_computation.3 | async-start | bytes 393216 | tf_op jit(solution)/shard_map/all_to_all | solution.py:24
  107.0 11.8 %all-to-all-done.3 = bf16[64,4,384]{2,1,0:T(4,128)(2,1)S(1)} async-done(((bf16[64,4,384]{2,1,0:T(4,128)(2,1)}), bf16[64,4,384]{2,1,0:T(4,128)(2,1)S(1)}, u32[]{:S(2)}, u32[]{:S(2)}) %all-to-all-start.3) | async-done | bytes 196640 | tf_op jit(solution)/shard_map/all_to_all | solution.py:24
  118.9 0.9 broadcast_in_dim.62
  119.9 3.6 %all-to-all-start.4 = ((bf16[4,256,384]{2,1,0:T(8,128)(2,1)}), bf16[4,256,384]{2,1,0:T(8,128)(2,1)S(1)}, u32[]{:S(2)}, u32[]{:S(2)}) async-start(bf16[4,256,384]{2,1,0:T(8,128)(2,1)} %broadcast_in_dim.62), calls=%async_computation.4 | async-start | bytes 1572864 | tf_op jit(solution)/shard_map/all_to_all | solution.py:24
  123.7 0.9 fusion.119
  124.6 8.0 %all-to-all-done.4 = bf16[4,256,384]{2,1,0:T(8,128)(2,1)S(1)} async-done(((bf16[4,256,384]{2,1,0:T(8,128)(2,1)}), bf16[4,256,384]{2,1,0:T(8,128)(2,1)S(1)}, u32[]{:S(2)}, u32[]{:S(2)}) %all-to-all-start.4) | async-done | bytes 786464 | tf_op jit(solution)/shard_map/all_to_all | solution.py:24
  133.2 6.2 %collective-permute-start.4 = (bf16[4,256,384]{2,1,0:T(8,128)(2,1)S(1)}, bf16[4,256,384]{2,1,0:T(8,128)(2,1)S(1)}, u32[]{:S(2)}, u32[]{:S(2)}) collective-permute-start(bf16[4,256,384]{2,1,0:T(8,128)(2,1)S(1)} %all-to-all-done.4), channel_id=1, source_target_pairs={{0,1},{1,0},{2,3},{3,2},{4,5},{5,4},{6,7},{7,6},{8,9},{9,8},{10,11... | collective-permute-start | bytes 2359304 | tf_op jit(solution)/shard_map/ppermute | solution.py:32
  143.7 0.9 copy.52
  144.5 1.5 %add_convert_fusion = bf16[512,1000]{0,1:T(8,128)(2,1)} fusion(f32[512,1000]{0,1:T(8,128)S(1)} %fusion.49, s32[256]{0:T(256)S(1)} %copy-done.8, s32[512]{0:T(512)S(1)} %add_select_fusion, bf16[256,256]{1,0:T(8,128)(2,1)S(1)} %get-tuple-element.26, bf16[256,256]{1,0:T(8,128)(2,1)S(1)} %get-tuple-element.27, bf16[256,256]{1,0:T(8,128)(2,1)S(1)} %get-tuple-element.28, ...), kind=kOutput, calls=%fused_computation | convolution fusion | flops 265347072 | bytes 3599360 | tf_op jit(solution)/shard_map/dot_general | solution.py:67
  (107 shorter events, 10.6 us)
Async XLA Ops:
  0.6 2.6 %copy-start = (bf16[128,512]{1,0:T(8,128)(2,1)S(1)}, bf16[128,512]{1,0:T(8,128)(2,1)}, u32[]{:S(2)}) copy-start(bf16[128,512]{1,0:T(8,128)(2,1)} %centers_ref.1) | copy-start | bytes 393220
  3.3 30.8 %copy-start.1 = (bf16[128,512]{1,0:T(8,128)(2,1)S(1)}, bf16[128,512]{1,0:T(8,128)(2,1)}, u32[]{:S(2)}) copy-start(bf16[128,512]{1,0:T(8,128)(2,1)} %centers_ref.1) | copy-start | bytes 393220
  3.4 30.7 %collective-permute-start = (bf16[128,896]{1,0:T(8,128)(2,1)S(1)}, bf16[128,896]{1,0:T(8,128)(2,1)S(1)}, u32[]{:S(2)}, u32[]{:S(2)}) collective-permute-start(bf16[128,896]{1,0:T(8,128)(2,1)S(1)} %get-tuple-element.42), channel_id=1, source_target_pairs={{0,2},{2,4},{4,6},{6,0},{1,3},{3,5},{5,7},{7,1},{8,10},{10,12},{12... | collective-permute-start | bytes 688136 | tf_op jit(solution)/shard_map/ppermute | solution.py:37
  7.3 26.7 %collective-permute-start.1 = (bf16[128,896]{1,0:T(8,128)(2,1)S(1)}, bf16[128,896]{1,0:T(8,128)(2,1)S(1)}, u32[]{:S(2)}, u32[]{:S(2)}) collective-permute-start(bf16[128,896]{1,0:T(8,128)(2,1)S(1)} %get-tuple-element.43), channel_id=1, source_target_pairs={{0,4},{2,6},{4,0},{6,2},{1,5},{3,7},{5,1},{7,3},{8,12},{10,14},{12... | collective-permute-start | bytes 688136 | tf_op jit(solution)/shard_map/ppermute | solution.py:37
  11.7 22.4 %collective-permute-start.2 = (bf16[128,896]{1,0:T(8,128)(2,1)S(1)}, bf16[128,896]{1,0:T(8,128)(2,1)S(1)}, u32[]{:S(2)}, u32[]{:S(2)}) collective-permute-start(bf16[128,896]{1,0:T(8,128)(2,1)S(1)} %get-tuple-element.44), channel_id=1, source_target_pairs={{0,6},{2,0},{4,2},{6,4},{1,7},{3,1},{5,3},{7,5},{8,14},{10,8},{12,... | collective-permute-start | bytes 688136 | tf_op jit(solution)/shard_map/ppermute | solution.py:37
  17.4 20.5 %copy-start.5 = (s32[512]{0:T(512)S(1)}, s32[512]{0:T(512)}, u32[]{:S(2)}) copy-start(s32[512]{0:T(512)} %param.9) | copy-start | bytes 6148
  17.4 20.5 %copy-start.6 = (s32[512]{0:T(512)S(1)}, s32[512]{0:T(512)}, u32[]{:S(2)}) copy-start(s32[512]{0:T(512)} %param.10) | copy-start | bytes 6148
  17.4 22.7 %copy-start.4 = (bf16[8,160]{1,0:T(8,128)(2,1)S(1)}, bf16[8,160]{1,0:T(8,128)(2,1)}, u32[]{:S(2)}) copy-start(bf16[8,160]{1,0:T(8,128)(2,1)} %eigvecs_ref.1) | copy-start | bytes 7684
  17.4 37.6 %all-to-all-start = ((bf16[64,8,736]{2,1,0:T(8,128)(2,1)}), bf16[64,8,736]{2,1,0:T(8,128)(2,1)S(1)}, u32[]{:S(2)}, u32[]{:S(2)}) async-start(bf16[64,8,736]{2,1,0:T(8,128)(2,1)} %packed_rows.1), calls=%async_computation | async-start | bytes 1572864 | tf_op jit(solution)/shard_map/all_to_all | solution.py:24
  34.0 5.3 %copy-start.7 = (s32[256]{0:T(256)}, s32[256]{0:T(256)S(1)}, u32[]{:S(2)}) copy-start(s32[256]{0:T(256)S(1)} %broadcast_add_fusion) | copy-start | bytes 3076
  34.1 6.7 %collective-permute-start.3 = (bf16[512,896]{1,0:T(8,128)(2,1)S(1)}, bf16[512,896]{1,0:T(8,128)(2,1)S(1)}, u32[]{:S(2)}, u32[]{:S(2)}) collective-permute-start(bf16[512,896]{1,0:T(8,128)(2,1)S(1)} %pad_maximum_fusion), channel_id=1, source_target_pairs={{0,1},{1,0},{2,3},{3,2},{4,5},{5,4},{6,7},{7,6},{8,9},{9,8},{10,11... | collective-permute-start | bytes 2752520 | tf_op jit(solution)/shard_map/ppermute | solution.py:32
  55.2 6.2 %copy-start.10 = (f32[512]{0:T(512)}, f32[512]{0:T(512)S(1)}, u32[]{:S(2)}) copy-start(f32[512]{0:T(512)S(1)} %add.336) | copy-start | bytes 6148
  56.2 11.6 %all-to-all-start.1 = ((bf16[4,64,512]{2,1,0:T(8,128)(2,1)}), bf16[4,64,512]{2,1,0:T(8,128)(2,1)S(1)}, u32[]{:S(2)}, u32[]{:S(2)}) async-start(bf16[4,64,512]{2,1,0:T(8,128)(2,1)} %broadcast_in_dim.53), calls=%async_computation.1 | async-start | bytes 524288 | tf_op jit(solution)/shard_map/all_to_all | solution.py:24
  61.3 8.1 %copy-start.9 = (f32[512]{0:T(512)S(1)}, f32[512]{0:T(512)}, u32[]{:S(2)}) copy-start(f32[512]{0:T(512)} %multiply_reduce_fusion.2) | copy-start | bytes 6148
  61.3 21.9 %collective-permute-start.5 = (f32[512,160]{0,1:T(8,128)}, f32[512,160]{0,1:T(8,128)}, u32[]{:S(2)}, u32[]{:S(2)}) collective-permute-start(f32[512,160]{0,1:T(8,128)} %fusion.15), channel_id=1, source_target_pairs={{0,1},{1,0},{2,3},{3,2},{4,5},{5,4},{6,7},{7,6},{8,9},{9,8},{10,11... | collective-permute-start | bytes 983048 | tf_op jit(solution)/shard_map/ppermute | solution.py:32
  69.5 8.2 %copy-start.13 = (f32[160]{0:T(256)S(1)}, f32[160]{0:T(256)}, u32[]{:S(2)}) copy-start(f32[160]{0:T(256)} %param.13) | copy-start | bytes 1924
  69.5 13.5 %copy-start.16 = (f32[128]{0:T(128)S(1)}, f32[128]{0:T(128)}, u32[]{:S(2)}) copy-start(f32[128]{0:T(128)} %multiply_reduce_fusion.5) | copy-start | bytes 1540
  71.2 12.1 %copy-start.11 = (f32[512]{0:T(512)S(1)}, f32[512]{0:T(512)}, u32[]{:S(2)}) copy-start(f32[512]{0:T(512)} %copy-done.10) | copy-start | bytes 6148
  72.0 21.1 %all-to-all-start.2 = ((f32[64,4,384]{2,1,0:T(4,128)}), f32[64,4,384]{2,1,0:T(4,128)S(1)}, u32[]{:S(2)}, u32[]{:S(2)}) async-start(f32[64,4,384]{2,1,0:T(4,128)} %reshape.155), calls=%async_computation.2 | async-start | bytes 786432 | tf_op jit(solution)/shard_map/all_to_all | solution.py:24
  77.9 45.7 %collective-permute-start.9 = (bf16[256,512]{1,0:T(8,128)(2,1)S(1)}, bf16[256,512]{1,0:T(8,128)(2,1)S(1)}, u32[]{:S(2)}, u32[]{:S(2)}) collective-permute-start(bf16[256,512]{1,0:T(8,128)(2,1)S(1)} %bitcast.106), channel_id=1, source_target_pairs={{0,1},{1,0},{2,3},{3,2},{4,5},{5,4},{6,7},{7,6},{8,9},{9,8},{10,11... | collective-permute-start | bytes 786440 | tf_op jit(solution)/shard_map/ppermute | solution.py:32
  83.2 10.1 %copy-start.12 = (s32[4]{0:T(128)S(1)}, s32[4]{0:T(128)}, u32[]{:S(2)}) copy-start(s32[4]{0:T(128)} %select_reduce_fusion) | copy-start | bytes 52
  85.3 21.6 %collective-permute-start.6 = (f32[128,160]{0,1:T(8,128)S(1)}, f32[128,160]{0,1:T(8,128)S(1)}, u32[]{:S(2)}, u32[]{:S(2)}) collective-permute-start(f32[128,160]{0,1:T(8,128)S(1)} %get-tuple-element.39), channel_id=1, source_target_pairs={{0,6},{2,0},{4,2},{6,4},{1,7},{3,1},{5,3},{7,5},{8,14},{10,8},{12,... | collective-permute-start | bytes 245768 | tf_op jit(solution)/shard_map/ppermute | solution.py:37
  88.1 18.8 %collective-permute-start.8 = (f32[128,160]{0,1:T(8,128)S(1)}, f32[128,160]{0,1:T(8,128)S(1)}, u32[]{:S(2)}, u32[]{:S(2)}) collective-permute-start(f32[128,160]{0,1:T(8,128)S(1)} %get-tuple-element.40), channel_id=1, source_target_pairs={{0,2},{2,4},{4,6},{6,0},{1,3},{3,5},{5,7},{7,1},{8,10},{10,12},{12... | collective-permute-start | bytes 245768 | tf_op jit(solution)/shard_map/ppermute | solution.py:37
  90.6 16.3 %collective-permute-start.7 = (f32[128,160]{0,1:T(8,128)S(1)}, f32[128,160]{0,1:T(8,128)S(1)}, u32[]{:S(2)}, u32[]{:S(2)}) collective-permute-start(f32[128,160]{0,1:T(8,128)S(1)} %get-tuple-element.41), channel_id=1, source_target_pairs={{0,4},{2,6},{4,0},{6,2},{1,5},{3,7},{5,1},{7,3},{8,12},{10,14},{12... | collective-permute-start | bytes 245768 | tf_op jit(solution)/shard_map/ppermute | solution.py:37
  94.4 24.5 %all-to-all-start.3 = ((bf16[64,4,384]{2,1,0:T(4,128)(2,1)}), bf16[64,4,384]{2,1,0:T(4,128)(2,1)S(1)}, u32[]{:S(2)}, u32[]{:S(2)}) async-start(bf16[64,4,384]{2,1,0:T(4,128)(2,1)} %broadcast_in_dim.57), calls=%async_computation.3 | async-start | bytes 393216 | tf_op jit(solution)/shard_map/all_to_all | solution.py:24
  119.9 12.8 %all-to-all-start.4 = ((bf16[4,256,384]{2,1,0:T(8,128)(2,1)}), bf16[4,256,384]{2,1,0:T(8,128)(2,1)S(1)}, u32[]{:S(2)}, u32[]{:S(2)}) async-start(bf16[4,256,384]{2,1,0:T(8,128)(2,1)} %broadcast_in_dim.62), calls=%async_computation.4 | async-start | bytes 1572864 | tf_op jit(solution)/shard_map/all_to_all | solution.py:24
  123.6 9.6 %copy-start.2 = (bf16[136,512]{0,1:T(8,128)(2,1)}, bf16[136,512]{0,1:T(8,128)(2,1)S(1)}, u32[]{:S(2)}) copy-start(bf16[136,512]{0,1:T(8,128)(2,1)S(1)} %get-tuple-element.33) | copy-start | bytes 417796
  132.7 7.0 %copy-start.15 = (s32[256]{0:T(256)S(1)}, s32[256]{0:T(256)}, u32[]{:S(2)}) copy-start(s32[256]{0:T(256)} %get-tuple-element.16) | copy-start | bytes 3076
  133.2 7.9 %collective-permute-start.4 = (bf16[4,256,384]{2,1,0:T(8,128)(2,1)S(1)}, bf16[4,256,384]{2,1,0:T(8,128)(2,1)S(1)}, u32[]{:S(2)}, u32[]{:S(2)}) collective-permute-start(bf16[4,256,384]{2,1,0:T(8,128)(2,1)S(1)} %all-to-all-done.4), channel_id=1, source_target_pairs={{0,1},{1,0},{2,3},{3,2},{4,5},{5,4},{6,7},{7,6},{8,9},{9,8},{10,11... | collective-permute-start | bytes 2359304 | tf_op jit(solution)/shard_map/ppermute | solution.py:32
  140.5 1.0 copy-start.3
  140.5 1.2 copy-start.17
  142.6 1.9 %copy-start.8 = (s32[256]{0:T(256)S(1)}, s32[256]{0:T(256)}, u32[]{:S(2)}) copy-start(s32[256]{0:T(256)} %copy-done.7) | copy-start | bytes 3076
  (1 other events, 0.8 us)

commit v6 on v5

--- a/solution.py
+++ b/solution.py
@@ -65,6 +65,12 @@
 
 def dot(left, right, contract=((1,), (0,))):
     return lax.dot_general(left, right, (contract, ((), ())), preferred_element_type=jnp.float32)
+
+
+def dot_pieces(pieces, right, contract):
+    count = pieces[0].shape[0]
+    both = dot(jnp.concatenate(pieces, axis=0), right, contract)
+    return both[:count] + both[count:]
 
 
 def with_columns(array, columns):
@@ -190,18 +196,17 @@
         chosen = owner[:, None] == device_of(numbers, core)[None, :]
         label = jnp.sum(jnp.where(chosen, labels[:, None], 0), axis=0)
         pred = jnp.concatenate([half_rows[i, :, :block] for i in range(nx)], axis=1)[:, :classes]
-        predictions = predictions + dot(pred, chosen.astype(jnp.bfloat16), ((0,), (1,)))
+        placed = dot(pred, chosen.astype(jnp.bfloat16), ((0,), (1,)))
+        predictions = (predictions + placed).astype(jnp.bfloat16)
         value = half_rows[:, :, block + label_at].astype(jnp.float32).sum(axis=0)
         mark = label[:, None] == jnp.arange(classes, dtype=jnp.int32)[None, :]
         resid = jnp.where(mark, value[:, None].astype(jnp.bfloat16), pred)
         proj = jnp.concatenate([half_rows[i, :, block:] for i in range(nx)], axis=1)
-        back = sum(dot(piece, proj, ((1,), (1,))) for piece in left)
+        back = dot_pieces(left, proj, ((1,), (1,)))
         near = jnp.pad(near.astype(jnp.float32), ((0, points), (0, 0)))
-        gradient = gradient + sum(
-            dot(resid, piece, ((0,), (1,))) for piece in parts_of(near - back, 2)
-        )
-    center_grad = gradient[:, :held].astype(jnp.bfloat16).T
-    return (predictions.astype(jnp.bfloat16).T, center_grad, gradient[:, held:].T)
+        gradient = gradient + dot_pieces(parts_of(near - back, 2), resid, ((1,), (0,)))
+    center_grad = gradient[:held].astype(jnp.bfloat16)
+    return (predictions.T, center_grad, gradient[held:])
 
 
 def solution(mesh):

time: 147 us -> 147 us (level)
  waiting for transfers between devices: 33.9 us -> 37.1 us
  other arithmetic: 5.93 us -> 3.92 us
    ppermute x4, waiting for transfers between devices: 0.09 us -> 1.71 us  [from_other_core(): return lax.ppermute(array, CORE, [(0, 1), (1, 0)])]
    all_to_all x5, waiting for transfers between devices: 33.8 us -> 35.3 us  [exchange(): return lax.all_to_all(pieces, axis, 0, 0, tiled=True)]
    dot_general x15 -> x11, matrix products: 12.4 us -> 11.7 us  [dot(): lax.dot_general(left, right, (contract, ((), ())), preferred_element_type...]
  transfers between devices with their start and end apart: 15 -> 15, of which waited for: 4 -> 5; matrix products, arithmetic and copies ran while one was open for 12% -> 9% of each run, Pallas kernels for 2% -> 2%
where the time goes in v6:
time: 147 us; the launch traced here: 146 us
  starting transfers between devices  82.1 us (56%)
  waiting for transfers between devices  37.1 us (25%)
  matrix products  12.2 us (8%)
  local copies, waits for them, and re-layouts  6.73 us (5%)
  other arithmetic  3.92 us (3%)
  Pallas kernels  2.61 us (2%)
    all_to_all x5, starting transfers between devices, exchange(): return lax.all_to_all(pieces, axis, 0, 0, tiled=True)  41.5 us
    all_to_all x5, waiting for transfers between devices, exchange(): return lax.all_to_all(pieces, axis, 0, 0, tiled=True)  35.3 us
    ppermute x4, starting transfers between devices, from_other_core(): return lax.ppermute(array, CORE, [(0, 1), (1, 0)])  21.4 us
    ppermute x6, starting transfers between devices, to_next(): lax.ppermute(array, axis, [(i, (i + step) % count) for i in range(count)])  19.2 us
    dot_general x11, matrix products, dot(): lax.dot_general(left, right, (contract, ((), ())), preferred_element_type...  11.7 us
  transfers between devices with their start and end apart: 15, of which 5 were waited for; matrix products, arithmetic and copies ran while one was open for 9% of the time, Pallas kernels for 2%

profile of v6, /device:TPU:1, one launch (start us, length us, event | category | flops | bytes accessed | tf_op | source)
XLA Modules:
  0.0 145.9 jit_solution(18248735231477209039)
XLA Ops:
  0.7 1.1 convert_element_type.141
  1.8 1.0 reduce-precision_convert_fusion.3
  3.7 3.9 %collective-permute-start = (bf16[128,896]{1,0:T(8,128)(2,1)S(1)}, bf16[128,896]{1,0:T(8,128)(2,1)S(1)}, u32[]{:S(2)}, u32[]{:S(2)}) collective-permute-start(bf16[128,896]{1,0:T(8,128)(2,1)S(1)} %get-tuple-element.46), channel_id=1, source_target_pairs={{0,2},{2,4},{4,6},{6,0},{1,3},{3,5},{5,7},{7,1},{8,10},{10,12},{12... | collective-permute-start | bytes 688136 | tf_op jit(solution)/shard_map/ppermute | solution.py:37
  7.7 4.4 %collective-permute-start.1 = (bf16[128,896]{1,0:T(8,128)(2,1)S(1)}, bf16[128,896]{1,0:T(8,128)(2,1)S(1)}, u32[]{:S(2)}, u32[]{:S(2)}) collective-permute-start(bf16[128,896]{1,0:T(8,128)(2,1)S(1)} %get-tuple-element.47), channel_id=1, source_target_pairs={{0,4},{2,6},{4,0},{6,2},{1,5},{3,7},{5,1},{7,3},{8,12},{10,14},{12... | collective-permute-start | bytes 688136 | tf_op jit(solution)/shard_map/ppermute | solution.py:37
  12.0 3.1 %collective-permute-start.2 = (bf16[128,896]{1,0:T(8,128)(2,1)S(1)}, bf16[128,896]{1,0:T(8,128)(2,1)S(1)}, u32[]{:S(2)}, u32[]{:S(2)}) collective-permute-start(bf16[128,896]{1,0:T(8,128)(2,1)S(1)} %get-tuple-element.48), channel_id=1, source_target_pairs={{0,6},{2,0},{4,2},{6,4},{1,7},{3,1},{5,3},{7,5},{8,14},{10,8},{12,... | collective-permute-start | bytes 688136 | tf_op jit(solution)/shard_map/ppermute | solution.py:37
  15.1 2.6 %packed_rows.1 = bf16[64,8,736]{2,1,0:T(8,128)(2,1)} custom-call(s32[8]{0:T(128)} %sub_ref.1, s32[4,128]{1,0:T(4,128)} %bitcast.108, bf16[128,512]{1,0:T(8,128)(2,1)} %centers_ref.1, bf16[8,160]{1,0:T(8,128)(2,1)} %eigvecs_ref.1), custom_call_target="tpu_custom_call" | custom-call | tf_op jit(solution)/shard_map/packed_rows/pallas_call | solution.py:106
  17.7 16.4 %all-to-all-start = ((bf16[64,8,736]{2,1,0:T(8,128)(2,1)}), bf16[64,8,736]{2,1,0:T(8,128)(2,1)S(1)}, u32[]{:S(2)}, u32[]{:S(2)}) async-start(bf16[64,8,736]{2,1,0:T(8,128)(2,1)} %packed_rows.1), calls=%async_computation | async-start | bytes 1572864 | tf_op jit(solution)/shard_map/all_to_all | solution.py:24
  34.5 3.7 %collective-permute-start.3 = (bf16[512,896]{1,0:T(8,128)(2,1)S(1)}, bf16[512,896]{1,0:T(8,128)(2,1)S(1)}, u32[]{:S(2)}, u32[]{:S(2)}) collective-permute-start(bf16[512,896]{1,0:T(8,128)(2,1)S(1)} %pad_maximum_fusion), channel_id=1, source_target_pairs={{0,1},{1,0},{2,3},{3,2},{4,5},{5,4},{6,7},{7,6},{8,9},{9,8},{10,11... | collective-permute-start | bytes 2752520 | tf_op jit(solution)/shard_map/ppermute | solution.py:32
  39.0 1.3 collective-permute-done.3
  40.5 14.8 %all-to-all-done = bf16[64,8,736]{2,1,0:T(8,128)(2,1)S(1)} async-done(((bf16[64,8,736]{2,1,0:T(8,128)(2,1)}), bf16[64,8,736]{2,1,0:T(8,128)(2,1)S(1)}, u32[]{:S(2)}, u32[]{:S(2)}) %all-to-all-start) | async-done | bytes 753696 | tf_op jit(solution)/shard_map/all_to_all | solution.py:24
  55.8 0.7 broadcast_in_dim.53
  56.5 3.4 %all-to-all-start.1 = ((bf16[4,64,512]{2,1,0:T(8,128)(2,1)}), bf16[4,64,512]{2,1,0:T(8,128)(2,1)S(1)}, u32[]{:S(2)}, u32[]{:S(2)}) async-start(bf16[4,64,512]{2,1,0:T(8,128)(2,1)} %broadcast_in_dim.53), calls=%async_computation.1 | async-start | bytes 524288 | tf_op jit(solution)/shard_map/all_to_all | solution.py:24
  59.9 1.7 %fusion.14 = f32[512,160]{0,1:T(8,128)} fusion(f32[512]{0:T(512)S(1)} %multiply_reduce_fusion.1, f32[512]{0:T(512)S(1)} %add.336, bf16[64,8,736]{2,1,0:T(8,128)(2,1)S(1)} %all-to-all-done, bf16[512,896]{1,0:T(8,128)(2,1)S(1)} %collective-permute-done.3), kind=kOutput, calls=%fused_computation.20 | convolution fusion | flops 354680832 | bytes 1642496 | tf_op jit(solution)/shard_map/dot_general | solution.py:67
  61.7 6.3 %collective-permute-start.5 = (f32[512,160]{0,1:T(8,128)}, f32[512,160]{0,1:T(8,128)}, u32[]{:S(2)}, u32[]{:S(2)}) collective-permute-start(f32[512,160]{0,1:T(8,128)} %fusion.14), channel_id=1, source_target_pairs={{0,1},{1,0},{2,3},{3,2},{4,5},{5,4},{6,7},{7,6},{8,9},{9,8},{10,11... | collective-permute-start | bytes 983048 | tf_op jit(solution)/shard_map/ppermute | solution.py:32
  68.2 1.4 fusion.41
  69.7 1.7 %convolution_add_fusion = f32[256,384]{1,0:T(8,128)S(1)} fusion(f32[256,384]{1,0:T(8,128)} %fusion.41, bf16[256,512]{1,0:T(8,128)(2,1)S(1)} %bitcast.97, bf16[512,896]{1,0:T(8,128)(2,1)S(1)} %pad_maximum_fusion, f32[512]{0:T(512)S(1)} %multiply_reduce_fusion.2, f32[256]{0:T(256)S(1)} %add.298), kind=kOutput, calls=%fused_computation.32 | convolution fusion | flops 236158976 | bytes 1969152 | tf_op jit(solution)/shard_map/dot_general | solution.py:67
  71.3 0.9 reshape.155
  72.2 5.7 %all-to-all-start.2 = ((f32[64,4,384]{2,1,0:T(4,128)}), f32[64,4,384]{2,1,0:T(4,128)S(1)}, u32[]{:S(2)}, u32[]{:S(2)}) async-start(f32[64,4,384]{2,1,0:T(4,128)} %reshape.155), calls=%async_computation.2 | async-start | bytes 786432 | tf_op jit(solution)/shard_map/all_to_all | solution.py:24
  78.1 5.2 %collective-permute-start.9 = (bf16[256,512]{1,0:T(8,128)(2,1)S(1)}, bf16[256,512]{1,0:T(8,128)(2,1)S(1)}, u32[]{:S(2)}, u32[]{:S(2)}) collective-permute-start(bf16[256,512]{1,0:T(8,128)(2,1)S(1)} %bitcast.98), channel_id=1, source_target_pairs={{0,1},{1,0},{2,3},{3,2},{4,5},{5,4},{6,7},{7,6},{8,9},{9,8},{10,11... | collective-permute-start | bytes 786440 | tf_op jit(solution)/shard_map/ppermute | solution.py:32
  83.5 2.0 %fusion.24 = f32[512,160]{0,1:T(8,128)S(1)} fusion(f32[512,160]{0,1:T(8,128)} %collective-permute-done.5, f32[512]{0:T(512)S(1)} %add.336, f32[512]{0:T(512)S(1)} %multiply_reduce_fusion.2, bf16[64,8,736]{2,1,0:T(8,128)(2,1)S(1)} %all-to-all-done, bf16[512,896]{1,0:T(8,128)(2,1)S(1)} %pad_maximum_fusion), kind=kOutput, calls=%fused_computation.33 | convolution fusion | flops 354762752 | bytes 1970176 | tf_op jit(solution)/shard_map/dot_general | solution.py:67
  85.6 2.8 %collective-permute-start.6 = (f32[128,160]{0,1:T(8,128)S(1)}, f32[128,160]{0,1:T(8,128)S(1)}, u32[]{:S(2)}, u32[]{:S(2)}) collective-permute-start(f32[128,160]{0,1:T(8,128)S(1)} %get-tuple-element.43), channel_id=1, source_target_pairs={{0,6},{2,0},{4,2},{6,4},{1,7},{3,1},{5,3},{7,5},{8,14},{10,8},{12,... | collective-permute-start | bytes 245768 | tf_op jit(solution)/shard_map/ppermute | solution.py:37
  88.4 2.5 %collective-permute-start.8 = (f32[128,160]{0,1:T(8,128)S(1)}, f32[128,160]{0,1:T(8,128)S(1)}, u32[]{:S(2)}, u32[]{:S(2)}) collective-permute-start(f32[128,160]{0,1:T(8,128)S(1)} %get-tuple-element.44), channel_id=1, source_target_pairs={{0,2},{2,4},{4,6},{6,0},{1,3},{3,5},{5,7},{7,1},{8,10},{10,12},{12... | collective-permute-start | bytes 245768 | tf_op jit(solution)/shard_map/ppermute | solution.py:37
  90.9 2.5 %collective-permute-start.7 = (f32[128,160]{0,1:T(8,128)S(1)}, f32[128,160]{0,1:T(8,128)S(1)}, u32[]{:S(2)}, u32[]{:S(2)}) collective-permute-start(f32[128,160]{0,1:T(8,128)S(1)} %get-tuple-element.45), channel_id=1, source_target_pairs={{0,4},{2,6},{4,0},{6,2},{1,5},{3,7},{5,1},{7,3},{8,12},{10,14},{12... | collective-permute-start | bytes 245768 | tf_op jit(solution)/shard_map/ppermute | solution.py:37
  94.0 0.7 broadcast_in_dim.57
  94.7 12.4 %all-to-all-start.3 = ((bf16[64,4,384]{2,1,0:T(4,128)(2,1)}), bf16[64,4,384]{2,1,0:T(4,128)(2,1)S(1)}, u32[]{:S(2)}, u32[]{:S(2)}) async-start(bf16[64,4,384]{2,1,0:T(4,128)(2,1)} %broadcast_in_dim.57), calls=%async_computation.3 | async-start | bytes 393216 | tf_op jit(solution)/shard_map/all_to_all | solution.py:24
  107.3 11.9 %all-to-all-done.3 = bf16[64,4,384]{2,1,0:T(4,128)(2,1)S(1)} async-done(((bf16[64,4,384]{2,1,0:T(4,128)(2,1)}), bf16[64,4,384]{2,1,0:T(4,128)(2,1)S(1)}, u32[]{:S(2)}, u32[]{:S(2)}) %all-to-all-start.3) | async-done | bytes 196640 | tf_op jit(solution)/shard_map/all_to_all | solution.py:24
  119.3 0.9 broadcast_in_dim.62
  120.2 3.6 %all-to-all-start.4 = ((bf16[4,256,384]{2,1,0:T(8,128)(2,1)}), bf16[4,256,384]{2,1,0:T(8,128)(2,1)S(1)}, u32[]{:S(2)}, u32[]{:S(2)}) async-start(bf16[4,256,384]{2,1,0:T(8,128)(2,1)} %broadcast_in_dim.62), calls=%async_computation.4 | async-start | bytes 1572864 | tf_op jit(solution)/shard_map/all_to_all | solution.py:24
  124.3 8.7 %all-to-all-done.4 = bf16[4,256,384]{2,1,0:T(8,128)(2,1)S(1)} async-done(((bf16[4,256,384]{2,1,0:T(8,128)(2,1)}), bf16[4,256,384]{2,1,0:T(8,128)(2,1)S(1)}, u32[]{:S(2)}, u32[]{:S(2)}) %all-to-all-start.4) | async-done | bytes 786464 | tf_op jit(solution)/shard_map/all_to_all | solution.py:24
  133.5 6.2 %collective-permute-start.4 = (bf16[4,256,384]{2,1,0:T(8,128)(2,1)S(1)}, bf16[4,256,384]{2,1,0:T(8,128)(2,1)S(1)}, u32[]{:S(2)}, u32[]{:S(2)}) collective-permute-start(bf16[4,256,384]{2,1,0:T(8,128)(2,1)S(1)} %all-to-all-done.4), channel_id=1, source_target_pairs={{0,1},{1,0},{2,3},{3,2},{4,5},{5,4},{6,7},{7,6},{8,9},{9,8},{10,11... | collective-permute-start | bytes 2359304 | tf_op jit(solution)/shard_map/ppermute | solution.py:32
  143.5 0.9 copy.52
  144.3 1.5 %add_convert_fusion = bf16[512,1000]{0,1:T(8,128)(2,1)} fusion(bf16[512,1000]{0,1:T(8,128)(2,1)S(1)} %convolution_convert_fusion, s32[256]{0:T(256)S(1)} %broadcast_add_fusion, s32[512]{0:T(512)S(1)} %add_select_fusion, bf16[256,256]{1,0:T(8,128)(2,1)S(1)} %get-tuple-element.26, bf16[256,256]{1,0:T(8,128)(2,1)S(1)} %get-tuple-element.27, ...), kind=kOutput, calls=%fused_computation | convolution fusion | flops 265859072 | bytes 2575360 | tf_op jit(solution)/shard_map/dot_general | solution.py:67
  (82 shorter events, 8.7 us)
Async XLA Ops:
  2.8 0.9 copy-start
  3.7 30.7 %collective-permute-start = (bf16[128,896]{1,0:T(8,128)(2,1)S(1)}, bf16[128,896]{1,0:T(8,128)(2,1)S(1)}, u32[]{:S(2)}, u32[]{:S(2)}) collective-permute-start(bf16[128,896]{1,0:T(8,128)(2,1)S(1)} %get-tuple-element.46), channel_id=1, source_target_pairs={{0,2},{2,4},{4,6},{6,0},{1,3},{3,5},{5,7},{7,1},{8,10},{10,12},{12... | collective-permute-start | bytes 688136 | tf_op jit(solution)/shard_map/ppermute | solution.py:37
  7.7 26.7 %collective-permute-start.1 = (bf16[128,896]{1,0:T(8,128)(2,1)S(1)}, bf16[128,896]{1,0:T(8,128)(2,1)S(1)}, u32[]{:S(2)}, u32[]{:S(2)}) collective-permute-start(bf16[128,896]{1,0:T(8,128)(2,1)S(1)} %get-tuple-element.47), channel_id=1, source_target_pairs={{0,4},{2,6},{4,0},{6,2},{1,5},{3,7},{5,1},{7,3},{8,12},{10,14},{12... | collective-permute-start | bytes 688136 | tf_op jit(solution)/shard_map/ppermute | solution.py:37
  12.0 22.4 %collective-permute-start.2 = (bf16[128,896]{1,0:T(8,128)(2,1)S(1)}, bf16[128,896]{1,0:T(8,128)(2,1)S(1)}, u32[]{:S(2)}, u32[]{:S(2)}) collective-permute-start(bf16[128,896]{1,0:T(8,128)(2,1)S(1)} %get-tuple-element.48), channel_id=1, source_target_pairs={{0,6},{2,0},{4,2},{6,4},{1,7},{3,1},{5,3},{7,5},{8,14},{10,8},{12,... | collective-permute-start | bytes 688136 | tf_op jit(solution)/shard_map/ppermute | solution.py:37
  17.7 16.7 %copy-start.1 = (bf16[128,512]{1,0:T(8,128)(2,1)S(1)}, bf16[128,512]{1,0:T(8,128)(2,1)}, u32[]{:S(2)}) copy-start(bf16[128,512]{1,0:T(8,128)(2,1)} %centers_ref.1) | copy-start | bytes 393220
  17.7 37.6 %all-to-all-start = ((bf16[64,8,736]{2,1,0:T(8,128)(2,1)}), bf16[64,8,736]{2,1,0:T(8,128)(2,1)S(1)}, u32[]{:S(2)}, u32[]{:S(2)}) async-start(bf16[64,8,736]{2,1,0:T(8,128)(2,1)} %packed_rows.1), calls=%async_computation | async-start | bytes 1572864 | tf_op jit(solution)/shard_map/all_to_all | solution.py:24
  34.2 4.1 %copy-start.3 = (s32[512]{0:T(512)S(1)}, s32[512]{0:T(512)}, u32[]{:S(2)}) copy-start(s32[512]{0:T(512)} %param.9) | copy-start | bytes 6148
  34.2 4.1 %copy-start.4 = (s32[512]{0:T(512)S(1)}, s32[512]{0:T(512)}, u32[]{:S(2)}) copy-start(s32[512]{0:T(512)} %param.10) | copy-start | bytes 6148
  34.2 4.6 %copy-start.2 = (bf16[8,160]{1,0:T(8,128)(2,1)S(1)}, bf16[8,160]{1,0:T(8,128)(2,1)}, u32[]{:S(2)}) copy-start(bf16[8,160]{1,0:T(8,128)(2,1)} %eigvecs_ref.1) | copy-start | bytes 7684
  34.5 5.8 %collective-permute-start.3 = (bf16[512,896]{1,0:T(8,128)(2,1)S(1)}, bf16[512,896]{1,0:T(8,128)(2,1)S(1)}, u32[]{:S(2)}, u32[]{:S(2)}) collective-permute-start(bf16[512,896]{1,0:T(8,128)(2,1)S(1)} %pad_maximum_fusion), channel_id=1, source_target_pairs={{0,1},{1,0},{2,3},{3,2},{4,5},{5,4},{6,7},{7,6},{8,9},{9,8},{10,11... | collective-permute-start | bytes 2752520 | tf_op jit(solution)/shard_map/ppermute | solution.py:32
  56.5 11.5 %all-to-all-start.1 = ((bf16[4,64,512]{2,1,0:T(8,128)(2,1)}), bf16[4,64,512]{2,1,0:T(8,128)(2,1)S(1)}, u32[]{:S(2)}, u32[]{:S(2)}) async-start(bf16[4,64,512]{2,1,0:T(8,128)(2,1)} %broadcast_in_dim.53), calls=%async_computation.1 | async-start | bytes 524288 | tf_op jit(solution)/shard_map/all_to_all | solution.py:24
  61.7 21.9 %collective-permute-start.5 = (f32[512,160]{0,1:T(8,128)}, f32[512,160]{0,1:T(8,128)}, u32[]{:S(2)}, u32[]{:S(2)}) collective-permute-start(f32[512,160]{0,1:T(8,128)} %fusion.14), channel_id=1, source_target_pairs={{0,1},{1,0},{2,3},{3,2},{4,5},{5,4},{6,7},{7,6},{8,9},{9,8},{10,11... | collective-permute-start | bytes 983048 | tf_op jit(solution)/shard_map/ppermute | solution.py:32
  71.3 6.6 %copy-start.5 = (f32[160]{0:T(256)S(1)}, f32[160]{0:T(256)}, u32[]{:S(2)}) copy-start(f32[160]{0:T(256)} %param.13) | copy-start | bytes 1924
  72.2 21.2 %all-to-all-start.2 = ((f32[64,4,384]{2,1,0:T(4,128)}), f32[64,4,384]{2,1,0:T(4,128)S(1)}, u32[]{:S(2)}, u32[]{:S(2)}) async-start(f32[64,4,384]{2,1,0:T(4,128)} %reshape.155), calls=%async_computation.2 | async-start | bytes 786432 | tf_op jit(solution)/shard_map/all_to_all | solution.py:24
  78.1 45.8 %collective-permute-start.9 = (bf16[256,512]{1,0:T(8,128)(2,1)S(1)}, bf16[256,512]{1,0:T(8,128)(2,1)S(1)}, u32[]{:S(2)}, u32[]{:S(2)}) collective-permute-start(bf16[256,512]{1,0:T(8,128)(2,1)S(1)} %bitcast.98), channel_id=1, source_target_pairs={{0,1},{1,0},{2,3},{3,2},{4,5},{5,4},{6,7},{7,6},{8,9},{9,8},{10,11... | collective-permute-start | bytes 786440 | tf_op jit(solution)/shard_map/ppermute | solution.py:32
  85.6 21.6 %collective-permute-start.6 = (f32[128,160]{0,1:T(8,128)S(1)}, f32[128,160]{0,1:T(8,128)S(1)}, u32[]{:S(2)}, u32[]{:S(2)}) collective-permute-start(f32[128,160]{0,1:T(8,128)S(1)} %get-tuple-element.43), channel_id=1, source_target_pairs={{0,6},{2,0},{4,2},{6,4},{1,7},{3,1},{5,3},{7,5},{8,14},{10,8},{12,... | collective-permute-start | bytes 245768 | tf_op jit(solution)/shard_map/ppermute | solution.py:37
  88.4 18.8 %collective-permute-start.8 = (f32[128,160]{0,1:T(8,128)S(1)}, f32[128,160]{0,1:T(8,128)S(1)}, u32[]{:S(2)}, u32[]{:S(2)}) collective-permute-start(f32[128,160]{0,1:T(8,128)S(1)} %get-tuple-element.44), channel_id=1, source_target_pairs={{0,2},{2,4},{4,6},{6,0},{1,3},{3,5},{5,7},{7,1},{8,10},{10,12},{12... | collective-permute-start | bytes 245768 | tf_op jit(solution)/shard_map/ppermute | solution.py:37
  90.9 16.3 %collective-permute-start.7 = (f32[128,160]{0,1:T(8,128)S(1)}, f32[128,160]{0,1:T(8,128)S(1)}, u32[]{:S(2)}, u32[]{:S(2)}) collective-permute-start(f32[128,160]{0,1:T(8,128)S(1)} %get-tuple-element.45), channel_id=1, source_target_pairs={{0,4},{2,6},{4,0},{6,2},{1,5},{3,7},{5,1},{7,3},{8,12},{10,14},{12... | collective-permute-start | bytes 245768 | tf_op jit(solution)/shard_map/ppermute | solution.py:37
  94.7 24.5 %all-to-all-start.3 = ((bf16[64,4,384]{2,1,0:T(4,128)(2,1)}), bf16[64,4,384]{2,1,0:T(4,128)(2,1)S(1)}, u32[]{:S(2)}, u32[]{:S(2)}) async-start(bf16[64,4,384]{2,1,0:T(4,128)(2,1)} %broadcast_in_dim.57), calls=%async_computation.3 | async-start | bytes 393216 | tf_op jit(solution)/shard_map/all_to_all | solution.py:24
  120.2 12.7 %all-to-all-start.4 = ((bf16[4,256,384]{2,1,0:T(8,128)(2,1)}), bf16[4,256,384]{2,1,0:T(8,128)(2,1)S(1)}, u32[]{:S(2)}, u32[]{:S(2)}) async-start(bf16[4,256,384]{2,1,0:T(8,128)(2,1)} %broadcast_in_dim.62), calls=%async_computation.4 | async-start | bytes 1572864 | tf_op jit(solution)/shard_map/all_to_all | solution.py:24
  133.5 7.9 %collective-permute-start.4 = (bf16[4,256,384]{2,1,0:T(8,128)(2,1)S(1)}, bf16[4,256,384]{2,1,0:T(8,128)(2,1)S(1)}, u32[]{:S(2)}, u32[]{:S(2)}) collective-permute-start(bf16[4,256,384]{2,1,0:T(8,128)(2,1)S(1)} %all-to-all-done.4), channel_id=1, source_target_pairs={{0,1},{1,0},{2,3},{3,2},{4,5},{5,4},{6,7},{7,6},{8,9},{9,8},{10,11... | collective-permute-start | bytes 2359304 | tf_op jit(solution)/shard_map/ppermute | solution.py:32

commit v7 on v5

--- a/solution.py
+++ b/solution.py
@@ -80,9 +80,10 @@
         start = lax.axis_index(ALL) * held
         within = batch_ref[...] - start
         inside = jnp.logical_and(within >= 0, within < held)
-        row = jnp.sum(jnp.where(inside, within, 0).astype(jnp.float32)).astype(jnp.int32)
+        hits = jnp.where(inside, within, 0).astype(jnp.float32)
+        row = jnp.sum(jnp.sum(hits, axis=0, keepdims=True), axis=1, keepdims=True)
         lines = lax.broadcasted_iota(jnp.int32, (2 * points, held), 0)
-        target = jnp.full((2 * points, held), row, jnp.int32)
+        target = jnp.broadcast_to(row.astype(jnp.int32), (2 * points, held))
         for i in range(points):
             target = jnp.where(lines == i, sub_ref[i], target)
         lanes = lax.broadcasted_iota(jnp.int32, (2 * points, held), 1)

time: 147 us -> 147 us (level)
  no operation moved by 1% of the time
where the time goes in v7:
time: 147 us; the launch traced here: 146 us
  starting transfers between devices  82.1 us (56%)
  waiting for transfers between devices  33.9 us (23%)
  matrix products  13.6 us (9%)
  local copies, waits for them, and re-layouts  6.57 us (4%)
  other arithmetic  5.93 us (4%)
  Pallas kernels  2.58 us (2%)
    all_to_all x5, starting transfers between devices, exchange(): return lax.all_to_all(pieces, axis, 0, 0, tiled=True)  41.6 us
    all_to_all x5, waiting for transfers between devices, exchange(): return lax.all_to_all(pieces, axis, 0, 0, tiled=True)  33.8 us
    ppermute x4, starting transfers between devices, from_other_core(): return lax.ppermute(array, CORE, [(0, 1), (1, 0)])  21.4 us
    ppermute x6, starting transfers between devices, to_next(): lax.ppermute(array, axis, [(i, (i + step) % count) for i in range(count)])  19.2 us
    dot_general x15, matrix products, dot(): lax.dot_general(left, right, (contract, ((), ())), preferred_element_type...  12.4 us
  transfers between devices with their start and end apart: 15, of which 4 were waited for; matrix products, arithmetic and copies ran while one was open for 12% of the time, Pallas kernels for 2%

profile of v7, /device:TPU:1, one launch (start us, length us, event | category | flops | bytes accessed | tf_op | source)
XLA Modules:
  0.0 146.0 jit_solution(6250178423699065806)
XLA Ops:
  0.7 1.1 convert_element_type.133
  1.8 1.0 reduce-precision_convert_fusion.3
  3.4 3.9 %collective-permute-start = (bf16[128,896]{1,0:T(8,128)(2,1)S(1)}, bf16[128,896]{1,0:T(8,128)(2,1)S(1)}, u32[]{:S(2)}, u32[]{:S(2)}) collective-permute-start(bf16[128,896]{1,0:T(8,128)(2,1)S(1)} %get-tuple-element.42), channel_id=1, source_target_pairs={{0,2},{2,4},{4,6},{6,0},{1,3},{3,5},{5,7},{7,1},{8,10},{10,12},{12... | collective-permute-start | bytes 688136 | tf_op jit(solution)/shard_map/ppermute | solution.py:37
  7.3 4.4 %collective-permute-start.1 = (bf16[128,896]{1,0:T(8,128)(2,1)S(1)}, bf16[128,896]{1,0:T(8,128)(2,1)S(1)}, u32[]{:S(2)}, u32[]{:S(2)}) collective-permute-start(bf16[128,896]{1,0:T(8,128)(2,1)S(1)} %get-tuple-element.43), channel_id=1, source_target_pairs={{0,4},{2,6},{4,0},{6,2},{1,5},{3,7},{5,1},{7,3},{8,12},{10,14},{12... | collective-permute-start | bytes 688136 | tf_op jit(solution)/shard_map/ppermute | solution.py:37
  11.7 3.1 %collective-permute-start.2 = (bf16[128,896]{1,0:T(8,128)(2,1)S(1)}, bf16[128,896]{1,0:T(8,128)(2,1)S(1)}, u32[]{:S(2)}, u32[]{:S(2)}) collective-permute-start(bf16[128,896]{1,0:T(8,128)(2,1)S(1)} %get-tuple-element.44), channel_id=1, source_target_pairs={{0,6},{2,0},{4,2},{6,4},{1,7},{3,1},{5,3},{7,5},{8,14},{10,8},{12,... | collective-permute-start | bytes 688136 | tf_op jit(solution)/shard_map/ppermute | solution.py:37
  14.7 2.6 %packed_rows.1 = bf16[64,8,736]{2,1,0:T(8,128)(2,1)} custom-call(s32[8]{0:T(128)} %sub_ref.1, s32[4,128]{1,0:T(4,128)} %bitcast.116, bf16[128,512]{1,0:T(8,128)(2,1)} %centers_ref.1, bf16[8,160]{1,0:T(8,128)(2,1)} %eigvecs_ref.1), custom_call_target="tpu_custom_call" | custom-call | tf_op jit(solution)/shard_map/packed_rows/pallas_call | solution.py:101
  17.3 16.4 %all-to-all-start = ((bf16[64,8,736]{2,1,0:T(8,128)(2,1)}), bf16[64,8,736]{2,1,0:T(8,128)(2,1)S(1)}, u32[]{:S(2)}, u32[]{:S(2)}) async-start(bf16[64,8,736]{2,1,0:T(8,128)(2,1)} %packed_rows.1), calls=%async_computation | async-start | bytes 1572864 | tf_op jit(solution)/shard_map/all_to_all | solution.py:24
  34.1 3.7 %collective-permute-start.3 = (bf16[512,896]{1,0:T(8,128)(2,1)S(1)}, bf16[512,896]{1,0:T(8,128)(2,1)S(1)}, u32[]{:S(2)}, u32[]{:S(2)}) collective-permute-start(bf16[512,896]{1,0:T(8,128)(2,1)S(1)} %pad_maximum_fusion), channel_id=1, source_target_pairs={{0,1},{1,0},{2,3},{3,2},{4,5},{5,4},{6,7},{7,6},{8,9},{9,8},{10,11... | collective-permute-start | bytes 2752520 | tf_op jit(solution)/shard_map/ppermute | solution.py:32
  39.2 0.8 fusion.52
  40.0 0.8 multiply_reduce_fusion.2
  41.0 13.9 %all-to-all-done = bf16[64,8,736]{2,1,0:T(8,128)(2,1)S(1)} async-done(((bf16[64,8,736]{2,1,0:T(8,128)(2,1)}), bf16[64,8,736]{2,1,0:T(8,128)(2,1)S(1)}, u32[]{:S(2)}, u32[]{:S(2)}) %all-to-all-start) | async-done | bytes 753696 | tf_op jit(solution)/shard_map/all_to_all | solution.py:24
  56.1 3.4 %all-to-all-start.1 = ((bf16[4,64,512]{2,1,0:T(8,128)(2,1)}), bf16[4,64,512]{2,1,0:T(8,128)(2,1)S(1)}, u32[]{:S(2)}, u32[]{:S(2)}) async-start(bf16[4,64,512]{2,1,0:T(8,128)(2,1)} %broadcast_in_dim.53), calls=%async_computation.1 | async-start | bytes 524288 | tf_op jit(solution)/shard_map/all_to_all | solution.py:24
  59.6 1.7 %fusion.15 = f32[512,160]{0,1:T(8,128)} fusion(f32[512]{0:T(512)S(1)} %multiply_reduce_fusion.1, f32[512]{0:T(512)S(1)} %add.336, bf16[64,8,736]{2,1,0:T(8,128)(2,1)S(1)} %all-to-all-done, bf16[512,896]{1,0:T(8,128)(2,1)S(1)} %collective-permute-done.3), kind=kOutput, calls=%fused_computation.22 | convolution fusion | flops 354680832 | bytes 1642496 | tf_op jit(solution)/shard_map/dot_general | solution.py:67
  61.3 6.5 %collective-permute-start.5 = (f32[512,160]{0,1:T(8,128)}, f32[512,160]{0,1:T(8,128)}, u32[]{:S(2)}, u32[]{:S(2)}) collective-permute-start(f32[512,160]{0,1:T(8,128)} %fusion.15), channel_id=1, source_target_pairs={{0,1},{1,0},{2,3},{3,2},{4,5},{5,4},{6,7},{7,6},{8,9},{9,8},{10,11... | collective-permute-start | bytes 983048 | tf_op jit(solution)/shard_map/ppermute | solution.py:32
  68.0 1.4 fusion.44
  69.4 1.7 %convolution_add_fusion.2 = f32[256,384]{1,0:T(8,128)S(1)} fusion(f32[256,384]{1,0:T(8,128)} %fusion.44, bf16[256,512]{1,0:T(8,128)(2,1)S(1)} %bitcast.105, bf16[512,896]{1,0:T(8,128)(2,1)S(1)} %pad_maximum_fusion, f32[512]{0:T(512)S(1)} %copy-done.9, f32[256]{0:T(256)S(1)} %add.298), kind=kOutput, calls=%fused_computation.34 | convolution fusion | flops 236158976 | bytes 1969152 | tf_op jit(solution)/shard_map/dot_general | solution.py:67
  71.2 0.9 reshape.155
  72.0 5.6 %all-to-all-start.2 = ((f32[64,4,384]{2,1,0:T(4,128)}), f32[64,4,384]{2,1,0:T(4,128)S(1)}, u32[]{:S(2)}, u32[]{:S(2)}) async-start(f32[64,4,384]{2,1,0:T(4,128)} %reshape.155), calls=%async_computation.2 | async-start | bytes 786432 | tf_op jit(solution)/shard_map/all_to_all | solution.py:24
  77.9 5.0 %collective-permute-start.9 = (bf16[256,512]{1,0:T(8,128)(2,1)S(1)}, bf16[256,512]{1,0:T(8,128)(2,1)S(1)}, u32[]{:S(2)}, u32[]{:S(2)}) collective-permute-start(bf16[256,512]{1,0:T(8,128)(2,1)S(1)} %bitcast.106), channel_id=1, source_target_pairs={{0,1},{1,0},{2,3},{3,2},{4,5},{5,4},{6,7},{7,6},{8,9},{9,8},{10,11... | collective-permute-start | bytes 786440 | tf_op jit(solution)/shard_map/ppermute | solution.py:32
  83.2 2.0 %fusion.25 = f32[512,160]{0,1:T(8,128)S(1)} fusion(f32[512,160]{0,1:T(8,128)} %collective-permute-done.5, f32[512]{0:T(512)S(1)} %copy-done.11, f32[512]{0:T(512)S(1)} %copy-done.9, bf16[64,8,736]{2,1,0:T(8,128)(2,1)S(1)} %all-to-all-done, bf16[512,896]{1,0:T(8,128)(2,1)S(1)} %pad_maximum_fusion), kind=kOutput, calls=%fused_computation.35 | convolution fusion | flops 354762752 | bytes 1970176 | tf_op jit(solution)/shard_map/dot_general | solution.py:67
  85.2 2.8 %collective-permute-start.6 = (f32[128,160]{0,1:T(8,128)S(1)}, f32[128,160]{0,1:T(8,128)S(1)}, u32[]{:S(2)}, u32[]{:S(2)}) collective-permute-start(f32[128,160]{0,1:T(8,128)S(1)} %get-tuple-element.39), channel_id=1, source_target_pairs={{0,6},{2,0},{4,2},{6,4},{1,7},{3,1},{5,3},{7,5},{8,14},{10,8},{12,... | collective-permute-start | bytes 245768 | tf_op jit(solution)/shard_map/ppermute | solution.py:37
  88.0 2.5 %collective-permute-start.8 = (f32[128,160]{0,1:T(8,128)S(1)}, f32[128,160]{0,1:T(8,128)S(1)}, u32[]{:S(2)}, u32[]{:S(2)}) collective-permute-start(f32[128,160]{0,1:T(8,128)S(1)} %get-tuple-element.40), channel_id=1, source_target_pairs={{0,2},{2,4},{4,6},{6,0},{1,3},{3,5},{5,7},{7,1},{8,10},{10,12},{12... | collective-permute-start | bytes 245768 | tf_op jit(solution)/shard_map/ppermute | solution.py:37
  90.5 2.5 %collective-permute-start.7 = (f32[128,160]{0,1:T(8,128)S(1)}, f32[128,160]{0,1:T(8,128)S(1)}, u32[]{:S(2)}, u32[]{:S(2)}) collective-permute-start(f32[128,160]{0,1:T(8,128)S(1)} %get-tuple-element.41), channel_id=1, source_target_pairs={{0,4},{2,6},{4,0},{6,2},{1,5},{3,7},{5,1},{7,3},{8,12},{10,14},{12... | collective-permute-start | bytes 245768 | tf_op jit(solution)/shard_map/ppermute | solution.py:37
  94.4 12.4 %all-to-all-start.3 = ((bf16[64,4,384]{2,1,0:T(4,128)(2,1)}), bf16[64,4,384]{2,1,0:T(4,128)(2,1)S(1)}, u32[]{:S(2)}, u32[]{:S(2)}) async-start(bf16[64,4,384]{2,1,0:T(4,128)(2,1)} %broadcast_in_dim.57), calls=%async_computation.3 | async-start | bytes 393216 | tf_op jit(solution)/shard_map/all_to_all | solution.py:24
  107.0 11.8 %all-to-all-done.3 = bf16[64,4,384]{2,1,0:T(4,128)(2,1)S(1)} async-done(((bf16[64,4,384]{2,1,0:T(4,128)(2,1)}), bf16[64,4,384]{2,1,0:T(4,128)(2,1)S(1)}, u32[]{:S(2)}, u32[]{:S(2)}) %all-to-all-start.3) | async-done | bytes 196640 | tf_op jit(solution)/shard_map/all_to_all | solution.py:24
  118.9 0.9 broadcast_in_dim.62
  119.8 3.6 %all-to-all-start.4 = ((bf16[4,256,384]{2,1,0:T(8,128)(2,1)}), bf16[4,256,384]{2,1,0:T(8,128)(2,1)S(1)}, u32[]{:S(2)}, u32[]{:S(2)}) async-start(bf16[4,256,384]{2,1,0:T(8,128)(2,1)} %broadcast_in_dim.62), calls=%async_computation.4 | async-start | bytes 1572864 | tf_op jit(solution)/shard_map/all_to_all | solution.py:24
  123.7 0.9 fusion.119
  124.6 8.0 %all-to-all-done.4 = bf16[4,256,384]{2,1,0:T(8,128)(2,1)S(1)} async-done(((bf16[4,256,384]{2,1,0:T(8,128)(2,1)}), bf16[4,256,384]{2,1,0:T(8,128)(2,1)S(1)}, u32[]{:S(2)}, u32[]{:S(2)}) %all-to-all-start.4) | async-done | bytes 786464 | tf_op jit(solution)/shard_map/all_to_all | solution.py:24
  133.2 6.2 %collective-permute-start.4 = (bf16[4,256,384]{2,1,0:T(8,128)(2,1)S(1)}, bf16[4,256,384]{2,1,0:T(8,128)(2,1)S(1)}, u32[]{:S(2)}, u32[]{:S(2)}) collective-permute-start(bf16[4,256,384]{2,1,0:T(8,128)(2,1)S(1)} %all-to-all-done.4), channel_id=1, source_target_pairs={{0,1},{1,0},{2,3},{3,2},{4,5},{5,4},{6,7},{7,6},{8,9},{9,8},{10,11... | collective-permute-start | bytes 2359304 | tf_op jit(solution)/shard_map/ppermute | solution.py:32
  143.6 0.9 copy.52
  144.5 1.5 %add_convert_fusion = bf16[512,1000]{0,1:T(8,128)(2,1)} fusion(f32[512,1000]{0,1:T(8,128)S(1)} %fusion.49, s32[256]{0:T(256)S(1)} %copy-done.8, s32[512]{0:T(512)S(1)} %add_select_fusion, bf16[256,256]{1,0:T(8,128)(2,1)S(1)} %get-tuple-element.26, bf16[256,256]{1,0:T(8,128)(2,1)S(1)} %get-tuple-element.27, bf16[256,256]{1,0:T(8,128)(2,1)S(1)} %get-tuple-element.28, ...), kind=kOutput, calls=%fused_computation | convolution fusion | flops 265347072 | bytes 3599360 | tf_op jit(solution)/shard_map/dot_general | solution.py:67
  (107 shorter events, 10.6 us)
Async XLA Ops:
  0.6 2.6 %copy-start = (bf16[128,512]{1,0:T(8,128)(2,1)S(1)}, bf16[128,512]{1,0:T(8,128)(2,1)}, u32[]{:S(2)}) copy-start(bf16[128,512]{1,0:T(8,128)(2,1)} %centers_ref.1) | copy-start | bytes 393220
  3.3 30.7 %copy-start.1 = (bf16[128,512]{1,0:T(8,128)(2,1)S(1)}, bf16[128,512]{1,0:T(8,128)(2,1)}, u32[]{:S(2)}) copy-start(bf16[128,512]{1,0:T(8,128)(2,1)} %centers_ref.1) | copy-start | bytes 393220
  3.4 30.6 %collective-permute-start = (bf16[128,896]{1,0:T(8,128)(2,1)S(1)}, bf16[128,896]{1,0:T(8,128)(2,1)S(1)}, u32[]{:S(2)}, u32[]{:S(2)}) collective-permute-start(bf16[128,896]{1,0:T(8,128)(2,1)S(1)} %get-tuple-element.42), channel_id=1, source_target_pairs={{0,2},{2,4},{4,6},{6,0},{1,3},{3,5},{5,7},{7,1},{8,10},{10,12},{12... | collective-permute-start | bytes 688136 | tf_op jit(solution)/shard_map/ppermute | solution.py:37
  7.3 26.7 %collective-permute-start.1 = (bf16[128,896]{1,0:T(8,128)(2,1)S(1)}, bf16[128,896]{1,0:T(8,128)(2,1)S(1)}, u32[]{:S(2)}, u32[]{:S(2)}) collective-permute-start(bf16[128,896]{1,0:T(8,128)(2,1)S(1)} %get-tuple-element.43), channel_id=1, source_target_pairs={{0,4},{2,6},{4,0},{6,2},{1,5},{3,7},{5,1},{7,3},{8,12},{10,14},{12... | collective-permute-start | bytes 688136 | tf_op jit(solution)/shard_map/ppermute | solution.py:37
  11.7 22.3 %collective-permute-start.2 = (bf16[128,896]{1,0:T(8,128)(2,1)S(1)}, bf16[128,896]{1,0:T(8,128)(2,1)S(1)}, u32[]{:S(2)}, u32[]{:S(2)}) collective-permute-start(bf16[128,896]{1,0:T(8,128)(2,1)S(1)} %get-tuple-element.44), channel_id=1, source_target_pairs={{0,6},{2,0},{4,2},{6,4},{1,7},{3,1},{5,3},{7,5},{8,14},{10,8},{12,... | collective-permute-start | bytes 688136 | tf_op jit(solution)/shard_map/ppermute | solution.py:37
  17.3 20.5 %copy-start.5 = (s32[512]{0:T(512)S(1)}, s32[512]{0:T(512)}, u32[]{:S(2)}) copy-start(s32[512]{0:T(512)} %param.9) | copy-start | bytes 6148
  17.3 20.5 %copy-start.6 = (s32[512]{0:T(512)S(1)}, s32[512]{0:T(512)}, u32[]{:S(2)}) copy-start(s32[512]{0:T(512)} %param.10) | copy-start | bytes 6148
  17.3 22.7 %copy-start.4 = (bf16[8,160]{1,0:T(8,128)(2,1)S(1)}, bf16[8,160]{1,0:T(8,128)(2,1)}, u32[]{:S(2)}) copy-start(bf16[8,160]{1,0:T(8,128)(2,1)} %eigvecs_ref.1) | copy-start | bytes 7684
  17.3 37.6 %all-to-all-start = ((bf16[64,8,736]{2,1,0:T(8,128)(2,1)}), bf16[64,8,736]{2,1,0:T(8,128)(2,1)S(1)}, u32[]{:S(2)}, u32[]{:S(2)}) async-start(bf16[64,8,736]{2,1,0:T(8,128)(2,1)} %packed_rows.1), calls=%async_computation | async-start | bytes 1572864 | tf_op jit(solution)/shard_map/all_to_all | solution.py:24
  34.0 5.3 %copy-start.7 = (s32[256]{0:T(256)}, s32[256]{0:T(256)S(1)}, u32[]{:S(2)}) copy-start(s32[256]{0:T(256)S(1)} %broadcast_add_fusion) | copy-start | bytes 3076
  34.1 6.7 %collective-permute-start.3 = (bf16[512,896]{1,0:T(8,128)(2,1)S(1)}, bf16[512,896]{1,0:T(8,128)(2,1)S(1)}, u32[]{:S(2)}, u32[]{:S(2)}) collective-permute-start(bf16[512,896]{1,0:T(8,128)(2,1)S(1)} %pad_maximum_fusion), channel_id=1, source_target_pairs={{0,1},{1,0},{2,3},{3,2},{4,5},{5,4},{6,7},{7,6},{8,9},{9,8},{10,11... | collective-permute-start | bytes 2752520 | tf_op jit(solution)/shard_map/ppermute | solution.py:32
  55.2 6.2 %copy-start.10 = (f32[512]{0:T(512)}, f32[512]{0:T(512)S(1)}, u32[]{:S(2)}) copy-start(f32[512]{0:T(512)S(1)} %add.336) | copy-start | bytes 6148
  56.1 11.6 %all-to-all-start.1 = ((bf16[4,64,512]{2,1,0:T(8,128)(2,1)}), bf16[4,64,512]{2,1,0:T(8,128)(2,1)S(1)}, u32[]{:S(2)}, u32[]{:S(2)}) async-start(bf16[4,64,512]{2,1,0:T(8,128)(2,1)} %broadcast_in_dim.53), calls=%async_computation.1 | async-start | bytes 524288 | tf_op jit(solution)/shard_map/all_to_all | solution.py:24
  61.3 8.1 %copy-start.9 = (f32[512]{0:T(512)S(1)}, f32[512]{0:T(512)}, u32[]{:S(2)}) copy-start(f32[512]{0:T(512)} %multiply_reduce_fusion.2) | copy-start | bytes 6148
  61.3 21.9 %collective-permute-start.5 = (f32[512,160]{0,1:T(8,128)}, f32[512,160]{0,1:T(8,128)}, u32[]{:S(2)}, u32[]{:S(2)}) collective-permute-start(f32[512,160]{0,1:T(8,128)} %fusion.15), channel_id=1, source_target_pairs={{0,1},{1,0},{2,3},{3,2},{4,5},{5,4},{6,7},{7,6},{8,9},{9,8},{10,11... | collective-permute-start | bytes 983048 | tf_op jit(solution)/shard_map/ppermute | solution.py:32
  69.4 8.2 %copy-start.13 = (f32[160]{0:T(256)S(1)}, f32[160]{0:T(256)}, u32[]{:S(2)}) copy-start(f32[160]{0:T(256)} %param.13) | copy-start | bytes 1924
  69.4 13.5 %copy-start.16 = (f32[128]{0:T(128)S(1)}, f32[128]{0:T(128)}, u32[]{:S(2)}) copy-start(f32[128]{0:T(128)} %multiply_reduce_fusion.5) | copy-start | bytes 1540
  71.1 12.1 %copy-start.11 = (f32[512]{0:T(512)S(1)}, f32[512]{0:T(512)}, u32[]{:S(2)}) copy-start(f32[512]{0:T(512)} %copy-done.10) | copy-start | bytes 6148
  72.0 21.1 %all-to-all-start.2 = ((f32[64,4,384]{2,1,0:T(4,128)}), f32[64,4,384]{2,1,0:T(4,128)S(1)}, u32[]{:S(2)}, u32[]{:S(2)}) async-start(f32[64,4,384]{2,1,0:T(4,128)} %reshape.155), calls=%async_computation.2 | async-start | bytes 786432 | tf_op jit(solution)/shard_map/all_to_all | solution.py:24
  77.9 45.7 %collective-permute-start.9 = (bf16[256,512]{1,0:T(8,128)(2,1)S(1)}, bf16[256,512]{1,0:T(8,128)(2,1)S(1)}, u32[]{:S(2)}, u32[]{:S(2)}) collective-permute-start(bf16[256,512]{1,0:T(8,128)(2,1)S(1)} %bitcast.106), channel_id=1, source_target_pairs={{0,1},{1,0},{2,3},{3,2},{4,5},{5,4},{6,7},{7,6},{8,9},{9,8},{10,11... | collective-permute-start | bytes 786440 | tf_op jit(solution)/shard_map/ppermute | solution.py:32
  83.2 10.1 %copy-start.12 = (s32[4]{0:T(128)S(1)}, s32[4]{0:T(128)}, u32[]{:S(2)}) copy-start(s32[4]{0:T(128)} %select_reduce_fusion) | copy-start | bytes 52
  85.2 21.6 %collective-permute-start.6 = (f32[128,160]{0,1:T(8,128)S(1)}, f32[128,160]{0,1:T(8,128)S(1)}, u32[]{:S(2)}, u32[]{:S(2)}) collective-permute-start(f32[128,160]{0,1:T(8,128)S(1)} %get-tuple-element.39), channel_id=1, source_target_pairs={{0,6},{2,0},{4,2},{6,4},{1,7},{3,1},{5,3},{7,5},{8,14},{10,8},{12,... | collective-permute-start | bytes 245768 | tf_op jit(solution)/shard_map/ppermute | solution.py:37
  88.0 18.8 %collective-permute-start.8 = (f32[128,160]{0,1:T(8,128)S(1)}, f32[128,160]{0,1:T(8,128)S(1)}, u32[]{:S(2)}, u32[]{:S(2)}) collective-permute-start(f32[128,160]{0,1:T(8,128)S(1)} %get-tuple-element.40), channel_id=1, source_target_pairs={{0,2},{2,4},{4,6},{6,0},{1,3},{3,5},{5,7},{7,1},{8,10},{10,12},{12... | collective-permute-start | bytes 245768 | tf_op jit(solution)/shard_map/ppermute | solution.py:37
  90.5 16.3 %collective-permute-start.7 = (f32[128,160]{0,1:T(8,128)S(1)}, f32[128,160]{0,1:T(8,128)S(1)}, u32[]{:S(2)}, u32[]{:S(2)}) collective-permute-start(f32[128,160]{0,1:T(8,128)S(1)} %get-tuple-element.41), channel_id=1, source_target_pairs={{0,4},{2,6},{4,0},{6,2},{1,5},{3,7},{5,1},{7,3},{8,12},{10,14},{12... | collective-permute-start | bytes 245768 | tf_op jit(solution)/shard_map/ppermute | solution.py:37
  94.4 24.5 %all-to-all-start.3 = ((bf16[64,4,384]{2,1,0:T(4,128)(2,1)}), bf16[64,4,384]{2,1,0:T(4,128)(2,1)S(1)}, u32[]{:S(2)}, u32[]{:S(2)}) async-start(bf16[64,4,384]{2,1,0:T(4,128)(2,1)} %broadcast_in_dim.57), calls=%async_computation.3 | async-start | bytes 393216 | tf_op jit(solution)/shard_map/all_to_all | solution.py:24
  119.8 12.8 %all-to-all-start.4 = ((bf16[4,256,384]{2,1,0:T(8,128)(2,1)}), bf16[4,256,384]{2,1,0:T(8,128)(2,1)S(1)}, u32[]{:S(2)}, u32[]{:S(2)}) async-start(bf16[4,256,384]{2,1,0:T(8,128)(2,1)} %broadcast_in_dim.62), calls=%async_computation.4 | async-start | bytes 1572864 | tf_op jit(solution)/shard_map/all_to_all | solution.py:24
  123.6 9.6 %copy-start.2 = (bf16[136,512]{0,1:T(8,128)(2,1)}, bf16[136,512]{0,1:T(8,128)(2,1)S(1)}, u32[]{:S(2)}) copy-start(bf16[136,512]{0,1:T(8,128)(2,1)S(1)} %get-tuple-element.33) | copy-start | bytes 417796
  132.7 7.0 %copy-start.15 = (s32[256]{0:T(256)S(1)}, s32[256]{0:T(256)}, u32[]{:S(2)}) copy-start(s32[256]{0:T(256)} %get-tuple-element.16) | copy-start | bytes 3076
  133.2 7.9 %collective-permute-start.4 = (bf16[4,256,384]{2,1,0:T(8,128)(2,1)S(1)}, bf16[4,256,384]{2,1,0:T(8,128)(2,1)S(1)}, u32[]{:S(2)}, u32[]{:S(2)}) collective-permute-start(bf16[4,256,384]{2,1,0:T(8,128)(2,1)S(1)} %all-to-all-done.4), channel_id=1, source_target_pairs={{0,1},{1,0},{2,3},{3,2},{4,5},{5,4},{6,7},{7,6},{8,9},{9,8},{10,11... | collective-permute-start | bytes 2359304 | tf_op jit(solution)/shard_map/ppermute | solution.py:32
  140.4 1.0 copy-start.3
  140.4 1.2 copy-start.17
  142.6 1.9 %copy-start.8 = (s32[256]{0:T(256)S(1)}, s32[256]{0:T(256)}, u32[]{:S(2)}) copy-start(s32[256]{0:T(256)} %copy-done.7) | copy-start | bytes 3076
  (1 other events, 0.8 us)
